TPU v7x, 512 devices: a whole 4x4x16 slice. The times are simulated.
512 devices in a mesh: client: 4 (over z_hi), expert: 16 (over y, x), shard: 8 (over z_lo, core).
Axes of the slice: x: 4, y: 4, z: 16 (z_hi: 4, z_lo: 4; z = z_hi * 4 + z_lo), core: 2. Of those that a mesh axis runs over, the one named last changes fastest.
Arguments:
- tokens: bfloat16 [4, 2048, 2048], P('client', 'expert'), may hold values from -6 to 6
- target: bfloat16 [4, 2048, 2048], P('client', 'expert'), may hold values from -6 to 6
- routes: int32 [4, 2048, 2], P('client', 'expert'), may hold values from 0 to 7, all different within a row; in each aligned block of 128 rows (0 to 127, 128 to 255, ..., all dimensions but the last counted through in order) at most 32 rows name the same one
- gate_weights: float32 [4, 2048, 2], P('client', 'expert'), may hold values from 0.1 to 1
- counts: int32 [4], replicated, may hold values from 512 to 2048
- gate_proj: bfloat16 [57344, 2048], P(('expert', 'shard'), 'client'), may hold values from -0.125 to 0.125
- up_proj: bfloat16 [57344, 2048], P(('expert', 'shard'), 'client'), may hold values from -0.125 to 0.125
- down_proj: bfloat16 [57344, 2048], P(('expert', 'shard'), 'client'), may hold values from -0.0625 to 0.0625
- correction: bfloat16 [4, 57344, 2048], P('client', ('expert', 'shard')), may hold values from -6 to 6
Outputs:
- pseudo_gradient: float32 [57344, 2048], P(('expert', 'shard'), 'client')
Inputs may be any that keep to these rules, and one draw needn't show every extreme that they name: `routes`: in each aligned block of 128 rows of a client, every expert is named by exactly 32 rows; the 2 ids of a row differ.
All inputs are finite; a program needn't handle non-finite values.
Results may differ from a plain program's by a relative error of at most 0.015.
Values may be sent and summed in bfloat16 or wider, within the bound.
No kernel may reach another device: no remote copies, remote signals or barrier semaphores. Data moves between devices by JAX's collectives and lax.ppermute only.
A program may use at most 64 MiB of HBM per device.

v0:
```python
import jax
import jax.numpy as jnp
from jax import lax
from jax.sharding import Mesh, PartitionSpec as P


EXPERTS = 8
LOCAL_STEPS = 2
CORES = 2


F32 = jnp.float32
BF16 = jnp.bfloat16
EXACT = lax.Precision.HIGHEST


def shift(x, axis, by):
    n = lax.axis_size(axis)
    return lax.ppermute(x, axis, [(i, (i + by) % n) for i in range(n)])


def at(x, start, size, axis):
    return lax.dynamic_slice_in_dim(x, start, size, axis)


def dot(a, b, da, db, **kw):
    return lax.dot_general(a, b, (((da,), (db,)), ((), ())), preferred_element_type=F32, **kw)


def ranks(flat):
    n = flat.shape[0]
    onehot = (flat[:, None] == jnp.arange(EXPERTS, dtype=jnp.int32)[None, :]).astype(BF16)
    row = lax.broadcasted_iota(jnp.int32, (n, n), 0)
    col = lax.broadcasted_iota(jnp.int32, (n, n), 1)
    before = dot((col < row).astype(BF16), onehot, 1, 0)
    return jnp.sum(before * onehot.astype(F32), axis=1).astype(jnp.int32)


def place(parts, index_of, axis):
    size = parts[0].shape[axis]
    shape = list(parts[0].shape)
    shape[axis] = size * len(parts)
    out = jnp.zeros(shape, parts[0].dtype)
    for k, part in enumerate(parts):
        out = lax.dynamic_update_slice_in_dim(out, part, index_of(k) * size, axis)
    return out


def local(tokens, target, routes, gate_weights, counts, gate_proj, up_proj, down_proj, correction):
    nc = lax.axis_size("client")
    nm = lax.axis_size("expert")
    nz = lax.axis_size("zlo")
    c = lax.axis_index("client")
    m = lax.axis_index("expert")
    zl = lax.axis_index("zlo")
    q = lax.axis_index("core")
    ns = nz * CORES
    sub = zl * CORES + q
    units, wide = down_proj.shape
    quarter = units // nc
    tok = tokens.shape[1]
    top = routes.shape[2]
    cap = tok * top // EXPERTS
    few = cap // ns
    copies = nm // EXPERTS
    rows = nm * cap
    cols = wide // nz
    pair = nc // CORES
    step_size = 2.0 / (nm * ns * units // EXPERTS)

    def from_client(k):
        return (c - k) % nc

    weights = []
    for k in range(nc):
        to = (c + k) % nc * quarter
        block = jnp.concatenate([at(gate_proj, to, quarter, 0), at(up_proj, to, quarter, 0)], axis=0)
        weights.append(shift(block, "client", k) if k else block)
    weights = place(weights, from_client, 1)

    flat = routes[0].reshape(-1)
    rank = ranks(flat).reshape(tok, top)
    slot = routes[0] * cap + rank
    wanted = (
        jnp.arange(EXPERTS, dtype=jnp.int32)[:, None] * cap + sub * few + jnp.arange(few, dtype=jnp.int32)[None, :]
    ).reshape(-1)
    pick = jnp.zeros((EXPERTS * few, tok), BF16)
    for k in range(top):
        pick = pick + (slot[None, :, k] == wanted[:, None]).astype(BF16)
    sent = dot(pick, tokens[0], 1, 0).astype(BF16).reshape(EXPERTS, few, -1)
    sent = jnp.repeat(sent, copies, axis=0)
    features = lax.all_to_all(sent, "expert", 0, 0, tiled=True).reshape(nm * few, -1)
    features = lax.all_gather(features, ("client", "zlo", "core"), axis=0, tiled=True)

    pre = dot(weights, features, 1, 1)
    hidden = (jax.nn.silu(pre[:quarter]) * pre[quarter:]).astype(BF16)
    old = lax.broadcasted_iota(jnp.int32, (rows, rows), 0)
    new = lax.broadcasted_iota(jnp.int32, (rows, rows), 1)
    part, src, within = old // (nm * few), old // few % nm, old % few
    order = (src * cap + part * few + within == new).astype(BF16)
    hidden = jnp.concatenate(
        [dot(hidden[:, i * rows : (i + 1) * rows], order, 1, 0).astype(BF16) for i in range(nc)], axis=1
    )
    half = quarter // 2
    top_half, low_half = hidden[:half], hidden[half:]
    right_top = shift(top_half, "client", 1)
    left_low = shift(low_half, "client", -1)
    right_low = shift(low_half, "client", 1)
    left_top = shift(top_half, "client", -1)
    across_top = shift(right_top, "client", 1)
    across_low = shift(left_low, "client", -1)
    full = jnp.zeros((units, nc * rows), BF16)
    for k, upper, lower in ((0, top_half, low_half), (1, right_top, right_low), (2, across_top, across_low), (3, left_top, left_low)):
        full = lax.dynamic_update_slice_in_dim(full, upper, from_client(k) * quarter, 0)
        full = lax.dynamic_update_slice_in_dim(full, lower, from_client(k) * quarter + half, 0)

    def over_zlo(x):
        x = x.astype(BF16).reshape(x.shape[0], nz, x.shape[1] // nz).transpose(1, 0, 2)
        x = lax.all_to_all(x, "zlo", 0, 0, tiled=True)
        return jnp.sum(x.astype(F32), axis=0)

    own = at(full, c * rows, rows, 1)
    some = rows // CORES

    def products(core):
        value = dot(at(full, core * pair * rows, pair * rows, 1), down_proj, 0, 0)
        gram = dot(at(own, core * some, some, 1), own, 0, 0)
        return jnp.concatenate([value, gram], axis=0)

    give = products(1 - q).astype(BF16)
    got = shift(give, "core", 1)
    both = over_zlo(products(q) + got.astype(F32)).astype(BF16)

    def control_products(core):
        first = core * pair * wide
        return jnp.concatenate([dot(own, at(correction[0], first + a * wide, wide, 1), 0, 0) for a in range(pair)], axis=0)

    give = control_products(1 - q).astype(BF16)
    got = shift(give, "core", 1)
    control_move = (control_products(q) + got.astype(F32)).astype(BF16)
    control_move, _ = lax.optimization_barrier((control_move, both))
    totals = at(control_move, zl * cols, cols, 1).astype(F32)
    for k in range(1, nz):
        part = at(control_move, (zl + k) % nz * cols, cols, 1)
        part = shift(part, "zlo", k)
        totals = totals + part.astype(F32)
    control_move = totals

    odd = c % 2

    def hop(x):
        arrived = []
        for d in range(2):
            item = lax.dynamic_index_in_dim(x, odd ^ d, 0, keepdims=False)
            ends = [
                ((2 * p + e) * CORES + r, (2 * r + (e ^ d)) * CORES + p)
                for p in range(CORES)
                for e in range(2)
                for r in range(CORES)
            ]
            arrived.append(lax.ppermute(item, ("client", "core"), ends))
        arrived = jnp.stack(arrived)
        return jnp.stack([lax.dynamic_index_in_dim(arrived, odd ^ a, 0, keepdims=False) for a in range(2)])

    value = hop(both[: pair * rows].reshape(pair, rows, cols))
    value = value.transpose(1, 0, 2).reshape(rows, pair * cols)
    gram = both[pair * rows :]
    gram = [gram] + [shift(gram, "zlo", k) for k in range(1, nz)]
    gram = place(gram, lambda k: (zl - k) % nz, 1)
    other = shift(gram, "core", 1)
    gram = place([gram, other], lambda k: (q + k) % CORES, 0)
    control_move = control_move.reshape(pair, rows, cols).transpose(1, 0, 2).reshape(rows, pair * cols)

    share = counts.astype(F32) / jnp.sum(counts).astype(F32)
    control, _ = lax.optimization_barrier((correction[0], full))

    def control_to(k):
        return share[c] * at(control, (c + k) % nc * wide, wide, 1).astype(F32)

    mid = units // 2
    far = control_to(2).astype(BF16)
    from_left = shift(far[:mid], "client", 1)
    from_right = shift(far[mid:], "client", -1)
    to_right, to_left = control_to(1), control_to(3)
    to_right = jnp.concatenate([to_right[:mid] + from_left.astype(F32), to_right[mid:]], axis=0).astype(BF16)
    to_left = jnp.concatenate([to_left[:mid], to_left[mid:] + from_right.astype(F32)], axis=0).astype(BF16)
    from_left, from_right = shift(to_right, "client", 1), shift(to_left, "client", -1)
    control_sum = control_to(0) + from_left.astype(F32) + from_right.astype(F32)

    slots = jnp.arange(EXPERTS * cap, dtype=jnp.int32)
    combine = jnp.zeros((tok, EXPERTS * cap), F32)
    for k in range(top):
        combine = combine + jnp.where(slot[:, k][:, None] == slots[None, :], gate_weights[0, :, k][:, None], 0.0)
    positions = m * tok + jnp.arange(tok, dtype=jnp.int32)
    live = (positions < counts[c]).astype(F32)[:, None]
    goal = jnp.concatenate(
        [at(target[0], ((q * pair + a) * nz + zl) * cols, cols, 1) for a in range(pair)], axis=1
    ).astype(F32)

    def at_owner(x):
        x = x.astype(BF16).reshape(nm, cap, pair * cols)
        x = lax.all_to_all(x, "expert", 0, 0, tiled=True)
        x = jnp.sum(x.astype(F32).reshape(EXPERTS, copies, cap, pair * cols), axis=1)
        return dot(combine, x.reshape(EXPERTS * cap, pair * cols), 1, 0, precision=EXACT)

    def at_expert(x):
        x = dot(combine, x, 0, 0, precision=EXACT).astype(BF16).reshape(EXPERTS, cap, pair * cols)
        x = jnp.repeat(x, copies, axis=0)
        x = lax.all_to_all(x, "expert", 0, 0, tiled=True)
        return x.reshape(rows, pair * cols)

    residual = live * (at_owner(value) - goal)
    cotangent = at_expert(residual)
    change = dot(gram, cotangent, 1, 0) + control_move
    mean = share[c] * (residual - (step_size / LOCAL_STEPS) * live * at_owner(change))
    cotangent = at_expert(mean)

    cotangent = hop(cotangent.reshape(rows, pair, cols).transpose(1, 0, 2)).reshape(pair * rows, cols)
    cotangent = jnp.broadcast_to(cotangent[None], (nz, pair * rows, cols))
    cotangent = lax.all_to_all(cotangent, "zlo", 0, 0, tiled=True)
    cotangent = cotangent.transpose(1, 0, 2).reshape(pair * rows, wide)
    other = shift(cotangent, "core", 1)
    cotangent = place([cotangent, other], lambda k: (q + k) % CORES, 0)
    return dot(full, cotangent, 1, 0) + control_sum


def solution(mesh):
    nc, nm, ns = mesh.devices.shape
    grid = Mesh(mesh.devices.reshape(nc, nm, ns // CORES, CORES), ("client", "expert", "zlo", "core"))
    by_token = P("client", "expert", None)
    by_unit = P(("expert", "zlo", "core"), "client")
    return jax.shard_map(
        local,
        mesh=grid,
        in_specs=(
            by_token,
            by_token,
            by_token,
            by_token,
            P(),
            by_unit,
            by_unit,
            by_unit,
            P("client", ("expert", "zlo", "core"), None),
        ),
        out_specs=by_unit,
        check_vma=False,
    )
```

profile of v0, /device:TPU:1, one launch (start us, length us, event | category | flops | bytes accessed | tf_op | source)
XLA Modules:
  0.0 508.2 jit_solution(13521399652627804071)
XLA Ops:
  8.7 14.9 %all_to_all.35 = bf16[16,4,2048]{2,1,0:T(4,128)(2,1)S(1)} all-to-all(bf16[16,4,2048]{2,1,0:T(4,128)(2,1)S(1)} %bitcast.102), channel_id=1, replica_groups=mesh['client'=4,'expert'=16,'zlo'=4,'core'=2] {'expert'}, dimensions={0} | all-to-all | bytes 524288 | tf_op jit(solution)/shard_map/all_to_all | solution.py:92
  24.6 15.4 %collective-permute-start.1 = (bf16[224,512]{1,0:T(8,128)(2,1)S(1)}, bf16[224,512]{1,0:T(8,128)(2,1)S(1)}, u32[]{:S(2)}, u32[]{:S(2)}) collective-permute-start(bf16[224,512]{1,0:T(8,128)(2,1)S(1)} %pad_maximum_fusion.7), channel_id=1, source_target_pairs={{0,256},{128,384},{256,0},{384,128},{1,257},{129,385},{257,1},{385... | collective-permute-start | bytes 688136 | tf_op jit(solution)/shard_map/ppermute | solution.py:19
  40.1 4.0 collective-permute-start
  44.2 5.2 %collective-permute-start.2 = (bf16[224,512]{1,0:T(8,128)(2,1)S(1)}, bf16[224,512]{1,0:T(8,128)(2,1)S(1)}, u32[]{:S(2)}, u32[]{:S(2)}) collective-permute-start(bf16[224,512]{1,0:T(8,128)(2,1)S(1)} %pad_maximum_fusion.8), channel_id=1, source_target_pairs={{0,384},{128,0},{256,128},{384,256},{1,385},{129,1},{257,129},{385... | collective-permute-start | bytes 688136 | tf_op jit(solution)/shard_map/ppermute | solution.py:19
  50.7 28.4 %collective-permute-done = bf16[224,512]{1,0:T(8,128)(2,1)S(1)} collective-permute-done((bf16[224,512]{1,0:T(8,128)(2,1)S(1)}, bf16[224,512]{1,0:T(8,128)(2,1)S(1)}, u32[]{:S(2)}, u32[]{:S(2)}) %collective-permute-start) | collective-permute-done | bytes 229408 | tf_op jit(solution)/shard_map/ppermute | solution.py:19
  79.2 4.1 collective-permute-done.2
  83.3 51.5 %all-gather.2.cloned.1.call-done = bf16[2048,2048]{1,0:T(8,128)(2,1)} async-done(((bf16[64,2048]{1,0:T(8,128)(2,1)}), bf16[2048,2048]{1,0:T(8,128)(2,1)}) %all-gather.2.cloned.1.call-update) | async-done | bytes 8388624 | tf_op jit(solution)/shard_map/all_gather | solution.py:93
  134.8 6.0 %fusion.97 = f32[224,2048]{1,0:T(8,128)S(1)} fusion(bf16[224,2048]{1,0:T(8,128)(2,1)S(1)} %constant_dynamic-update-slice_fusion.16, bf16[2048,2048]{1,0:T(8,128)(2,1)} %all-gather.2.cloned.1.call-done), kind=kOutput, calls=%fused_computation.213 | convolution fusion | flops 1879048192 | bytes 11141120 | tf_op jit(solution)/shard_map/dot_general | solution.py:27
  142.6 4.9 collective-permute-start.4
  147.5 4.3 collective-permute-start.6
  151.8 4.9 collective-permute-start.3
  156.7 4.3 collective-permute-start.8
  161.0 20.4 %collective-permute-done.3 = bf16[56,2048]{1,0:T(8,128)(2,1)S(1)} collective-permute-done((bf16[56,2048]{1,0:T(8,128)(2,1)S(1)}, bf16[56,2048]{1,0:T(8,128)(2,1)S(1)}, u32[]{:S(2)}, u32[]{:S(2)}) %collective-permute-start.3) | collective-permute-done | bytes 229408 | tf_op jit(solution)/shard_map/ppermute | solution.py:19
  181.4 7.1 %collective-permute-start.5 = (bf16[56,2048]{1,0:T(8,128)(2,1)S(1)}, bf16[56,2048]{1,0:T(8,128)(2,1)S(1)}, u32[]{:S(2)}, u32[]{:S(2)}) collective-permute-start(bf16[56,2048]{1,0:T(8,128)(2,1)S(1)} %collective-permute-done.3), channel_id=1, source_target_pairs={{0,128},{128,256},{256,384},{384,0},{1,129},{129,257},{257,385},{3... | collective-permute-start | bytes 688136 | tf_op jit(solution)/shard_map/ppermute | solution.py:19
  188.5 2.1 collective-permute-start.7
  190.7 11.1 %collective-permute-done.5 = bf16[56,2048]{1,0:T(8,128)(2,1)S(1)} collective-permute-done((bf16[56,2048]{1,0:T(8,128)(2,1)S(1)}, bf16[56,2048]{1,0:T(8,128)(2,1)S(1)}, u32[]{:S(2)}, u32[]{:S(2)}) %collective-permute-start.5) | collective-permute-done | bytes 229408 | tf_op jit(solution)/shard_map/ppermute | solution.py:19
  201.8 5.9 %collective-permute-done.7 = bf16[56,2048]{1,0:T(8,128)(2,1)S(1)} collective-permute-done((bf16[56,2048]{1,0:T(8,128)(2,1)S(1)}, bf16[56,2048]{1,0:T(8,128)(2,1)S(1)}, u32[]{:S(2)}, u32[]{:S(2)}) %collective-permute-start.7) | collective-permute-done | bytes 229408 | tf_op jit(solution)/shard_map/ppermute | solution.py:19
  210.2 7.1 %collective-permute-start.9 = (bf16[1280,512]{1,0:T(8,128)(2,1)}, bf16[1280,512]{1,0:T(8,128)(2,1)}, u32[]{:S(2)}, u32[]{:S(2)}) collective-permute-start(bf16[1280,512]{1,0:T(8,128)(2,1)} %pad_maximum_fusion), channel_id=1, source_target_pairs={{0,1},{1,0},{2,3},{3,2},{4,5},{5,4},{6,7},{7,6},{8,9},{9,8},{10,11... | collective-permute-start | bytes 3932168 | tf_op jit(solution)/shard_map/ppermute | solution.py:19
  218.6 1.8 collective-permute-done.9
  220.3 2.7 bitcast_bitcast_fusion
  223.0 6.8 %all-to-all-start.1 = ((bf16[4,1280,128]{2,1,0:T(8,128)(2,1)}), bf16[4,1280,128]{2,1,0:T(8,128)(2,1)}, u32[]{:S(2)}, u32[]{:S(2)}) async-start(bf16[4,1280,128]{2,1,0:T(8,128)(2,1)} %bitcast_bitcast_fusion), calls=%async_computation.1 | async-start | bytes 2621440 | tf_op jit(solution)/shard_map/all_to_all | solution.py:119
  229.8 1.5 convolution_convert_fusion.3
  231.3 1.5 convolution_convert_fusion.2
  232.9 2.6 collective-permute-start.16
  240.1 1.5 fusion.24
  241.6 1.5 fusion.22
  243.1 1.6 fusion.1
  244.7 16.1 %all-to-all-done.1 = bf16[4,1280,128]{2,1,0:T(8,128)(2,1)} async-done(((bf16[4,1280,128]{2,1,0:T(8,128)(2,1)}), bf16[4,1280,128]{2,1,0:T(8,128)(2,1)}, u32[]{:S(2)}, u32[]{:S(2)}) %all-to-all-start.1) | async-done | bytes 1310752 | tf_op jit(solution)/shard_map/all_to_all | solution.py:119
  260.8 2.3 reduce_sum.50
  265.4 1.9 collective-permute-start.12
  267.3 3.3 collective-permute-start.13
  270.5 3.8 collective-permute-start.14
  275.4 9.5 %collective-permute-start.10 = (bf16[512,128]{1,0:T(8,128)(2,1)S(1)}, bf16[512,128]{1,0:T(8,128)(2,1)S(1)}, u32[]{:S(2)}, u32[]{:S(2)}) collective-permute-start(bf16[512,128]{1,0:T(8,128)(2,1)S(1)} %get-tuple-element.41), channel_id=1, source_target_pairs={{0,0},{1,256},{128,128},{129,384},{256,1},{257,257},{384,129},{385... | collective-permute-start | bytes 393224 | tf_op jit(solution)/shard_map/ppermute | solution.py:161
  284.9 3.4 collective-permute-start.11
  289.3 2.2 collective-permute-start.17
  292.1 8.3 %collective-permute-start.18 = (bf16[1024,128]{1,0:T(8,128)(2,1)}, bf16[1024,128]{1,0:T(8,128)(2,1)}, u32[]{:S(2)}, u32[]{:S(2)}) collective-permute-start(bf16[1024,128]{1,0:T(8,128)(2,1)} %get-tuple-element.16), channel_id=1, source_target_pairs={{0,4},{2,6},{4,0},{6,2},{1,5},{3,7},{5,1},{7,3},{8,12},{10,14},{12... | collective-permute-start | bytes 786440 | tf_op jit(solution)/shard_map/ppermute | solution.py:19
  300.4 2.1 collective-permute-start.19
  303.6 1.8 reshape_reshape.6
  305.5 4.2 all-to-all-start.2
  309.7 1.5 constant_dynamic-update-slice_fusion.5
  311.8 1.9 collective-permute-start.15
  314.6 1.7 constant_dynamic-update-slice_fusion.3
  320.7 5.6 %all-to-all-start.3 = ((bf16[16,32,256]{2,1,0:T(8,128)(2,1)}), bf16[16,32,256]{2,1,0:T(8,128)(2,1)}, u32[]{:S(2)}, u32[]{:S(2)}) async-start(bf16[16,32,256]{2,1,0:T(8,128)(2,1)} %bitcast.99), calls=%async_computation.3 | async-start | bytes 524288 | tf_op jit(solution)/shard_map/all_to_all | solution.py:209
  328.0 1.7 constant_dynamic-update-slice_fusion.2
  329.6 4.7 all-to-all-done.3
  334.3 2.1 fusion.3
  336.4 3.5 all-to-all-start.4
  341.2 6.3 %all-to-all-done.4 = bf16[16,32,256]{2,1,0:T(8,128)(2,1)S(1)} async-done(((bf16[16,32,256]{2,1,0:T(8,128)(2,1)}), bf16[16,32,256]{2,1,0:T(8,128)(2,1)S(1)}, u32[]{:S(2)}, u32[]{:S(2)}) %all-to-all-start.4) | async-done | bytes 262176 | tf_op jit(solution)/shard_map/all_to_all | solution.py:202
  349.1 10.5 %all_to_all.36 = bf16[16,32,256]{2,1,0:T(8,128)(2,1)S(1)} all-to-all(bf16[16,32,256]{2,1,0:T(8,128)(2,1)S(1)} %bitcast.103), channel_id=1, replica_groups=mesh['client'=4,'expert'=16,'zlo'=4,'core'=2] {'expert'}, dimensions={0} | all-to-all | bytes 524288 | tf_op jit(solution)/shard_map/all_to_all | solution.py:209
  360.2 15.9 %collective-permute-start.20 = (bf16[512,128]{1,0:T(8,128)(2,1)S(1)}, bf16[512,128]{1,0:T(8,128)(2,1)S(1)}, u32[]{:S(2)}, u32[]{:S(2)}) collective-permute-start(bf16[512,128]{1,0:T(8,128)(2,1)S(1)} %bitcast.105), channel_id=1, source_target_pairs={{0,0},{1,256},{128,128},{129,384},{256,1},{257,257},{384,129},{385... | collective-permute-start | bytes 393224 | tf_op jit(solution)/shard_map/ppermute | solution.py:161
  376.2 3.0 collective-permute-start.21
  379.3 9.8 %collective-permute-done.21 = bf16[512,128]{1,0:T(8,128)(2,1)S(1)} collective-permute-done((bf16[512,128]{1,0:T(8,128)(2,1)S(1)}, bf16[512,128]{1,0:T(8,128)(2,1)S(1)}, u32[]{:S(2)}, u32[]{:S(2)}) %collective-permute-start.21) | collective-permute-done | bytes 131104 | tf_op jit(solution)/shard_map/ppermute | solution.py:161
  390.4 8.2 %all-to-all-start.6 = ((bf16[4,1024,128]{2,1,0:T(8,128)(2,1)}), bf16[4,1024,128]{2,1,0:T(8,128)(2,1)}, u32[]{:S(2)}, u32[]{:S(2)}) async-start(bf16[4,1024,128]{2,1,0:T(8,128)(2,1)} %broadcast_in_dim.73), calls=%async_computation.6 | async-start | bytes 2097152 | tf_op jit(solution)/shard_map/all_to_all | solution.py:220
  398.6 2.2 convert_multiply_fusion.1
  401.7 7.2 %collective-permute-start.23 = (bf16[224,512]{1,0:T(8,128)(2,1)}, bf16[224,512]{1,0:T(8,128)(2,1)}, u32[]{:S(2)}, u32[]{:S(2)}) collective-permute-start(bf16[224,512]{1,0:T(8,128)(2,1)} %get-tuple-element.19), channel_id=1, source_target_pairs={{0,128},{128,256},{256,384},{384,0},{1,129},{129,257},{257,385},{3... | collective-permute-start | bytes 688136 | tf_op jit(solution)/shard_map/ppermute | solution.py:19
  409.7 1.9 collective-permute-start.25
  412.3 23.7 %all-to-all-done.6 = bf16[4,1024,128]{2,1,0:T(8,128)(2,1)} async-done(((bf16[4,1024,128]{2,1,0:T(8,128)(2,1)}), bf16[4,1024,128]{2,1,0:T(8,128)(2,1)}, u32[]{:S(2)}, u32[]{:S(2)}) %all-to-all-start.6) | async-done | bytes 1048608 | tf_op jit(solution)/shard_map/all_to_all | solution.py:220
  437.5 2.1 collective-permute-start.22
  440.7 1.7 pad_maximum_fusion.3
  442.5 8.2 %collective-permute-start.24 = (bf16[448,512]{1,0:T(8,128)(2,1)}, bf16[448,512]{1,0:T(8,128)(2,1)}, u32[]{:S(2)}, u32[]{:S(2)}) collective-permute-start(bf16[448,512]{1,0:T(8,128)(2,1)} %pad_maximum_fusion.3), channel_id=1, source_target_pairs={{0,128},{128,256},{256,384},{384,0},{1,129},{129,257},{257,385},{3... | collective-permute-start | bytes 1376264 | tf_op jit(solution)/shard_map/ppermute | solution.py:19
  452.5 1.9 collective-permute-start.26
  456.1 30.6 %collective-permute-done.24 = bf16[448,512]{1,0:T(8,128)(2,1)} collective-permute-done((bf16[448,512]{1,0:T(8,128)(2,1)}, bf16[448,512]{1,0:T(8,128)(2,1)}, u32[]{:S(2)}, u32[]{:S(2)}) %collective-permute-start.24) | collective-permute-done | bytes 458784 | tf_op jit(solution)/shard_map/ppermute | solution.py:19
  486.8 10.5 %collective-permute-done.26 = bf16[448,512]{1,0:T(8,128)(2,1)} collective-permute-done((bf16[448,512]{1,0:T(8,128)(2,1)}, bf16[448,512]{1,0:T(8,128)(2,1)}, u32[]{:S(2)}, u32[]{:S(2)}) %collective-permute-start.26) | collective-permute-done | bytes 458784 | tf_op jit(solution)/shard_map/ppermute | solution.py:19
  497.3 4.0 convolution_add_fusion
  (139 shorter events, 40.2 us)
Async XLA Ops:
  6.5 1.8 copy-start
  6.5 18.0 %copy-start.6 = (bf16[448,512]{1,0:T(8,128)(2,1)S(1)}, bf16[448,512]{1,0:T(8,128)(2,1)}, u32[]{:S(2)}) copy-start(bf16[448,512]{1,0:T(8,128)(2,1)} %param.14) | copy-start | bytes 1376260
  6.5 18.0 %copy-start.5 = (bf16[448,512]{1,0:T(8,128)(2,1)S(1)}, bf16[448,512]{1,0:T(8,128)(2,1)}, u32[]{:S(2)}) copy-start(bf16[448,512]{1,0:T(8,128)(2,1)} %param.15) | copy-start | bytes 1376260
  6.5 128.3 %all-gather.2.cloned.1.call-start = ((), (), s32[]{:S(2)}) async-start(), calls=%async_computation.7 | async-start | bytes 8650752 | tf_op jit(solution)/shard_map/all_gather | solution.py:93
  24.6 54.5 %collective-permute-start.1 = (bf16[224,512]{1,0:T(8,128)(2,1)S(1)}, bf16[224,512]{1,0:T(8,128)(2,1)S(1)}, u32[]{:S(2)}, u32[]{:S(2)}) collective-permute-start(bf16[224,512]{1,0:T(8,128)(2,1)S(1)} %pad_maximum_fusion.7), channel_id=1, source_target_pairs={{0,256},{128,384},{256,0},{384,128},{1,257},{129,385},{257,1},{385... | collective-permute-start | bytes 688136 | tf_op jit(solution)/shard_map/ppermute | solution.py:19
  40.1 39.0 %collective-permute-start = (bf16[224,512]{1,0:T(8,128)(2,1)S(1)}, bf16[224,512]{1,0:T(8,128)(2,1)S(1)}, u32[]{:S(2)}, u32[]{:S(2)}) collective-permute-start(bf16[224,512]{1,0:T(8,128)(2,1)S(1)} %pad_maximum_fusion.6), channel_id=1, source_target_pairs={{0,128},{128,256},{256,384},{384,0},{1,129},{129,257},{257,385},{3... | collective-permute-start | bytes 688136 | tf_op jit(solution)/shard_map/ppermute | solution.py:19
  44.2 39.1 %collective-permute-start.2 = (bf16[224,512]{1,0:T(8,128)(2,1)S(1)}, bf16[224,512]{1,0:T(8,128)(2,1)S(1)}, u32[]{:S(2)}, u32[]{:S(2)}) collective-permute-start(bf16[224,512]{1,0:T(8,128)(2,1)S(1)} %pad_maximum_fusion.8), channel_id=1, source_target_pairs={{0,384},{128,0},{256,128},{384,256},{1,385},{129,1},{257,129},{385... | collective-permute-start | bytes 688136 | tf_op jit(solution)/shard_map/ppermute | solution.py:19
  142.6 48.1 %collective-permute-start.4 = (bf16[56,2048]{1,0:T(8,128)(2,1)S(1)}, bf16[56,2048]{1,0:T(8,128)(2,1)S(1)}, u32[]{:S(2)}, u32[]{:S(2)}) collective-permute-start(bf16[56,2048]{1,0:T(8,128)(2,1)S(1)} %get-tuple-element.21), channel_id=1, source_target_pairs={{0,128},{128,256},{256,384},{384,0},{1,129},{129,257},{257,385},{3... | collective-permute-start | bytes 688136 | tf_op jit(solution)/shard_map/ppermute | solution.py:19
  147.5 41.0 %collective-permute-start.6 = (bf16[56,2048]{1,0:T(8,128)(2,1)S(1)}, bf16[56,2048]{1,0:T(8,128)(2,1)S(1)}, u32[]{:S(2)}, u32[]{:S(2)}) collective-permute-start(bf16[56,2048]{1,0:T(8,128)(2,1)S(1)} %get-tuple-element.21), channel_id=1, source_target_pairs={{0,384},{128,0},{256,128},{384,256},{1,385},{129,1},{257,129},{385... | collective-permute-start | bytes 688136 | tf_op jit(solution)/shard_map/ppermute | solution.py:19
  151.8 29.6 %collective-permute-start.3 = (bf16[56,2048]{1,0:T(8,128)(2,1)S(1)}, bf16[56,2048]{1,0:T(8,128)(2,1)S(1)}, u32[]{:S(2)}, u32[]{:S(2)}) collective-permute-start(bf16[56,2048]{1,0:T(8,128)(2,1)S(1)} %get-tuple-element.23), channel_id=1, source_target_pairs={{0,128},{128,256},{256,384},{384,0},{1,129},{129,257},{257,385},{3... | collective-permute-start | bytes 688136 | tf_op jit(solution)/shard_map/ppermute | solution.py:19
  156.7 51.0 %collective-permute-start.8 = (bf16[56,2048]{1,0:T(8,128)(2,1)S(1)}, bf16[56,2048]{1,0:T(8,128)(2,1)S(1)}, u32[]{:S(2)}, u32[]{:S(2)}) collective-permute-start(bf16[56,2048]{1,0:T(8,128)(2,1)S(1)} %get-tuple-element.23), channel_id=1, source_target_pairs={{0,384},{128,0},{256,128},{384,256},{1,385},{129,1},{257,129},{385... | collective-permute-start | bytes 688136 | tf_op jit(solution)/shard_map/ppermute | solution.py:19
  161.0 47.2 %copy-start.7 = (bf16[448,512]{1,0:T(8,128)(2,1)S(1)}, bf16[448,512]{1,0:T(8,128)(2,1)}, u32[]{:S(2)}) copy-start(bf16[448,512]{1,0:T(8,128)(2,1)} %param.16) | copy-start | bytes 1376260
  181.4 20.3 %collective-permute-start.5 = (bf16[56,2048]{1,0:T(8,128)(2,1)S(1)}, bf16[56,2048]{1,0:T(8,128)(2,1)S(1)}, u32[]{:S(2)}, u32[]{:S(2)}) collective-permute-start(bf16[56,2048]{1,0:T(8,128)(2,1)S(1)} %collective-permute-done.3), channel_id=1, source_target_pairs={{0,128},{128,256},{256,384},{384,0},{1,129},{129,257},{257,385},{3... | collective-permute-start | bytes 688136 | tf_op jit(solution)/shard_map/ppermute | solution.py:19
  188.5 19.1 %collective-permute-start.7 = (bf16[56,2048]{1,0:T(8,128)(2,1)S(1)}, bf16[56,2048]{1,0:T(8,128)(2,1)S(1)}, u32[]{:S(2)}, u32[]{:S(2)}) collective-permute-start(bf16[56,2048]{1,0:T(8,128)(2,1)S(1)} %collective-permute-done.6), channel_id=1, source_target_pairs={{0,384},{128,0},{256,128},{384,256},{1,385},{129,1},{257,129},{385... | collective-permute-start | bytes 688136 | tf_op jit(solution)/shard_map/ppermute | solution.py:19
  210.2 10.1 %collective-permute-start.9 = (bf16[1280,512]{1,0:T(8,128)(2,1)}, bf16[1280,512]{1,0:T(8,128)(2,1)}, u32[]{:S(2)}, u32[]{:S(2)}) collective-permute-start(bf16[1280,512]{1,0:T(8,128)(2,1)} %pad_maximum_fusion), channel_id=1, source_target_pairs={{0,1},{1,0},{2,3},{3,2},{4,5},{5,4},{6,7},{7,6},{8,9},{9,8},{10,11... | collective-permute-start | bytes 3932168 | tf_op jit(solution)/shard_map/ppermute | solution.py:19
  223.0 37.8 %all-to-all-start.1 = ((bf16[4,1280,128]{2,1,0:T(8,128)(2,1)}), bf16[4,1280,128]{2,1,0:T(8,128)(2,1)}, u32[]{:S(2)}, u32[]{:S(2)}) async-start(bf16[4,1280,128]{2,1,0:T(8,128)(2,1)} %bitcast_bitcast_fusion), calls=%async_computation.1 | async-start | bytes 2621440 | tf_op jit(solution)/shard_map/all_to_all | solution.py:119
  231.3 4.3 copy-start.9
  231.3 8.8 %copy-start.8 = (f32[1,128,2]{1,2,0:T(2,128)S(1)}, f32[1,128,2]{1,2,0:T(2,128)}, u32[]{:S(2)}) copy-start(f32[1,128,2]{1,2,0:T(2,128)} %param.12) | copy-start | bytes 3076
  232.9 10.2 %collective-permute-start.16 = (bf16[1024,512]{1,0:T(8,128)(2,1)S(1)}, bf16[1024,512]{1,0:T(8,128)(2,1)}, u32[]{:S(2)}, u32[]{:S(2)}) collective-permute-start(bf16[1024,512]{1,0:T(8,128)(2,1)S(1)} %pad_maximum_fusion.1), channel_id=1, source_target_pairs={{0,1},{1,0},{2,3},{3,2},{4,5},{5,4},{6,7},{7,6},{8,9},{9,8},{10,11... | collective-permute-start | bytes 3145736 | tf_op jit(solution)/shard_map/ppermute | solution.py:19
  265.4 23.9 %collective-permute-start.12 = (bf16[256,128]{1,0:T(8,128)(2,1)S(1)}, bf16[256,128]{1,0:T(8,128)(2,1)S(1)}, u32[]{:S(2)}, u32[]{:S(2)}) collective-permute-start(bf16[256,128]{1,0:T(8,128)(2,1)S(1)} %get-tuple-element.32), channel_id=1, source_target_pairs={{0,2},{2,4},{4,6},{6,0},{1,3},{3,5},{5,7},{7,1},{8,10},{10,12},{12... | collective-permute-start | bytes 196616 | tf_op jit(solution)/shard_map/ppermute | solution.py:19
  267.3 42.4 %collective-permute-start.13 = (bf16[256,128]{1,0:T(8,128)(2,1)S(1)}, bf16[256,128]{1,0:T(8,128)(2,1)}, u32[]{:S(2)}, u32[]{:S(2)}) collective-permute-start(bf16[256,128]{1,0:T(8,128)(2,1)S(1)} %get-tuple-element.32), channel_id=1, source_target_pairs={{0,4},{2,6},{4,0},{6,2},{1,5},{3,7},{5,1},{7,3},{8,12},{10,14},{12... | collective-permute-start | bytes 196616 | tf_op jit(solution)/shard_map/ppermute | solution.py:19
  270.5 40.7 %collective-permute-start.14 = (bf16[256,128]{1,0:T(8,128)(2,1)S(1)}, bf16[256,128]{1,0:T(8,128)(2,1)S(1)}, u32[]{:S(2)}, u32[]{:S(2)}) collective-permute-start(bf16[256,128]{1,0:T(8,128)(2,1)S(1)} %get-tuple-element.32), channel_id=1, source_target_pairs={{0,6},{2,0},{4,2},{6,4},{1,7},{3,1},{5,3},{7,5},{8,14},{10,8},{12,... | collective-permute-start | bytes 196616 | tf_op jit(solution)/shard_map/ppermute | solution.py:19
  275.4 16.7 %collective-permute-start.10 = (bf16[512,128]{1,0:T(8,128)(2,1)S(1)}, bf16[512,128]{1,0:T(8,128)(2,1)S(1)}, u32[]{:S(2)}, u32[]{:S(2)}) collective-permute-start(bf16[512,128]{1,0:T(8,128)(2,1)S(1)} %get-tuple-element.41), channel_id=1, source_target_pairs={{0,0},{1,256},{128,128},{129,384},{256,1},{257,257},{384,129},{385... | collective-permute-start | bytes 393224 | tf_op jit(solution)/shard_map/ppermute | solution.py:161
  284.9 15.5 %collective-permute-start.11 = (bf16[512,128]{1,0:T(8,128)(2,1)S(1)}, bf16[512,128]{1,0:T(8,128)(2,1)S(1)}, u32[]{:S(2)}, u32[]{:S(2)}) collective-permute-start(bf16[512,128]{1,0:T(8,128)(2,1)S(1)} %get-tuple-element.40), channel_id=1, source_target_pairs={{0,128},{1,384},{128,0},{129,256},{256,129},{257,385},{384,1},{385... | collective-permute-start | bytes 393224 | tf_op jit(solution)/shard_map/ppermute | solution.py:161
  289.3 37.0 %collective-permute-start.17 = (bf16[1024,128]{1,0:T(8,128)(2,1)}, bf16[1024,128]{1,0:T(8,128)(2,1)}, u32[]{:S(2)}, u32[]{:S(2)}) collective-permute-start(bf16[1024,128]{1,0:T(8,128)(2,1)} %get-tuple-element.14), channel_id=1, source_target_pairs={{0,2},{2,4},{4,6},{6,0},{1,3},{3,5},{5,7},{7,1},{8,10},{10,12},{12... | collective-permute-start | bytes 786440 | tf_op jit(solution)/shard_map/ppermute | solution.py:19
  292.1 34.1 %collective-permute-start.18 = (bf16[1024,128]{1,0:T(8,128)(2,1)}, bf16[1024,128]{1,0:T(8,128)(2,1)}, u32[]{:S(2)}, u32[]{:S(2)}) collective-permute-start(bf16[1024,128]{1,0:T(8,128)(2,1)} %get-tuple-element.16), channel_id=1, source_target_pairs={{0,4},{2,6},{4,0},{6,2},{1,5},{3,7},{5,1},{7,3},{8,12},{10,14},{12... | collective-permute-start | bytes 786440 | tf_op jit(solution)/shard_map/ppermute | solution.py:19
  300.4 25.9 %collective-permute-start.19 = (bf16[1024,128]{1,0:T(8,128)(2,1)}, bf16[1024,128]{1,0:T(8,128)(2,1)}, u32[]{:S(2)}, u32[]{:S(2)}) collective-permute-start(bf16[1024,128]{1,0:T(8,128)(2,1)} %get-tuple-element.15), channel_id=1, source_target_pairs={{0,6},{2,0},{4,2},{6,4},{1,7},{3,1},{5,3},{7,5},{8,14},{10,8},{12,... | collective-permute-start | bytes 786440 | tf_op jit(solution)/shard_map/ppermute | solution.py:19
  305.5 11.7 %all-to-all-start.2 = ((bf16[16,32,256]{2,1,0:T(8,128)(2,1)}), bf16[16,32,256]{2,1,0:T(8,128)(2,1)}, u32[]{:S(2)}, u32[]{:S(2)}) async-start(bf16[16,32,256]{2,1,0:T(8,128)(2,1)} %reshape_reshape.6), calls=%async_computation.2 | async-start | bytes 524288 | tf_op jit(solution)/shard_map/all_to_all | solution.py:202
  311.8 16.1 %collective-permute-start.15 = (bf16[256,512]{1,0:T(8,128)(2,1)}, bf16[256,512]{1,0:T(8,128)(2,1)}, u32[]{:S(2)}, u32[]{:S(2)}) collective-permute-start(bf16[256,512]{1,0:T(8,128)(2,1)} %constant_dynamic-update-slice_fusion.4), channel_id=1, source_target_pairs={{0,1},{1,0},{2,3},{3,2},{4,5},{5,4},{6,7},{7,6},{8,9},{9,8},{10,11... | collective-permute-start | bytes 786440 | tf_op jit(solution)/shard_map/ppermute | solution.py:19
  320.7 13.7 %all-to-all-start.3 = ((bf16[16,32,256]{2,1,0:T(8,128)(2,1)}), bf16[16,32,256]{2,1,0:T(8,128)(2,1)}, u32[]{:S(2)}, u32[]{:S(2)}) async-start(bf16[16,32,256]{2,1,0:T(8,128)(2,1)} %bitcast.99), calls=%async_computation.3 | async-start | bytes 524288 | tf_op jit(solution)/shard_map/all_to_all | solution.py:209
  327.5 12.4 %copy-start.10 = (s32[4]{0:T(128)S(1)}, s32[4]{0:T(128)}, u32[]{:S(2)}) copy-start(s32[4]{0:T(128)} %param.13) | copy-start | bytes 52
  336.4 11.1 %all-to-all-start.4 = ((bf16[16,32,256]{2,1,0:T(8,128)(2,1)}), bf16[16,32,256]{2,1,0:T(8,128)(2,1)S(1)}, u32[]{:S(2)}, u32[]{:S(2)}) async-start(bf16[16,32,256]{2,1,0:T(8,128)(2,1)} %bitcast.27), calls=%async_computation.4 | async-start | bytes 524288 | tf_op jit(solution)/shard_map/all_to_all | solution.py:202
  360.2 19.0 %collective-permute-start.20 = (bf16[512,128]{1,0:T(8,128)(2,1)S(1)}, bf16[512,128]{1,0:T(8,128)(2,1)S(1)}, u32[]{:S(2)}, u32[]{:S(2)}) collective-permute-start(bf16[512,128]{1,0:T(8,128)(2,1)S(1)} %bitcast.105), channel_id=1, source_target_pairs={{0,0},{1,256},{128,128},{129,384},{256,1},{257,257},{384,129},{385... | collective-permute-start | bytes 393224 | tf_op jit(solution)/shard_map/ppermute | solution.py:161
  376.2 12.9 %collective-permute-start.21 = (bf16[512,128]{1,0:T(8,128)(2,1)S(1)}, bf16[512,128]{1,0:T(8,128)(2,1)S(1)}, u32[]{:S(2)}, u32[]{:S(2)}) collective-permute-start(bf16[512,128]{1,0:T(8,128)(2,1)S(1)} %bitcast.106), channel_id=1, source_target_pairs={{0,128},{1,384},{128,0},{129,256},{256,129},{257,385},{384,1},{385... | collective-permute-start | bytes 393224 | tf_op jit(solution)/shard_map/ppermute | solution.py:161
  390.4 45.7 %all-to-all-start.6 = ((bf16[4,1024,128]{2,1,0:T(8,128)(2,1)}), bf16[4,1024,128]{2,1,0:T(8,128)(2,1)}, u32[]{:S(2)}, u32[]{:S(2)}) async-start(bf16[4,1024,128]{2,1,0:T(8,128)(2,1)} %broadcast_in_dim.73), calls=%async_computation.6 | async-start | bytes 2097152 | tf_op jit(solution)/shard_map/all_to_all | solution.py:220
  400.8 8.1 %copy-start.1 = (f32[448,512]{1,0:T(8,128)}, f32[448,512]{1,0:T(8,128)S(1)}, u32[]{:S(2)}) copy-start(f32[448,512]{1,0:T(8,128)S(1)} %get-tuple-element.11) | copy-start | bytes 2752516
  400.8 10.8 %copy-start.2 = (f32[448,512]{1,0:T(8,128)}, f32[448,512]{1,0:T(8,128)S(1)}, u32[]{:S(2)}) copy-start(f32[448,512]{1,0:T(8,128)S(1)} %get-tuple-element.12) | copy-start | bytes 2752516
  401.7 37.9 %collective-permute-start.23 = (bf16[224,512]{1,0:T(8,128)(2,1)}, bf16[224,512]{1,0:T(8,128)(2,1)}, u32[]{:S(2)}, u32[]{:S(2)}) collective-permute-start(bf16[224,512]{1,0:T(8,128)(2,1)} %get-tuple-element.19), channel_id=1, source_target_pairs={{0,128},{128,256},{256,384},{384,0},{1,129},{129,257},{257,385},{3... | collective-permute-start | bytes 688136 | tf_op jit(solution)/shard_map/ppermute | solution.py:19
  409.7 41.0 %collective-permute-start.25 = (bf16[224,512]{1,0:T(8,128)(2,1)}, bf16[224,512]{1,0:T(8,128)(2,1)}, u32[]{:S(2)}, u32[]{:S(2)}) collective-permute-start(bf16[224,512]{1,0:T(8,128)(2,1)} %get-tuple-element.20), channel_id=1, source_target_pairs={{0,384},{128,0},{256,128},{384,256},{1,385},{129,1},{257,129},{385... | collective-permute-start | bytes 688136 | tf_op jit(solution)/shard_map/ppermute | solution.py:19
  437.5 13.2 %copy-start.3 = (f32[448,512]{1,0:T(8,128)S(1)}, f32[448,512]{1,0:T(8,128)}, u32[]{:S(2)}) copy-start(f32[448,512]{1,0:T(8,128)} %copy-done.2) | copy-start | bytes 2752516
  437.5 14.2 %copy-start.4 = (bf16[224,512]{1,0:T(8,128)(2,1)S(1)}, bf16[224,512]{1,0:T(8,128)(2,1)}, u32[]{:S(2)}) copy-start(bf16[224,512]{1,0:T(8,128)(2,1)} %slice.129) | copy-start | bytes 688132
  437.5 17.3 %collective-permute-start.22 = (bf16[1024,512]{0,1:T(8,128)(2,1)S(1)}, bf16[1024,512]{0,1:T(8,128)(2,1)}, u32[]{:S(2)}, u32[]{:S(2)}) collective-permute-start(bf16[1024,512]{0,1:T(8,128)(2,1)S(1)} %bitcast.92), channel_id=1, source_target_pairs={{0,1},{1,0},{2,3},{3,2},{4,5},{5,4},{6,7},{7,6},{8,9},{9,8},{10,11... | collective-permute-start | bytes 3145736 | tf_op jit(solution)/shard_map/ppermute | solution.py:19
  442.5 44.3 %collective-permute-start.24 = (bf16[448,512]{1,0:T(8,128)(2,1)}, bf16[448,512]{1,0:T(8,128)(2,1)}, u32[]{:S(2)}, u32[]{:S(2)}) collective-permute-start(bf16[448,512]{1,0:T(8,128)(2,1)} %pad_maximum_fusion.3), channel_id=1, source_target_pairs={{0,128},{128,256},{256,384},{384,0},{1,129},{129,257},{257,385},{3... | collective-permute-start | bytes 1376264 | tf_op jit(solution)/shard_map/ppermute | solution.py:19
  452.5 44.8 %collective-permute-start.26 = (bf16[448,512]{1,0:T(8,128)(2,1)}, bf16[448,512]{1,0:T(8,128)(2,1)}, u32[]{:S(2)}, u32[]{:S(2)}) collective-permute-start(bf16[448,512]{1,0:T(8,128)(2,1)} %pad_maximum_fusion.4), channel_id=1, source_target_pairs={{0,384},{128,0},{256,128},{384,256},{1,385},{129,1},{257,129},{385... | collective-permute-start | bytes 1376264 | tf_op jit(solution)/shard_map/ppermute | solution.py:19
Sparse Core Ops, SparseCore 0:
  24.6 110.2 all-gather.1
where the time goes:
time: 510 us; the launch traced here: 508 us
  waiting for transfers between devices  226 us (44%)
  starting transfers between devices  167 us (33%)
  local copies, waits for them, and re-layouts  28 us (5%)
  blocking collectives  25.4 us (5%)
  matrix products  25.2 us (5%)
  other arithmetic  21.3 us (4%)
  between operations  15.5 us (3%)
    ppermute x23, waiting for transfers between devices, shift(): return lax.ppermute(x, axis, [(i, (i + by) % n) for i in range(n)])  113 us
    ppermute x23, starting transfers between devices, shift(): return lax.ppermute(x, axis, [(i, (i + by) % n) for i in range(n)])  107 us
    all_gather x1, waiting for transfers between devices, local(): lax.all_gather(features, ('client', 'zlo', 'core'), axis=0, tiled=True)  51.5 us
    ppermute x4, starting transfers between devices, hop(): arrived.append(lax.ppermute(item, ('client', 'core'), ends))  31.9 us
    dot_general x21, matrix products, dot(): lax.dot_general(a, b, (((da,), (db,)), ((), ())), preferred_element_type=...  25.2 us
    all_to_all x1, waiting for transfers between devices, local(): cotangent = lax.all_to_all(cotangent, 'zlo', 0, 0, tiled=True)  23.7 us
    all_to_all x1, waiting for transfers between devices, over_zlo(): x = lax.all_to_all(x, 'zlo', 0, 0, tiled=True)  16.1 us
    all_to_all x1, blocking collectives, local(): lax.all_to_all(sent, 'expert', 0, 0, tiled=True).reshape(nm * few, -1)  14.9 us
  transfers between devices with their start and end apart: 33, of which 15 were waited for; matrix products, arithmetic and copies ran while one was open for 9% of the time, Pallas kernels for 0%

commit v1 on v0

--- a/solution.py
+++ b/solution.py
@@ -71,6 +71,22 @@
     def from_client(k):
         return (c - k) % nc
 
+    odd = c % 2
+
+    def hop(x):
+        arrived = []
+        for d in range(2):
+            item = lax.dynamic_index_in_dim(x, odd ^ d, 0, keepdims=False)
+            ends = [
+                ((2 * p + e) * CORES + r, (2 * r + (e ^ d)) * CORES + p)
+                for p in range(CORES)
+                for e in range(2)
+                for r in range(CORES)
+            ]
+            arrived.append(lax.ppermute(item, ("client", "core"), ends))
+        arrived = jnp.stack(arrived)
+        return jnp.stack([lax.dynamic_index_in_dim(arrived, odd ^ a, 0, keepdims=False) for a in range(2)])
+
     weights = []
     for k in range(nc):
         to = (c + k) % nc * quarter
@@ -131,97 +147,71 @@
     got = shift(give, "core", 1)
     both = over_zlo(products(q) + got.astype(F32)).astype(BF16)
 
-    def control_products(core):
-        first = core * pair * wide
-        return jnp.concatenate([dot(own, at(correction[0], first + a * wide, wide, 1), 0, 0) for a in range(pair)], axis=0)
-
-    give = control_products(1 - q).astype(BF16)
-    got = shift(give, "core", 1)
-    control_move = (control_products(q) + got.astype(F32)).astype(BF16)
-    control_move, _ = lax.optimization_barrier((control_move, both))
-    totals = at(control_move, zl * cols, cols, 1).astype(F32)
-    for k in range(1, nz):
-        part = at(control_move, (zl + k) % nz * cols, cols, 1)
-        part = shift(part, "zlo", k)
-        totals = totals + part.astype(F32)
-    control_move = totals
-
-    odd = c % 2
-
-    def hop(x):
-        arrived = []
-        for d in range(2):
-            item = lax.dynamic_index_in_dim(x, odd ^ d, 0, keepdims=False)
-            ends = [
-                ((2 * p + e) * CORES + r, (2 * r + (e ^ d)) * CORES + p)
-                for p in range(CORES)
-                for e in range(2)
-                for r in range(CORES)
-            ]
-            arrived.append(lax.ppermute(item, ("client", "core"), ends))
-        arrived = jnp.stack(arrived)
-        return jnp.stack([lax.dynamic_index_in_dim(arrived, odd ^ a, 0, keepdims=False) for a in range(2)])
-
-    value = hop(both[: pair * rows].reshape(pair, rows, cols))
-    value = value.transpose(1, 0, 2).reshape(rows, pair * cols)
+    control = correction[0].reshape(units, CORES, pair, nz, cols).transpose(0, 3, 1, 2, 4).reshape(units, wide * nc)
+    control_move = jnp.concatenate(
+        [dot(own, control[:, k * pair * cols : (k + 1) * pair * cols], 0, 0).astype(BF16) for k in range(ns)], axis=0
+    )
+    control_move = lax.psum_scatter(control_move, ("zlo", "core"), scatter_dimension=0, tiled=True)
+
     gram = both[pair * rows :]
     gram = [gram] + [shift(gram, "zlo", k) for k in range(1, nz)]
     gram = place(gram, lambda k: (zl - k) % nz, 1)
     other = shift(gram, "core", 1)
     gram = place([gram, other], lambda k: (q + k) % CORES, 0)
-    control_move = control_move.reshape(pair, rows, cols).transpose(1, 0, 2).reshape(rows, pair * cols)
 
     share = counts.astype(F32) / jnp.sum(counts).astype(F32)
-    control, _ = lax.optimization_barrier((correction[0], full))
-
-    def control_to(k):
-        return share[c] * at(control, (c + k) % nc * wide, wide, 1).astype(F32)
-
-    mid = units // 2
-    far = control_to(2).astype(BF16)
-    from_left = shift(far[:mid], "client", 1)
-    from_right = shift(far[mid:], "client", -1)
-    to_right, to_left = control_to(1), control_to(3)
-    to_right = jnp.concatenate([to_right[:mid] + from_left.astype(F32), to_right[mid:]], axis=0).astype(BF16)
-    to_left = jnp.concatenate([to_left[:mid], to_left[mid:] + from_right.astype(F32)], axis=0).astype(BF16)
-    from_left, from_right = shift(to_right, "client", 1), shift(to_left, "client", -1)
-    control_sum = control_to(0) + from_left.astype(F32) + from_right.astype(F32)
+    control_sum = (share[c] * correction[0].astype(F32)).astype(BF16).reshape(units, nc, wide).transpose(1, 0, 2)
+    control_sum, _ = lax.optimization_barrier((control_sum.reshape(nc * units, wide), both))
+    control_sum = lax.psum_scatter(control_sum, "client", scatter_dimension=0, tiled=True)
 
     slots = jnp.arange(EXPERTS * cap, dtype=jnp.int32)
-    combine = jnp.zeros((tok, EXPERTS * cap), F32)
-    for k in range(top):
-        combine = combine + jnp.where(slot[:, k][:, None] == slots[None, :], gate_weights[0, :, k][:, None], 0.0)
+
+    def combine_of(slot_of, gates):
+        weight = jnp.zeros((tok, EXPERTS * cap), F32)
+        for k in range(top):
+            weight = weight + jnp.where(slot_of[:, k][:, None] == slots[None, :], gates[:, k][:, None], 0.0)
+        return weight
+
+    combine = combine_of(slot, gate_weights[0])
+    table = jnp.concatenate([slot.astype(F32), gate_weights[0]], axis=1).T
+    tables = hop(jnp.stack([table] * pair))
+    combines = [combine_of(tables[a, :top].T.astype(jnp.int32), tables[a, top:].T) for a in range(pair)]
     positions = m * tok + jnp.arange(tok, dtype=jnp.int32)
     live = (positions < counts[c]).astype(F32)[:, None]
     goal = jnp.concatenate(
         [at(target[0], ((q * pair + a) * nz + zl) * cols, cols, 1) for a in range(pair)], axis=1
     ).astype(F32)
 
-    def at_owner(x):
-        x = x.astype(BF16).reshape(nm, cap, pair * cols)
-        x = lax.all_to_all(x, "expert", 0, 0, tiled=True)
-        x = jnp.sum(x.astype(F32).reshape(EXPERTS, copies, cap, pair * cols), axis=1)
-        return dot(combine, x.reshape(EXPERTS * cap, pair * cols), 1, 0, precision=EXACT)
-
-    def at_expert(x):
-        x = dot(combine, x, 0, 0, precision=EXACT).astype(BF16).reshape(EXPERTS, cap, pair * cols)
-        x = jnp.repeat(x, copies, axis=0)
-        x = lax.all_to_all(x, "expert", 0, 0, tiled=True)
-        return x.reshape(rows, pair * cols)
-
-    residual = live * (at_owner(value) - goal)
-    cotangent = at_expert(residual)
-    change = dot(gram, cotangent, 1, 0) + control_move
-    mean = share[c] * (residual - (step_size / LOCAL_STEPS) * live * at_owner(change))
-    cotangent = at_expert(mean)
-
-    cotangent = hop(cotangent.reshape(rows, pair, cols).transpose(1, 0, 2)).reshape(pair * rows, cols)
+    def to_tokens(weight, x):
+        x = jnp.sum(x.astype(F32).reshape(EXPERTS, copies, cap, x.shape[-1]), axis=1)
+        return dot(weight, x.reshape(EXPERTS * cap, x.shape[-1]), 1, 0, precision=EXACT)
+
+    def to_rows(weight, x):
+        return dot(weight, x, 0, 0, precision=EXACT).astype(BF16).reshape(EXPERTS, cap, x.shape[-1])
+
+    def exchange(x):
+        return lax.all_to_all(x, "expert", 0, 0, tiled=True)
+
+    value = both[: pair * rows].reshape(pair, nm, cap, cols).transpose(1, 0, 2, 3)
+    value = exchange(value)
+    value = hop(jnp.stack([to_tokens(combines[a], value[:, a]) for a in range(pair)]).astype(BF16))
+    residual = live * (jnp.concatenate([value[a] for a in range(pair)], axis=1).astype(F32) - goal)
+    cotangent = exchange(jnp.repeat(to_rows(combine, residual), copies, axis=0))
+    cotangent = cotangent.reshape(rows, pair * cols)
+    change = dot(gram, cotangent, 1, 0) + control_move.astype(F32)
+    change = exchange(change.astype(BF16).reshape(nm, cap, pair * cols))
+    mean = share[c] * (residual - (step_size / LOCAL_STEPS) * live * to_tokens(combine, change))
+    mean = hop(jnp.stack([mean[:, a * cols : (a + 1) * cols] for a in range(pair)]).astype(BF16))
+    cotangent = jnp.stack([to_rows(combines[a], mean[a].astype(F32)) for a in range(pair)], axis=1)
+    cotangent = exchange(jnp.repeat(cotangent, copies, axis=0))
+    cotangent = cotangent.transpose(1, 0, 2, 3).reshape(pair * rows, cols)
+
     cotangent = jnp.broadcast_to(cotangent[None], (nz, pair * rows, cols))
     cotangent = lax.all_to_all(cotangent, "zlo", 0, 0, tiled=True)
     cotangent = cotangent.transpose(1, 0, 2).reshape(pair * rows, wide)
     other = shift(cotangent, "core", 1)
     cotangent = place([cotangent, other], lambda k: (q + k) % CORES, 0)
-    return dot(full, cotangent, 1, 0) + control_sum
+    return dot(full, cotangent, 1, 0) + control_sum.astype(F32)
 
 
 def solution(mesh):

time: 510 us -> 476 us (0.933)
  starting transfers between devices: 167 us -> 139 us
  waiting for transfers between devices: 226 us -> 210 us
  local copies, waits for them, and re-layouts: 28 us -> 39.7 us
  other arithmetic: 21.3 us -> 14.3 us
  matrix products: 25.2 us -> 30.5 us
    reduce_scatter x0 -> x2, waiting for transfers between devices: none -> 57.5 us  [the longest x1 57.5 us: local(): lax.psum_scatter(control_sum, 'client', scatter_dimension=0, tiled=True)]
    ppermute x23 -> x15, waiting for transfers between devices: 113 us -> 69.4 us  [shift(): return lax.ppermute(x, axis, [(i, (i + by) % n) for i in range(n)])]
    ppermute x23 -> x15, starting transfers between devices: 107 us -> 77.8 us  [shift(): return lax.ppermute(x, axis, [(i, (i + by) % n) for i in range(n)])]
    all_to_all x1, waiting for transfers between devices: 16.1 us -> 0.01 us  [over_zlo(): x = lax.all_to_all(x, 'zlo', 0, 0, tiled=True)]
    all_to_all x1, waiting for transfers between devices: 23.7 us -> 10.9 us  [local(): cotangent = lax.all_to_all(cotangent, 'zlo', 0, 0, tiled=True)]
    convert_element_type x0 -> x3, local copies, waits for them, and re-layouts: none -> 8.19 us  [the longest x2 8.13 us: local(): (share[c] * correction[0].astype(F32)).astype(BF16).reshape(units, nc, wide)]
    another operation x3 -> x4, local copies, waits for them, and re-layouts: 2.45 us -> 9.7 us  [the longest x2 9.68 us: local(): correction[0].reshape(units, CORES, pair, nz, cols).transpose(0, 3, 1, 2, 4)]
    dot_general x21 -> x27, matrix products: 25.2 us -> 30.5 us  [dot(): lax.dot_general(a, b, (((da,), (db,)), ((), ())), preferred_element_type=...]
  transfers between devices with their start and end apart: 33 -> 29, of which waited for: 15 -> 17; matrix products, arithmetic and copies ran while one was open for 9% -> 12% of each run, Pallas kernels for 0% -> 0%
where the time goes in v1:
time: 476 us; the launch traced here: 474 us
  waiting for transfers between devices  210 us (44%)
  starting transfers between devices  139 us (29%)
  local copies, waits for them, and re-layouts  39.7 us (8%)
  matrix products  30.5 us (6%)
  blocking collectives  25.1 us (5%)
  between operations  15.2 us (3%)
  other arithmetic  14.3 us (3%)
    ppermute x15, starting transfers between devices, shift(): return lax.ppermute(x, axis, [(i, (i + by) % n) for i in range(n)])  77.8 us
    ppermute x15, waiting for transfers between devices, shift(): return lax.ppermute(x, axis, [(i, (i + by) % n) for i in range(n)])  69.4 us
    reduce_scatter x1, waiting for transfers between devices, local(): lax.psum_scatter(control_sum, 'client', scatter_dimension=0, tiled=True)  57.5 us
    all_gather x1, waiting for transfers between devices, local(): lax.all_gather(features, ('client', 'zlo', 'core'), axis=0, tiled=True)  51.3 us
    ppermute x6, starting transfers between devices, hop(): arrived.append(lax.ppermute(item, ('client', 'core'), ends))  37 us
    dot_general x27, matrix products, dot(): lax.dot_general(a, b, (((da,), (db,)), ((), ())), preferred_element_type=...  30.5 us
    all_to_all x1, blocking collectives, local(): lax.all_to_all(sent, 'expert', 0, 0, tiled=True).reshape(nm * few, -1)  14.9 us
    all_to_all x3, starting transfers between devices, exchange(): return lax.all_to_all(x, 'expert', 0, 0, tiled=True)  13.5 us
  transfers between devices with their start and end apart: 29, of which 17 were waited for; matrix products, arithmetic and copies ran while one was open for 12% of the time, Pallas kernels for 0%

profile of v1, /device:TPU:1, one launch (start us, length us, event | category | flops | bytes accessed | tf_op | source)
XLA Modules:
  0.0 474.4 jit_solution(15945222131819975782)
XLA Ops:
  8.7 14.9 %all_to_all.35 = bf16[16,4,2048]{2,1,0:T(4,128)(2,1)S(1)} all-to-all(bf16[16,4,2048]{2,1,0:T(4,128)(2,1)S(1)} %bitcast.154), channel_id=1, replica_groups=mesh['client'=4,'expert'=16,'zlo'=4,'core'=2] {'expert'}, dimensions={0} | all-to-all | bytes 524288 | tf_op jit(solution)/shard_map/all_to_all | solution.py:108
  24.6 15.4 %collective-permute-start.1 = (bf16[224,512]{1,0:T(8,128)(2,1)S(1)}, bf16[224,512]{1,0:T(8,128)(2,1)S(1)}, u32[]{:S(2)}, u32[]{:S(2)}) collective-permute-start(bf16[224,512]{1,0:T(8,128)(2,1)S(1)} %pad_maximum_fusion.3), channel_id=1, source_target_pairs={{0,256},{128,384},{256,0},{384,128},{1,257},{129,385},{257,1},{385... | collective-permute-start | bytes 688136 | tf_op jit(solution)/shard_map/ppermute | solution.py:19
  40.1 4.0 collective-permute-start
  44.2 5.2 %collective-permute-start.2 = (bf16[224,512]{1,0:T(8,128)(2,1)S(1)}, bf16[224,512]{1,0:T(8,128)(2,1)S(1)}, u32[]{:S(2)}, u32[]{:S(2)}) collective-permute-start(bf16[224,512]{1,0:T(8,128)(2,1)S(1)} %pad_maximum_fusion.4), channel_id=1, source_target_pairs={{0,384},{128,0},{256,128},{384,256},{1,385},{129,1},{257,129},{385... | collective-permute-start | bytes 688136 | tf_op jit(solution)/shard_map/ppermute | solution.py:19
  50.7 28.6 %collective-permute-done = bf16[224,512]{1,0:T(8,128)(2,1)} collective-permute-done((bf16[224,512]{1,0:T(8,128)(2,1)S(1)}, bf16[224,512]{1,0:T(8,128)(2,1)}, u32[]{:S(2)}, u32[]{:S(2)}) %collective-permute-start) | collective-permute-done | bytes 229408 | tf_op jit(solution)/shard_map/ppermute | solution.py:19
  80.2 3.3 collective-permute-done.2
  83.6 51.3 %all-gather.2.cloned.1.call-done = bf16[2048,2048]{1,0:T(8,128)(2,1)} async-done(((bf16[64,2048]{1,0:T(8,128)(2,1)}), bf16[2048,2048]{1,0:T(8,128)(2,1)}) %all-gather.2.cloned.1.call-update) | async-done | bytes 8388624 | tf_op jit(solution)/shard_map/all_gather | solution.py:109
  134.8 6.0 %fusion.131 = f32[224,2048]{1,0:T(8,128)S(1)} fusion(bf16[224,2048]{1,0:T(8,128)(2,1)S(1)} %constant_dynamic-update-slice_fusion.16, bf16[2048,2048]{1,0:T(8,128)(2,1)} %all-gather.2.cloned.1.call-done), kind=kOutput, calls=%fused_computation.275 | convolution fusion | flops 1879048192 | bytes 11141120 | tf_op jit(solution)/shard_map/dot_general | solution.py:27
  142.6 4.9 %collective-permute-start.4 = (bf16[56,2048]{1,0:T(8,128)(2,1)S(1)}, bf16[56,2048]{1,0:T(8,128)(2,1)S(1)}, u32[]{:S(2)}, u32[]{:S(2)}) collective-permute-start(bf16[56,2048]{1,0:T(8,128)(2,1)S(1)} %get-tuple-element.13), channel_id=1, source_target_pairs={{0,128},{128,256},{256,384},{384,0},{1,129},{129,257},{257,385},{3... | collective-permute-start | bytes 688136 | tf_op jit(solution)/shard_map/ppermute | solution.py:19
  147.5 4.3 collective-permute-start.6
  151.8 4.9 %collective-permute-start.3 = (bf16[56,2048]{1,0:T(8,128)(2,1)S(1)}, bf16[56,2048]{1,0:T(8,128)(2,1)S(1)}, u32[]{:S(2)}, u32[]{:S(2)}) collective-permute-start(bf16[56,2048]{1,0:T(8,128)(2,1)S(1)} %get-tuple-element.15), channel_id=1, source_target_pairs={{0,128},{128,256},{256,384},{384,0},{1,129},{129,257},{257,385},{3... | collective-permute-start | bytes 688136 | tf_op jit(solution)/shard_map/ppermute | solution.py:19
  156.7 4.3 collective-permute-start.8
  161.0 18.9 %collective-permute-done.3 = bf16[56,2048]{1,0:T(8,128)(2,1)S(1)} collective-permute-done((bf16[56,2048]{1,0:T(8,128)(2,1)S(1)}, bf16[56,2048]{1,0:T(8,128)(2,1)S(1)}, u32[]{:S(2)}, u32[]{:S(2)}) %collective-permute-start.3) | collective-permute-done | bytes 229408 | tf_op jit(solution)/shard_map/ppermute | solution.py:19
  179.9 8.4 %collective-permute-start.5 = (bf16[56,2048]{1,0:T(8,128)(2,1)S(1)}, bf16[56,2048]{1,0:T(8,128)(2,1)S(1)}, u32[]{:S(2)}, u32[]{:S(2)}) collective-permute-start(bf16[56,2048]{1,0:T(8,128)(2,1)S(1)} %collective-permute-done.3), channel_id=1, source_target_pairs={{0,128},{128,256},{256,384},{384,0},{1,129},{129,257},{257,385},{3... | collective-permute-start | bytes 688136 | tf_op jit(solution)/shard_map/ppermute | solution.py:19
  188.3 1.9 collective-permute-start.7
  190.3 9.0 %collective-permute-done.5 = bf16[56,2048]{1,0:T(8,128)(2,1)S(1)} collective-permute-done((bf16[56,2048]{1,0:T(8,128)(2,1)S(1)}, bf16[56,2048]{1,0:T(8,128)(2,1)S(1)}, u32[]{:S(2)}, u32[]{:S(2)}) %collective-permute-start.5) | collective-permute-done | bytes 229408 | tf_op jit(solution)/shard_map/ppermute | solution.py:19
  199.3 5.9 %collective-permute-done.7 = bf16[56,2048]{1,0:T(8,128)(2,1)S(1)} collective-permute-done((bf16[56,2048]{1,0:T(8,128)(2,1)S(1)}, bf16[56,2048]{1,0:T(8,128)(2,1)S(1)}, u32[]{:S(2)}, u32[]{:S(2)}) %collective-permute-start.7) | collective-permute-done | bytes 229408 | tf_op jit(solution)/shard_map/ppermute | solution.py:19
  207.7 9.8 %collective-permute-start.11 = (bf16[1280,512]{1,0:T(8,128)(2,1)}, bf16[1280,512]{1,0:T(8,128)(2,1)}, u32[]{:S(2)}, u32[]{:S(2)}) collective-permute-start(bf16[1280,512]{1,0:T(8,128)(2,1)} %pad_maximum_fusion), channel_id=1, source_target_pairs={{0,1},{1,0},{2,3},{3,2},{4,5},{5,4},{6,7},{7,6},{8,9},{9,8},{10,11... | collective-permute-start | bytes 3932168 | tf_op jit(solution)/shard_map/ppermute | solution.py:19
  218.7 1.8 collective-permute-done.11
  220.4 2.7 bitcast_bitcast_fusion
  223.1 6.7 %all-to-all-start.1 = ((bf16[4,1280,128]{2,1,0:T(8,128)(2,1)}), bf16[4,1280,128]{2,1,0:T(8,128)(2,1)}, u32[]{:S(2)}, u32[]{:S(2)}) async-start(bf16[4,1280,128]{2,1,0:T(8,128)(2,1)} %bitcast_bitcast_fusion), calls=%async_computation.1 | async-start | bytes 2621440 | tf_op jit(solution)/shard_map/all_to_all | solution.py:135
  229.8 5.0 %reshape_squeeze.3 = bf16[448,2,2,4,128]{4,3,2,1,0:T(4,128)(2,1)} reshape(bf16[1,448,2048]{2,1,0:T(8,128)(2,1)} %param.17) | data formatting | bytes 3670016 | tf_op jit(solution)/shard_map/reshape;squeeze | solution.py:150
  234.8 4.7 copy.43
  239.4 5.3 %reshape.122 = bf16[448,2048]{1,0:T(8,128)(2,1)} reshape(bf16[448,4,2,2,128]{4,3,2,1,0:T(2,128)(2,1)} %bitcast.149) | data formatting | bytes 3670016 | tf_op jit(solution)/shard_map/reshape | solution.py:150
  244.7 2.1 fusion.10
  246.9 2.0 fusion.9
  255.4 8.2 %collective-permute-start.9 = (f32[4,128]{1,0:T(4,128)S(1)}, f32[4,128]{1,0:T(4,128)S(1)}, u32[]{:S(2)}, u32[]{:S(2)}) collective-permute-start(f32[4,128]{1,0:T(4,128)S(1)} %get-tuple-element.42), channel_id=1, source_target_pairs={{0,0},{1,256},{128,128},{129,384},{256,1},{257,257},{384,129},{385... | collective-permute-start | bytes 6152 | tf_op jit(solution)/shard_map/ppermute | solution.py:86
  263.6 4.9 %collective-permute-start.10 = (f32[4,128]{1,0:T(4,128)S(1)}, f32[4,128]{1,0:T(4,128)S(1)}, u32[]{:S(2)}, u32[]{:S(2)}) collective-permute-start(f32[4,128]{1,0:T(4,128)S(1)} %get-tuple-element.43), channel_id=1, source_target_pairs={{0,128},{1,384},{128,0},{129,256},{256,129},{257,385},{384,1},{385... | collective-permute-start | bytes 6152 | tf_op jit(solution)/shard_map/ppermute | solution.py:86
  269.2 1.2 compare_convert_fusion.3
  271.3 1.2 collective-permute-done.10
  272.6 1.7 reduce_sum.59
  275.0 3.5 all-to-all-start.2
  278.6 3.8 collective-permute-start.14
  282.5 4.0 collective-permute-start.15
  286.4 3.1 collective-permute-start.16
  289.6 2.0 collective-permute-done.15
  292.5 6.6 %collective-permute-start.12 = (bf16[128,128]{1,0:T(8,128)(2,1)S(1)}, bf16[128,128]{1,0:T(8,128)(2,1)S(1)}, u32[]{:S(2)}, u32[]{:S(2)}) collective-permute-start(bf16[128,128]{1,0:T(8,128)(2,1)S(1)} %get-tuple-element.35), channel_id=1, source_target_pairs={{0,0},{1,256},{128,128},{129,384},{256,1},{257,257},{384,129},{385... | collective-permute-start | bytes 98312 | tf_op jit(solution)/shard_map/ppermute | solution.py:86
  299.0 5.5 %collective-permute-start.13 = (bf16[128,128]{1,0:T(8,128)(2,1)S(1)}, bf16[128,128]{1,0:T(8,128)(2,1)S(1)}, u32[]{:S(2)}, u32[]{:S(2)}) collective-permute-start(bf16[128,128]{1,0:T(8,128)(2,1)S(1)} %get-tuple-element.34), channel_id=1, source_target_pairs={{0,128},{1,384},{128,0},{129,256},{256,129},{257,385},{384,1},{385... | collective-permute-start | bytes 98312 | tf_op jit(solution)/shard_map/ppermute | solution.py:86
  304.6 1.9 collective-permute-start.17
  306.5 1.6 collective-permute-done.13
  308.2 1.2 convolution_convert_fusion.11
  310.2 6.4 %all-to-all-start.3 = ((bf16[16,32,256]{2,1,0:T(8,128)(2,1)}), bf16[16,32,256]{2,1,0:T(8,128)(2,1)S(1)}, u32[]{:S(2)}, u32[]{:S(2)}) async-start(bf16[16,32,256]{2,1,0:T(8,128)(2,1)} %bitcast.52), calls=%async_computation.3 | async-start | bytes 524288 | tf_op jit(solution)/shard_map/all_to_all | solution.py:193
  319.1 6.7 %all-to-all-done.3 = bf16[16,32,256]{2,1,0:T(8,128)(2,1)S(1)} async-done(((bf16[16,32,256]{2,1,0:T(8,128)(2,1)}), bf16[16,32,256]{2,1,0:T(8,128)(2,1)S(1)}, u32[]{:S(2)}, u32[]{:S(2)}) %all-to-all-start.3) | async-done | bytes 262176 | tf_op jit(solution)/shard_map/all_to_all | solution.py:193
  325.8 2.0 fusion.2
  327.8 3.5 all-to-all-start.4
  333.2 6.4 %all-to-all-done.4 = bf16[16,32,256]{2,1,0:T(8,128)(2,1)S(1)} async-done(((bf16[16,32,256]{2,1,0:T(8,128)(2,1)}), bf16[16,32,256]{2,1,0:T(8,128)(2,1)S(1)}, u32[]{:S(2)}, u32[]{:S(2)}) %all-to-all-start.4) | async-done | bytes 262176 | tf_op jit(solution)/shard_map/all_to_all | solution.py:193
  339.7 1.7 fusion.13
  341.5 7.9 %collective-permute-start.18 = (bf16[128,128]{1,0:T(8,128)(2,1)S(1)}, bf16[128,128]{1,0:T(8,128)(2,1)S(1)}, u32[]{:S(2)}, u32[]{:S(2)}) collective-permute-start(bf16[128,128]{1,0:T(8,128)(2,1)S(1)} %get-tuple-element.29), channel_id=1, source_target_pairs={{0,0},{1,256},{128,128},{129,384},{256,1},{257,257},{384,129},{385... | collective-permute-start | bytes 98312 | tf_op jit(solution)/shard_map/ppermute | solution.py:86
  349.4 3.8 collective-permute-start.19
  353.3 2.2 collective-permute-done.18
  355.4 3.1 collective-permute-done.19
  359.5 10.2 %all_to_all.36 = bf16[16,2,32,128]{3,2,1,0:T(8,128)(2,1)S(1)} all-to-all(bf16[16,2,32,128]{3,2,1,0:T(8,128)(2,1)S(1)} %bitcast.155), channel_id=1, replica_groups=mesh['client'=4,'expert'=16,'zlo'=4,'core'=2] {'expert'}, dimensions={0} | all-to-all | bytes 524288 | tf_op jit(solution)/shard_map/all_to_all | solution.py:193
  369.7 1.2 broadcast_in_dim.117
  370.9 4.3 all-to-all-start.6
  375.2 3.9 multiply_convert_fusion
  379.2 5.0 %convert_element_type.215 = bf16[448,4,512]{2,1,0:T(4,128)(2,1)} reshape(bf16[1,448,2048]{2,1,0:T(8,128)(2,1)} %multiply_convert_fusion) | data formatting | bytes 3670016 | tf_op jit(solution)/shard_map/convert_element_type | solution.py:163
  384.2 3.1 copy.39
  387.3 10.9 %all-to-all-done.6 = bf16[4,1024,128]{2,1,0:T(8,128)(2,1)} async-done(((bf16[4,1024,128]{2,1,0:T(8,128)(2,1)}), bf16[4,1024,128]{2,1,0:T(8,128)(2,1)}, u32[]{:S(2)}, u32[]{:S(2)}) %all-to-all-start.6) | async-done | bytes 1048608 | tf_op jit(solution)/shard_map/all_to_all | solution.py:210
  398.2 1.5 copy.38
  399.7 1.9 collective-permute-start.20
  401.6 1.6 broadcast_in_dim.98
  404.4 2.3 constant_dynamic-update-slice_fusion
  406.7 57.5 %reduce-scatter.5.cloned.1.call-done = bf16[448,512]{1,0:T(8,128)(2,1)} async-done(((bf16[1792,512]{1,0:T(8,128)(2,1)}), bf16[448,512]{1,0:T(8,128)(2,1)}) %reduce-scatter.5.cloned.1.call-update) | async-done | bytes 458768 | tf_op jit(solution)/shard_map/reduce_scatter | solution.py:165
  464.1 3.7 convolution_add_fusion
  (166 shorter events, 26.8 us)
Async XLA Ops:
  6.5 1.8 copy-start
  6.5 18.0 %copy-start.3 = (bf16[448,512]{1,0:T(8,128)(2,1)S(1)}, bf16[448,512]{1,0:T(8,128)(2,1)}, u32[]{:S(2)}) copy-start(bf16[448,512]{1,0:T(8,128)(2,1)} %param.14) | copy-start | bytes 1376260
  6.5 18.0 %copy-start.2 = (bf16[448,512]{1,0:T(8,128)(2,1)S(1)}, bf16[448,512]{1,0:T(8,128)(2,1)}, u32[]{:S(2)}) copy-start(bf16[448,512]{1,0:T(8,128)(2,1)} %param.15) | copy-start | bytes 1376260
  6.5 128.3 %all-gather.2.cloned.1.call-start = ((), (), s32[]{:S(2)}) async-start(), calls=%async_computation.9 | async-start | bytes 8650752 | tf_op jit(solution)/shard_map/all_gather | solution.py:109
  24.6 55.6 %collective-permute-start.1 = (bf16[224,512]{1,0:T(8,128)(2,1)S(1)}, bf16[224,512]{1,0:T(8,128)(2,1)S(1)}, u32[]{:S(2)}, u32[]{:S(2)}) collective-permute-start(bf16[224,512]{1,0:T(8,128)(2,1)S(1)} %pad_maximum_fusion.3), channel_id=1, source_target_pairs={{0,256},{128,384},{256,0},{384,128},{1,257},{129,385},{257,1},{385... | collective-permute-start | bytes 688136 | tf_op jit(solution)/shard_map/ppermute | solution.py:19
  40.1 39.1 %collective-permute-start = (bf16[224,512]{1,0:T(8,128)(2,1)S(1)}, bf16[224,512]{1,0:T(8,128)(2,1)}, u32[]{:S(2)}, u32[]{:S(2)}) collective-permute-start(bf16[224,512]{1,0:T(8,128)(2,1)S(1)} %pad_maximum_fusion.2), channel_id=1, source_target_pairs={{0,128},{128,256},{256,384},{384,0},{1,129},{129,257},{257,385},{3... | collective-permute-start | bytes 688136 | tf_op jit(solution)/shard_map/ppermute | solution.py:19
  44.2 39.4 %collective-permute-start.2 = (bf16[224,512]{1,0:T(8,128)(2,1)S(1)}, bf16[224,512]{1,0:T(8,128)(2,1)S(1)}, u32[]{:S(2)}, u32[]{:S(2)}) collective-permute-start(bf16[224,512]{1,0:T(8,128)(2,1)S(1)} %pad_maximum_fusion.4), channel_id=1, source_target_pairs={{0,384},{128,0},{256,128},{384,256},{1,385},{129,1},{257,129},{385... | collective-permute-start | bytes 688136 | tf_op jit(solution)/shard_map/ppermute | solution.py:19
  142.6 47.7 %collective-permute-start.4 = (bf16[56,2048]{1,0:T(8,128)(2,1)S(1)}, bf16[56,2048]{1,0:T(8,128)(2,1)S(1)}, u32[]{:S(2)}, u32[]{:S(2)}) collective-permute-start(bf16[56,2048]{1,0:T(8,128)(2,1)S(1)} %get-tuple-element.13), channel_id=1, source_target_pairs={{0,128},{128,256},{256,384},{384,0},{1,129},{129,257},{257,385},{3... | collective-permute-start | bytes 688136 | tf_op jit(solution)/shard_map/ppermute | solution.py:19
  147.5 40.8 %collective-permute-start.6 = (bf16[56,2048]{1,0:T(8,128)(2,1)S(1)}, bf16[56,2048]{1,0:T(8,128)(2,1)S(1)}, u32[]{:S(2)}, u32[]{:S(2)}) collective-permute-start(bf16[56,2048]{1,0:T(8,128)(2,1)S(1)} %get-tuple-element.13), channel_id=1, source_target_pairs={{0,384},{128,0},{256,128},{384,256},{1,385},{129,1},{257,129},{385... | collective-permute-start | bytes 688136 | tf_op jit(solution)/shard_map/ppermute | solution.py:19
  151.8 28.1 %collective-permute-start.3 = (bf16[56,2048]{1,0:T(8,128)(2,1)S(1)}, bf16[56,2048]{1,0:T(8,128)(2,1)S(1)}, u32[]{:S(2)}, u32[]{:S(2)}) collective-permute-start(bf16[56,2048]{1,0:T(8,128)(2,1)S(1)} %get-tuple-element.15), channel_id=1, source_target_pairs={{0,128},{128,256},{256,384},{384,0},{1,129},{129,257},{257,385},{3... | collective-permute-start | bytes 688136 | tf_op jit(solution)/shard_map/ppermute | solution.py:19
  156.7 48.5 %collective-permute-start.8 = (bf16[56,2048]{1,0:T(8,128)(2,1)S(1)}, bf16[56,2048]{1,0:T(8,128)(2,1)S(1)}, u32[]{:S(2)}, u32[]{:S(2)}) collective-permute-start(bf16[56,2048]{1,0:T(8,128)(2,1)S(1)} %get-tuple-element.15), channel_id=1, source_target_pairs={{0,384},{128,0},{256,128},{384,256},{1,385},{129,1},{257,129},{385... | collective-permute-start | bytes 688136 | tf_op jit(solution)/shard_map/ppermute | solution.py:19
  161.0 44.7 %copy-start.4 = (bf16[448,512]{1,0:T(8,128)(2,1)S(1)}, bf16[448,512]{1,0:T(8,128)(2,1)}, u32[]{:S(2)}) copy-start(bf16[448,512]{1,0:T(8,128)(2,1)} %param.16) | copy-start | bytes 1376260
  179.9 19.4 %collective-permute-start.5 = (bf16[56,2048]{1,0:T(8,128)(2,1)S(1)}, bf16[56,2048]{1,0:T(8,128)(2,1)S(1)}, u32[]{:S(2)}, u32[]{:S(2)}) collective-permute-start(bf16[56,2048]{1,0:T(8,128)(2,1)S(1)} %collective-permute-done.3), channel_id=1, source_target_pairs={{0,128},{128,256},{256,384},{384,0},{1,129},{129,257},{257,385},{3... | collective-permute-start | bytes 688136 | tf_op jit(solution)/shard_map/ppermute | solution.py:19
  188.3 16.9 %collective-permute-start.7 = (bf16[56,2048]{1,0:T(8,128)(2,1)S(1)}, bf16[56,2048]{1,0:T(8,128)(2,1)S(1)}, u32[]{:S(2)}, u32[]{:S(2)}) collective-permute-start(bf16[56,2048]{1,0:T(8,128)(2,1)S(1)} %collective-permute-done.6), channel_id=1, source_target_pairs={{0,384},{128,0},{256,128},{384,256},{1,385},{129,1},{257,129},{385... | collective-permute-start | bytes 688136 | tf_op jit(solution)/shard_map/ppermute | solution.py:19
  207.7 12.8 %collective-permute-start.11 = (bf16[1280,512]{1,0:T(8,128)(2,1)}, bf16[1280,512]{1,0:T(8,128)(2,1)}, u32[]{:S(2)}, u32[]{:S(2)}) collective-permute-start(bf16[1280,512]{1,0:T(8,128)(2,1)} %pad_maximum_fusion), channel_id=1, source_target_pairs={{0,1},{1,0},{2,3},{3,2},{4,5},{5,4},{6,7},{7,6},{8,9},{9,8},{10,11... | collective-permute-start | bytes 3932168 | tf_op jit(solution)/shard_map/ppermute | solution.py:19
  223.1 49.5 %all-to-all-start.1 = ((bf16[4,1280,128]{2,1,0:T(8,128)(2,1)}), bf16[4,1280,128]{2,1,0:T(8,128)(2,1)}, u32[]{:S(2)}, u32[]{:S(2)}) async-start(bf16[4,1280,128]{2,1,0:T(8,128)(2,1)} %bitcast_bitcast_fusion), calls=%async_computation.1 | async-start | bytes 2621440 | tf_op jit(solution)/shard_map/all_to_all | solution.py:135
  229.8 89.3 %reduce-scatter.3.cloned.1.call-start = ((), (), s32[]{:S(2)}) async-start(), calls=%async_computation.10 | async-start | bytes 2359296 | tf_op jit(solution)/shard_map/reduce_scatter | solution.py:154
  244.7 4.1 copy-start.1
  254.2 1.2 copy-start.5
  254.2 14.5 %copy-start.22 = (s32[4]{0:T(128)S(1)}, s32[4]{0:T(128)}, u32[]{:S(2)}) copy-start(s32[4]{0:T(128)} %param.13) | copy-start | bytes 52
  255.4 15.8 %collective-permute-start.9 = (f32[4,128]{1,0:T(4,128)S(1)}, f32[4,128]{1,0:T(4,128)S(1)}, u32[]{:S(2)}, u32[]{:S(2)}) collective-permute-start(f32[4,128]{1,0:T(4,128)S(1)} %get-tuple-element.42), channel_id=1, source_target_pairs={{0,0},{1,256},{128,128},{129,384},{256,1},{257,257},{384,129},{385... | collective-permute-start | bytes 6152 | tf_op jit(solution)/shard_map/ppermute | solution.py:86
  263.6 8.8 %collective-permute-start.10 = (f32[4,128]{1,0:T(4,128)S(1)}, f32[4,128]{1,0:T(4,128)S(1)}, u32[]{:S(2)}, u32[]{:S(2)}) collective-permute-start(f32[4,128]{1,0:T(4,128)S(1)} %get-tuple-element.43), channel_id=1, source_target_pairs={{0,128},{1,384},{128,0},{129,256},{256,129},{257,385},{384,1},{385... | collective-permute-start | bytes 6152 | tf_op jit(solution)/shard_map/ppermute | solution.py:86
  272.5 19.2 %copy-start.6 = (s32[128]{0:T(128)}, s32[128]{0:T(128)S(1)}, u32[]{:S(2)}) copy-start(s32[128]{0:T(128)S(1)} %get-tuple-element.50) | copy-start | bytes 1540
  272.5 19.2 %copy-start.8 = (s32[128]{0:T(128)}, s32[128]{0:T(128)S(1)}, u32[]{:S(2)}) copy-start(s32[128]{0:T(128)S(1)} %get-tuple-element.51) | copy-start | bytes 1540
  272.5 19.2 %copy-start.10 = (f32[128]{0:T(128)}, f32[128]{0:T(128)S(1)}, u32[]{:S(2)}) copy-start(f32[128]{0:T(128)S(1)} %get-tuple-element.52) | copy-start | bytes 1540
  272.5 19.2 %copy-start.12 = (f32[128]{0:T(128)}, f32[128]{0:T(128)S(1)}, u32[]{:S(2)}) copy-start(f32[128]{0:T(128)S(1)} %get-tuple-element.53) | copy-start | bytes 1540
  272.6 19.5 %copy-start.14 = (s32[128]{0:T(128)}, s32[128]{0:T(128)S(1)}, u32[]{:S(2)}) copy-start(s32[128]{0:T(128)S(1)} %get-tuple-element.44) | copy-start | bytes 1540
  272.6 19.5 %copy-start.16 = (s32[128]{0:T(128)}, s32[128]{0:T(128)S(1)}, u32[]{:S(2)}) copy-start(s32[128]{0:T(128)S(1)} %get-tuple-element.45) | copy-start | bytes 1540
  275.0 16.6 %all-to-all-start.2 = ((bf16[16,2,32,128]{3,2,1,0:T(8,128)(2,1)}), bf16[16,2,32,128]{3,2,1,0:T(8,128)(2,1)S(1)}, u32[]{:S(2)}, u32[]{:S(2)}) async-start(bf16[16,2,32,128]{3,2,1,0:T(8,128)(2,1)} %copy.34), calls=%async_computation.2 | async-start | bytes 524288 | tf_op jit(solution)/shard_map/all_to_all | solution.py:193
  278.6 10.9 %collective-permute-start.14 = (bf16[256,128]{1,0:T(8,128)(2,1)S(1)}, bf16[256,128]{1,0:T(8,128)(2,1)S(1)}, u32[]{:S(2)}, u32[]{:S(2)}) collective-permute-start(bf16[256,128]{1,0:T(8,128)(2,1)S(1)} %get-tuple-element.24), channel_id=1, source_target_pairs={{0,2},{2,4},{4,6},{6,0},{1,3},{3,5},{5,7},{7,1},{8,10},{10,12},{12... | collective-permute-start | bytes 196616 | tf_op jit(solution)/shard_map/ppermute | solution.py:19
  282.4 25.7 %copy-start.18 = (f32[128]{0:T(128)}, f32[128]{0:T(128)S(1)}, u32[]{:S(2)}) copy-start(f32[128]{0:T(128)S(1)} %get-tuple-element.46) | copy-start | bytes 1540
  282.4 25.7 %copy-start.20 = (f32[128]{0:T(128)}, f32[128]{0:T(128)S(1)}, u32[]{:S(2)}) copy-start(f32[128]{0:T(128)S(1)} %get-tuple-element.47) | copy-start | bytes 1540
  282.5 9.1 %collective-permute-start.15 = (bf16[256,128]{1,0:T(8,128)(2,1)S(1)}, bf16[256,128]{1,0:T(8,128)(2,1)S(1)}, u32[]{:S(2)}, u32[]{:S(2)}) collective-permute-start(bf16[256,128]{1,0:T(8,128)(2,1)S(1)} %get-tuple-element.24), channel_id=1, source_target_pairs={{0,4},{2,6},{4,0},{6,2},{1,5},{3,7},{5,1},{7,3},{8,12},{10,14},{12... | collective-permute-start | bytes 196616 | tf_op jit(solution)/shard_map/ppermute | solution.py:19
  286.4 18.1 %collective-permute-start.16 = (bf16[256,128]{1,0:T(8,128)(2,1)S(1)}, bf16[256,128]{1,0:T(8,128)(2,1)S(1)}, u32[]{:S(2)}, u32[]{:S(2)}) collective-permute-start(bf16[256,128]{1,0:T(8,128)(2,1)S(1)} %get-tuple-element.24), channel_id=1, source_target_pairs={{0,6},{2,0},{4,2},{6,4},{1,7},{3,1},{5,3},{7,5},{8,14},{10,8},{12,... | collective-permute-start | bytes 196616 | tf_op jit(solution)/shard_map/ppermute | solution.py:19
  291.6 25.0 %copy-start.23 = (s32[4]{0:T(128)S(1)}, s32[4]{0:T(128)}, u32[]{:S(2)}) copy-start(s32[4]{0:T(128)} %param.13) | copy-start | bytes 52
  292.5 14.1 %collective-permute-start.12 = (bf16[128,128]{1,0:T(8,128)(2,1)S(1)}, bf16[128,128]{1,0:T(8,128)(2,1)S(1)}, u32[]{:S(2)}, u32[]{:S(2)}) collective-permute-start(bf16[128,128]{1,0:T(8,128)(2,1)S(1)} %get-tuple-element.35), channel_id=1, source_target_pairs={{0,0},{1,256},{128,128},{129,384},{256,1},{257,257},{384,129},{385... | collective-permute-start | bytes 98312 | tf_op jit(solution)/shard_map/ppermute | solution.py:86
  299.0 9.1 %collective-permute-start.13 = (bf16[128,128]{1,0:T(8,128)(2,1)S(1)}, bf16[128,128]{1,0:T(8,128)(2,1)S(1)}, u32[]{:S(2)}, u32[]{:S(2)}) collective-permute-start(bf16[128,128]{1,0:T(8,128)(2,1)S(1)} %get-tuple-element.34), channel_id=1, source_target_pairs={{0,128},{1,384},{128,0},{129,256},{256,129},{257,385},{384,1},{385... | collective-permute-start | bytes 98312 | tf_op jit(solution)/shard_map/ppermute | solution.py:86
  304.6 13.4 %collective-permute-start.17 = (bf16[256,512]{1,0:T(8,128)(2,1)S(1)}, bf16[256,512]{1,0:T(8,128)(2,1)}, u32[]{:S(2)}, u32[]{:S(2)}) collective-permute-start(bf16[256,512]{1,0:T(8,128)(2,1)S(1)} %constant_dynamic-update-slice_fusion.4), channel_id=1, source_target_pairs={{0,1},{1,0},{2,3},{3,2},{4,5},{5,4},{6,7},{7,6},{8,9},{9,8},{10,11... | collective-permute-start | bytes 786440 | tf_op jit(solution)/shard_map/ppermute | solution.py:19
  310.2 15.6 %all-to-all-start.3 = ((bf16[16,32,256]{2,1,0:T(8,128)(2,1)}), bf16[16,32,256]{2,1,0:T(8,128)(2,1)S(1)}, u32[]{:S(2)}, u32[]{:S(2)}) async-start(bf16[16,32,256]{2,1,0:T(8,128)(2,1)} %bitcast.52), calls=%async_computation.3 | async-start | bytes 524288 | tf_op jit(solution)/shard_map/all_to_all | solution.py:193
  318.0 40.5 %copy-start.15 = (s32[128]{0:T(128)S(1)}, s32[128]{0:T(128)}, u32[]{:S(2)}) copy-start(s32[128]{0:T(128)} %copy-done.14) | copy-start | bytes 1540
  318.0 40.5 %copy-start.17 = (s32[128]{0:T(128)S(1)}, s32[128]{0:T(128)}, u32[]{:S(2)}) copy-start(s32[128]{0:T(128)} %copy-done.16) | copy-start | bytes 1540
  318.0 40.5 %copy-start.19 = (f32[128]{0:T(128)S(1)}, f32[128]{0:T(128)}, u32[]{:S(2)}) copy-start(f32[128]{0:T(128)} %copy-done.18) | copy-start | bytes 1540
  318.0 40.5 %copy-start.21 = (f32[128]{0:T(128)S(1)}, f32[128]{0:T(128)}, u32[]{:S(2)}) copy-start(f32[128]{0:T(128)} %copy-done.20) | copy-start | bytes 1540
  325.8 33.2 %copy-start.7 = (s32[128]{0:T(128)S(1)}, s32[128]{0:T(128)}, u32[]{:S(2)}) copy-start(s32[128]{0:T(128)} %copy-done.6) | copy-start | bytes 1540
  325.8 33.2 %copy-start.9 = (s32[128]{0:T(128)S(1)}, s32[128]{0:T(128)}, u32[]{:S(2)}) copy-start(s32[128]{0:T(128)} %copy-done.8) | copy-start | bytes 1540
  325.8 33.2 %copy-start.11 = (f32[128]{0:T(128)S(1)}, f32[128]{0:T(128)}, u32[]{:S(2)}) copy-start(f32[128]{0:T(128)} %copy-done.10) | copy-start | bytes 1540
  325.8 33.2 %copy-start.13 = (f32[128]{0:T(128)S(1)}, f32[128]{0:T(128)}, u32[]{:S(2)}) copy-start(f32[128]{0:T(128)} %copy-done.12) | copy-start | bytes 1540
  327.8 11.9 %all-to-all-start.4 = ((bf16[16,32,256]{2,1,0:T(8,128)(2,1)}), bf16[16,32,256]{2,1,0:T(8,128)(2,1)S(1)}, u32[]{:S(2)}, u32[]{:S(2)}) async-start(bf16[16,32,256]{2,1,0:T(8,128)(2,1)} %bitcast.55), calls=%async_computation.5 | async-start | bytes 524288 | tf_op jit(solution)/shard_map/all_to_all | solution.py:193
  341.5 13.9 %collective-permute-start.18 = (bf16[128,128]{1,0:T(8,128)(2,1)S(1)}, bf16[128,128]{1,0:T(8,128)(2,1)S(1)}, u32[]{:S(2)}, u32[]{:S(2)}) collective-permute-start(bf16[128,128]{1,0:T(8,128)(2,1)S(1)} %get-tuple-element.29), channel_id=1, source_target_pairs={{0,0},{1,256},{128,128},{129,384},{256,1},{257,257},{384,129},{385... | collective-permute-start | bytes 98312 | tf_op jit(solution)/shard_map/ppermute | solution.py:86
  349.4 9.1 %collective-permute-start.19 = (bf16[128,128]{1,0:T(8,128)(2,1)S(1)}, bf16[128,128]{1,0:T(8,128)(2,1)S(1)}, u32[]{:S(2)}, u32[]{:S(2)}) collective-permute-start(bf16[128,128]{1,0:T(8,128)(2,1)S(1)} %get-tuple-element.28), channel_id=1, source_target_pairs={{0,128},{1,384},{128,0},{129,256},{256,129},{257,385},{384,1},{385... | collective-permute-start | bytes 98312 | tf_op jit(solution)/shard_map/ppermute | solution.py:86
  370.9 27.3 %all-to-all-start.6 = ((bf16[4,1024,128]{2,1,0:T(8,128)(2,1)}), bf16[4,1024,128]{2,1,0:T(8,128)(2,1)}, u32[]{:S(2)}, u32[]{:S(2)}) async-start(bf16[4,1024,128]{2,1,0:T(8,128)(2,1)} %broadcast_in_dim.117), calls=%async_computation.7 | async-start | bytes 2097152 | tf_op jit(solution)/shard_map/all_to_all | solution.py:210
  375.2 89.0 %reduce-scatter.5.cloned.1.call-start = ((), (), s32[]{:S(2)}) async-start(), calls=%async_computation.11 | async-start | bytes 2293760 | tf_op jit(solution)/shard_map/reduce_scatter | solution.py:165
  399.7 4.7 collective-permute-start.20
Sparse Core Ops, SparseCore 0:
  24.6 110.2 all-gather.1
  255.4 38.8 reduce-scatter.2
  387.4 76.6 reduce-scatter.4

commit v2 on v1

--- a/solution.py
+++ b/solution.py
@@ -108,6 +108,39 @@
     features = lax.all_to_all(sent, "expert", 0, 0, tiled=True).reshape(nm * few, -1)
     features = lax.all_gather(features, ("client", "zlo", "core"), axis=0, tiled=True)
 
+    slots = jnp.arange(EXPERTS * cap, dtype=jnp.int32)
+
+    def combine_of(slot_of, gates):
+        weight = jnp.zeros((tok, EXPERTS * cap), F32)
+        for k in range(top):
+            weight = weight + jnp.where(slot_of[:, k][:, None] == slots[None, :], gates[:, k][:, None], 0.0)
+        return weight
+
+    combine = combine_of(slot, gate_weights[0])
+    table = jnp.concatenate([slot.astype(F32), gate_weights[0]], axis=1).T
+    tables = hop(jnp.stack([table] * pair))
+    combines = [combine_of(tables[a, :top].T.astype(jnp.int32), tables[a, top:].T) for a in range(pair)]
+    positions = m * tok + jnp.arange(tok, dtype=jnp.int32)
+    live = (positions < counts[c]).astype(F32)[:, None]
+    goal = jnp.concatenate(
+        [at(target[0], ((q * pair + a) * nz + zl) * cols, cols, 1) for a in range(pair)], axis=1
+    ).astype(F32)
+
+    share = counts.astype(F32) / jnp.sum(counts).astype(F32)
+    pieces = [
+        correction[0][:, ((r * pair + e) * nz + z) * cols : ((r * pair + e) * nz + z + 1) * cols]
+        for z in range(nz)
+        for r in range(CORES)
+        for e in range(pair)
+    ]
+    control = jnp.concatenate(pieces, axis=1)
+    control_sum = jnp.concatenate([correction[0][:, k * wide : (k + 1) * wide] for k in range(nc)], axis=0)
+    control_sum = (share[c] * control_sum.astype(F32)).astype(BF16)
+
+    features, control, control_sum, combine, combines, goal = lax.optimization_barrier(
+        (features, control, control_sum, combine, combines, goal)
+    )
+
     pre = dot(weights, features, 1, 1)
     hidden = (jax.nn.silu(pre[:quarter]) * pre[quarter:]).astype(BF16)
     old = lax.broadcasted_iota(jnp.int32, (rows, rows), 0)
@@ -147,10 +180,8 @@
     got = shift(give, "core", 1)
     both = over_zlo(products(q) + got.astype(F32)).astype(BF16)
 
-    control = correction[0].reshape(units, CORES, pair, nz, cols).transpose(0, 3, 1, 2, 4).reshape(units, wide * nc)
-    control_move = jnp.concatenate(
-        [dot(own, control[:, k * pair * cols : (k + 1) * pair * cols], 0, 0).astype(BF16) for k in range(ns)], axis=0
-    )
+    control_move = dot(own, control, 0, 0).astype(BF16).reshape(rows, ns, pair * cols)
+    control_move = control_move.transpose(1, 0, 2).reshape(ns * rows, pair * cols)
     control_move = lax.psum_scatter(control_move, ("zlo", "core"), scatter_dimension=0, tiled=True)
 
     gram = both[pair * rows :]
@@ -159,28 +190,8 @@
     other = shift(gram, "core", 1)
     gram = place([gram, other], lambda k: (q + k) % CORES, 0)
 
-    share = counts.astype(F32) / jnp.sum(counts).astype(F32)
-    control_sum = (share[c] * correction[0].astype(F32)).astype(BF16).reshape(units, nc, wide).transpose(1, 0, 2)
-    control_sum, _ = lax.optimization_barrier((control_sum.reshape(nc * units, wide), both))
+    control_sum, _ = lax.optimization_barrier((control_sum, both))
     control_sum = lax.psum_scatter(control_sum, "client", scatter_dimension=0, tiled=True)
-
-    slots = jnp.arange(EXPERTS * cap, dtype=jnp.int32)
-
-    def combine_of(slot_of, gates):
-        weight = jnp.zeros((tok, EXPERTS * cap), F32)
-        for k in range(top):
-            weight = weight + jnp.where(slot_of[:, k][:, None] == slots[None, :], gates[:, k][:, None], 0.0)
-        return weight
-
-    combine = combine_of(slot, gate_weights[0])
-    table = jnp.concatenate([slot.astype(F32), gate_weights[0]], axis=1).T
-    tables = hop(jnp.stack([table] * pair))
-    combines = [combine_of(tables[a, :top].T.astype(jnp.int32), tables[a, top:].T) for a in range(pair)]
-    positions = m * tok + jnp.arange(tok, dtype=jnp.int32)
-    live = (positions < counts[c]).astype(F32)[:, None]
-    goal = jnp.concatenate(
-        [at(target[0], ((q * pair + a) * nz + zl) * cols, cols, 1) for a in range(pair)], axis=1
-    ).astype(F32)
 
     def to_tokens(weight, x):
         x = jnp.sum(x.astype(F32).reshape(EXPERTS, copies, cap, x.shape[-1]), axis=1)

time: 476 us -> 477 us (level)
  the two profiles are of different devices: /device:TPU:1 before, /device:TPU:33 now
where the time goes in v2:
time: 477 us; the launch traced here: 475 us
  waiting for transfers between devices  219 us (46%)
  starting transfers between devices  145 us (30%)
  local copies, waits for them, and re-layouts  36.2 us (8%)
  blocking collectives  24.3 us (5%)
  matrix products  21.9 us (5%)
  between operations  15.1 us (3%)
  other arithmetic  13.1 us (3%)
    all_to_all x1, waiting for transfers between devices, local(): cotangent = lax.all_to_all(cotangent, 'zlo', 0, 0, tiled=True)  60 us
    ppermute x15, starting transfers between devices, shift(): return lax.ppermute(x, axis, [(i, (i + by) % n) for i in range(n)])  59.1 us
    all_gather x1, waiting for transfers between devices, local(): lax.all_gather(features, ('client', 'zlo', 'core'), axis=0, tiled=True)  47.8 us
    ppermute x6, starting transfers between devices, hop(): arrived.append(lax.ppermute(item, ('client', 'core'), ends))  42.6 us
    ppermute x15, waiting for transfers between devices, shift(): return lax.ppermute(x, axis, [(i, (i + by) % n) for i in range(n)])  41.8 us
    all_to_all x1, waiting for transfers between devices, over_zlo(): x = lax.all_to_all(x, 'zlo', 0, 0, tiled=True)  32 us
    all_to_all x1, starting transfers between devices, over_zlo(): x = lax.all_to_all(x, 'zlo', 0, 0, tiled=True)  23.5 us
    dot_general x20, matrix products, dot(): lax.dot_general(a, b, (((da,), (db,)), ((), ())), preferred_element_type=...  21.9 us
  transfers between devices with their start and end apart: 29, of which 15 were waited for; matrix products, arithmetic and copies ran while one was open for 10% of the time, Pallas kernels for 0%

profile of v2, /device:TPU:33, one launch (start us, length us, event | category | flops | bytes accessed | tf_op | source)
XLA Modules:
  0.0 475.0 jit_solution(18325423874475927902)
XLA Ops:
  6.6 0.9 copy.27
  8.8 14.1 %all_to_all.35 = bf16[16,4,2048]{2,1,0:T(4,128)(2,1)S(1)} all-to-all(bf16[16,4,2048]{2,1,0:T(4,128)(2,1)S(1)} %bitcast.181), channel_id=1, replica_groups=mesh['client'=4,'expert'=16,'zlo'=4,'core'=2] {'expert'}, dimensions={0} | all-to-all | bytes 524288 | tf_op jit(solution)/shard_map/all_to_all | solution.py:108
  23.8 16.5 %collective-permute-start.3 = (f32[4,128]{1,0:T(4,128)S(1)}, f32[4,128]{1,0:T(4,128)S(1)}, u32[]{:S(2)}, u32[]{:S(2)}) collective-permute-start(f32[4,128]{1,0:T(4,128)S(1)} %get-tuple-element.60), channel_id=1, source_target_pairs={{0,0},{1,256},{128,128},{129,384},{256,1},{257,257},{384,129},{385... | collective-permute-start | bytes 6152 | tf_op jit(solution)/shard_map/ppermute | solution.py:86
  40.4 1.9 collective-permute-start.4
  42.5 2.1 collective-permute-start.1
  45.3 4.0 collective-permute-start
  50.0 7.0 %collective-permute-start.2 = (bf16[224,512]{1,0:T(8,128)(2,1)}, bf16[224,512]{1,0:T(8,128)(2,1)}, u32[]{:S(2)}, u32[]{:S(2)}) collective-permute-start(bf16[224,512]{1,0:T(8,128)(2,1)} %pad_maximum_fusion.4), channel_id=1, source_target_pairs={{0,384},{128,0},{256,128},{384,256},{1,385},{129,1},{257,129},{385... | collective-permute-start | bytes 688136 | tf_op jit(solution)/shard_map/ppermute | solution.py:19
  71.5 2.3 multiply_convert_fusion
  73.8 1.0 fusion.12
  75.2 14.4 %collective-permute-done = bf16[224,512]{1,0:T(8,128)(2,1)} collective-permute-done((bf16[224,512]{1,0:T(8,128)(2,1)}, bf16[224,512]{1,0:T(8,128)(2,1)}, u32[]{:S(2)}, u32[]{:S(2)}) %collective-permute-start) | collective-permute-done | bytes 229408 | tf_op jit(solution)/shard_map/ppermute | solution.py:19
  89.7 1.0 constant_dynamic-update-slice_fusion.18
  90.6 1.0 constant_dynamic-update-slice_fusion.17
  91.6 1.0 constant_dynamic-update-slice_fusion.16
  92.6 47.8 %all-gather.2.cloned.1.call-done = bf16[2048,2048]{1,0:T(8,128)(2,1)} async-done(((bf16[64,2048]{1,0:T(8,128)(2,1)}), bf16[2048,2048]{1,0:T(8,128)(2,1)}) %all-gather.2.cloned.1.call-update) | async-done | bytes 8388624 | tf_op jit(solution)/shard_map/all_gather | solution.py:109
  140.4 6.0 %fusion.84 = f32[224,2048]{1,0:T(8,128)S(1)} fusion(bf16[224,2048]{1,0:T(8,128)(2,1)S(1)} %constant_dynamic-update-slice_fusion.16, bf16[2048,2048]{1,0:T(8,128)(2,1)} %all-gather.2.cloned.1.call-done), kind=kOutput, calls=%fused_computation.236 | convolution fusion | flops 1879048192 | bytes 11141120 | tf_op jit(solution)/shard_map/dot_general | solution.py:27
  148.1 4.6 collective-permute-start.6
  152.8 4.6 collective-permute-start.8
  157.3 4.6 collective-permute-start.5
  162.0 4.6 collective-permute-start.10
  166.6 12.9 %collective-permute-done.5 = bf16[56,2048]{1,0:T(8,128)(2,1)S(1)} collective-permute-done((bf16[56,2048]{1,0:T(8,128)(2,1)S(1)}, bf16[56,2048]{1,0:T(8,128)(2,1)S(1)}, u32[]{:S(2)}, u32[]{:S(2)}) %collective-permute-start.5) | collective-permute-done | bytes 229408 | tf_op jit(solution)/shard_map/ppermute | solution.py:19
  179.5 5.0 %collective-permute-start.7 = (bf16[56,2048]{1,0:T(8,128)(2,1)S(1)}, bf16[56,2048]{1,0:T(8,128)(2,1)S(1)}, u32[]{:S(2)}, u32[]{:S(2)}) collective-permute-start(bf16[56,2048]{1,0:T(8,128)(2,1)S(1)} %collective-permute-done.5), channel_id=1, source_target_pairs={{0,128},{128,256},{256,384},{384,0},{1,129},{129,257},{257,385},{3... | collective-permute-start | bytes 688136 | tf_op jit(solution)/shard_map/ppermute | solution.py:19
  184.5 1.1 collective-permute-done.8
  185.6 4.6 collective-permute-start.9
  190.3 12.6 %collective-permute-done.7 = bf16[56,2048]{1,0:T(8,128)(2,1)S(1)} collective-permute-done((bf16[56,2048]{1,0:T(8,128)(2,1)S(1)}, bf16[56,2048]{1,0:T(8,128)(2,1)S(1)}, u32[]{:S(2)}, u32[]{:S(2)}) %collective-permute-start.7) | collective-permute-done | bytes 229408 | tf_op jit(solution)/shard_map/ppermute | solution.py:19
  204.2 1.2 pad_maximum_fusion
  205.4 3.1 collective-permute-start.11
  209.0 1.8 fusion.16
  211.5 2.6 bitcast_bitcast_fusion
  214.1 23.5 %all-to-all-start.1 = ((bf16[4,1280,128]{2,1,0:T(8,128)(2,1)}), bf16[4,1280,128]{2,1,0:T(8,128)(2,1)}, u32[]{:S(2)}, u32[]{:S(2)}) async-start(bf16[4,1280,128]{2,1,0:T(8,128)(2,1)} %bitcast_bitcast_fusion), calls=%async_computation.1 | async-start | bytes 2621440 | tf_op jit(solution)/shard_map/all_to_all | solution.py:168
  237.6 2.8 convolution_convert_fusion
  240.3 1.5 copy.40
  242.5 32.0 %all-to-all-done.1 = bf16[4,1280,128]{2,1,0:T(8,128)(2,1)} async-done(((bf16[4,1280,128]{2,1,0:T(8,128)(2,1)}), bf16[4,1280,128]{2,1,0:T(8,128)(2,1)}, u32[]{:S(2)}, u32[]{:S(2)}) %all-to-all-start.1) | async-done | bytes 1310752 | tf_op jit(solution)/shard_map/all_to_all | solution.py:168
  274.4 1.7 reduce_sum.59
  276.9 4.2 all-to-all-start.2
  282.4 2.7 collective-permute-start.14
  285.8 6.6 %collective-permute-start.15 = (bf16[256,128]{1,0:T(8,128)(2,1)S(1)}, bf16[256,128]{1,0:T(8,128)(2,1)S(1)}, u32[]{:S(2)}, u32[]{:S(2)}) collective-permute-start(bf16[256,128]{1,0:T(8,128)(2,1)S(1)} %get-tuple-element.42), channel_id=1, source_target_pairs={{0,4},{2,6},{4,0},{6,2},{1,5},{3,7},{5,1},{7,3},{8,12},{10,14},{12... | collective-permute-start | bytes 196616 | tf_op jit(solution)/shard_map/ppermute | solution.py:19
  292.4 1.9 collective-permute-start.16
  295.6 1.0 fusion.83
  297.2 9.8 %collective-permute-start.12 = (bf16[128,128]{1,0:T(8,128)(2,1)S(1)}, bf16[128,128]{1,0:T(8,128)(2,1)S(1)}, u32[]{:S(2)}, u32[]{:S(2)}) collective-permute-start(bf16[128,128]{1,0:T(8,128)(2,1)S(1)} %get-tuple-element.53), channel_id=1, source_target_pairs={{0,0},{1,256},{128,128},{129,384},{256,1},{257,257},{384,129},{385... | collective-permute-start | bytes 98312 | tf_op jit(solution)/shard_map/ppermute | solution.py:86
  307.1 1.9 collective-permute-start.13
  309.7 1.9 collective-permute-start.17
  311.6 4.6 collective-permute-done.13
  317.5 6.9 %all-to-all-start.3 = ((bf16[16,32,256]{2,1,0:T(8,128)(2,1)}), bf16[16,32,256]{2,1,0:T(8,128)(2,1)}, u32[]{:S(2)}, u32[]{:S(2)}) async-start(bf16[16,32,256]{2,1,0:T(8,128)(2,1)} %bitcast.53), calls=%async_computation.3 | async-start | bytes 524288 | tf_op jit(solution)/shard_map/all_to_all | solution.py:204
  324.4 1.0 constant_dynamic-update-slice_fusion.3
  325.4 1.0 constant_dynamic-update-slice_fusion.2
  326.4 5.5 %all-to-all-done.3 = bf16[16,32,256]{2,1,0:T(8,128)(2,1)} async-done(((bf16[16,32,256]{2,1,0:T(8,128)(2,1)}), bf16[16,32,256]{2,1,0:T(8,128)(2,1)}, u32[]{:S(2)}, u32[]{:S(2)}) %all-to-all-start.3) | async-done | bytes 262176 | tf_op jit(solution)/shard_map/all_to_all | solution.py:204
  331.9 2.0 fusion.2
  334.0 3.5 all-to-all-start.4
  338.1 6.9 %all-to-all-done.4 = bf16[16,32,256]{2,1,0:T(8,128)(2,1)S(1)} async-done(((bf16[16,32,256]{2,1,0:T(8,128)(2,1)}), bf16[16,32,256]{2,1,0:T(8,128)(2,1)S(1)}, u32[]{:S(2)}, u32[]{:S(2)}) %all-to-all-start.4) | async-done | bytes 262176 | tf_op jit(solution)/shard_map/all_to_all | solution.py:204
  346.0 9.0 %collective-permute-start.18 = (bf16[128,128]{1,0:T(8,128)(2,1)S(1)}, bf16[128,128]{1,0:T(8,128)(2,1)S(1)}, u32[]{:S(2)}, u32[]{:S(2)}) collective-permute-start(bf16[128,128]{1,0:T(8,128)(2,1)S(1)} %get-tuple-element.47), channel_id=1, source_target_pairs={{0,0},{1,256},{128,128},{129,384},{256,1},{257,257},{384,129},{385... | collective-permute-start | bytes 98312 | tf_op jit(solution)/shard_map/ppermute | solution.py:86
  355.0 3.3 collective-permute-start.19
  358.4 1.6 collective-permute-done.18
  360.0 4.3 collective-permute-done.19
  364.9 10.2 %all_to_all.36 = bf16[16,2,32,128]{3,2,1,0:T(8,128)(2,1)S(1)} all-to-all(bf16[16,2,32,128]{3,2,1,0:T(8,128)(2,1)S(1)} %bitcast.182), channel_id=1, replica_groups=mesh['client'=4,'expert'=16,'zlo'=4,'core'=2] {'expert'}, dimensions={0} | all-to-all | bytes 524288 | tf_op jit(solution)/shard_map/all_to_all | solution.py:204
  375.1 1.1 broadcast_in_dim.117
  376.2 5.6 %all-to-all-start.6 = ((bf16[4,1024,128]{2,1,0:T(8,128)(2,1)}), bf16[4,1024,128]{2,1,0:T(8,128)(2,1)}, u32[]{:S(2)}, u32[]{:S(2)}) async-start(bf16[4,1024,128]{2,1,0:T(8,128)(2,1)} %broadcast_in_dim.117), calls=%async_computation.7 | async-start | bytes 2097152 | tf_op jit(solution)/shard_map/all_to_all | solution.py:221
  382.5 60.0 %all-to-all-done.6 = bf16[4,1024,128]{2,1,0:T(8,128)(2,1)} async-done(((bf16[4,1024,128]{2,1,0:T(8,128)(2,1)}), bf16[4,1024,128]{2,1,0:T(8,128)(2,1)}, u32[]{:S(2)}, u32[]{:S(2)}) %all-to-all-start.6) | async-done | bytes 1048608 | tf_op jit(solution)/shard_map/all_to_all | solution.py:221
  442.6 1.5 copy.35
  444.1 1.9 collective-permute-start.20
  446.0 1.6 broadcast_in_dim.111
  447.6 1.1 constant_dynamic-update-slice_fusion.1
  448.8 2.3 constant_dynamic-update-slice_fusion
  451.1 13.7 %reduce-scatter.5.cloned.1.call-done = bf16[448,512]{1,0:T(8,128)(2,1)} async-done(((bf16[1792,512]{1,0:T(8,128)(2,1)}), bf16[448,512]{1,0:T(8,128)(2,1)}) %reduce-scatter.5.cloned.1.call-update) | async-done | bytes 458768 | tf_op jit(solution)/shard_map/reduce_scatter | solution.py:194
  464.8 3.7 convolution_add_fusion
  (146 shorter events, 32.1 us)
Async XLA Ops:
  6.5 1.8 copy-start
  6.5 17.2 %copy-start.7 = (f32[1,128,2]{1,2,0:T(2,128)S(1)}, f32[1,128,2]{1,2,0:T(2,128)}, u32[]{:S(2)}) copy-start(f32[1,128,2]{1,2,0:T(2,128)} %param.12) | copy-start | bytes 3076
  6.5 35.8 %copy-start.5 = (bf16[448,512]{1,0:T(8,128)(2,1)S(1)}, bf16[448,512]{1,0:T(8,128)(2,1)}, u32[]{:S(2)}) copy-start(bf16[448,512]{1,0:T(8,128)(2,1)} %param.14) | copy-start | bytes 1376260
  6.5 35.8 %copy-start.4 = (bf16[448,512]{1,0:T(8,128)(2,1)S(1)}, bf16[448,512]{1,0:T(8,128)(2,1)}, u32[]{:S(2)}) copy-start(bf16[448,512]{1,0:T(8,128)(2,1)} %param.15) | copy-start | bytes 1376260
  6.5 133.8 %all-gather.2.cloned.1.call-start = ((), (), s32[]{:S(2)}) async-start(), calls=%async_computation.9 | async-start | bytes 8650752 | tf_op jit(solution)/shard_map/all_gather | solution.py:109
  23.7 33.4 %copy-start.8 = (s32[4]{0:T(128)S(1)}, s32[4]{0:T(128)}, u32[]{:S(2)}) copy-start(s32[4]{0:T(128)} %param.13) | copy-start | bytes 52
  23.8 51.0 %collective-permute-start.3 = (f32[4,128]{1,0:T(4,128)S(1)}, f32[4,128]{1,0:T(4,128)S(1)}, u32[]{:S(2)}, u32[]{:S(2)}) collective-permute-start(f32[4,128]{1,0:T(4,128)S(1)} %get-tuple-element.60), channel_id=1, source_target_pairs={{0,0},{1,256},{128,128},{129,384},{256,1},{257,257},{384,129},{385... | collective-permute-start | bytes 6152 | tf_op jit(solution)/shard_map/ppermute | solution.py:86
  40.4 34.5 %collective-permute-start.4 = (f32[4,128]{1,0:T(4,128)S(1)}, f32[4,128]{1,0:T(4,128)S(1)}, u32[]{:S(2)}, u32[]{:S(2)}) collective-permute-start(f32[4,128]{1,0:T(4,128)S(1)} %get-tuple-element.61), channel_id=1, source_target_pairs={{0,128},{1,384},{128,0},{129,256},{256,129},{257,385},{384,1},{385... | collective-permute-start | bytes 6152 | tf_op jit(solution)/shard_map/ppermute | solution.py:86
  42.5 17.7 %copy-start.1 = (bf16[1,448,2048]{2,1,0:T(8,128)(2,1)S(1)}, bf16[1,448,2048]{2,1,0:T(8,128)(2,1)}, u32[]{:S(2)}) copy-start(bf16[1,448,2048]{2,1,0:T(8,128)(2,1)} %param.17) | copy-start | bytes 5505028
  42.5 48.1 %collective-permute-start.1 = (bf16[224,512]{1,0:T(8,128)(2,1)S(1)}, bf16[224,512]{1,0:T(8,128)(2,1)}, u32[]{:S(2)}, u32[]{:S(2)}) collective-permute-start(bf16[224,512]{1,0:T(8,128)(2,1)S(1)} %pad_maximum_fusion.3), channel_id=1, source_target_pairs={{0,256},{128,384},{256,0},{384,128},{1,257},{129,385},{257,1},{385... | collective-permute-start | bytes 688136 | tf_op jit(solution)/shard_map/ppermute | solution.py:19
  45.3 44.4 %collective-permute-start = (bf16[224,512]{1,0:T(8,128)(2,1)}, bf16[224,512]{1,0:T(8,128)(2,1)}, u32[]{:S(2)}, u32[]{:S(2)}) collective-permute-start(bf16[224,512]{1,0:T(8,128)(2,1)} %pad_maximum_fusion.2), channel_id=1, source_target_pairs={{0,128},{128,256},{256,384},{384,0},{1,129},{129,257},{257,385},{3... | collective-permute-start | bytes 688136 | tf_op jit(solution)/shard_map/ppermute | solution.py:19
  50.0 41.6 %collective-permute-start.2 = (bf16[224,512]{1,0:T(8,128)(2,1)}, bf16[224,512]{1,0:T(8,128)(2,1)}, u32[]{:S(2)}, u32[]{:S(2)}) collective-permute-start(bf16[224,512]{1,0:T(8,128)(2,1)} %pad_maximum_fusion.4), channel_id=1, source_target_pairs={{0,384},{128,0},{256,128},{384,256},{1,385},{129,1},{257,129},{385... | collective-permute-start | bytes 688136 | tf_op jit(solution)/shard_map/ppermute | solution.py:19
  60.0 10.7 %copy-start.2 = (bf16[224,2048]{1,0:T(8,128)(2,1)}, bf16[224,2048]{1,0:T(8,128)(2,1)S(1)}, u32[]{:S(2)}) copy-start(bf16[224,2048]{1,0:T(8,128)(2,1)S(1)} %maximum_dynamic-update-slice_fusion) | copy-start | bytes 2752516
  71.5 18.1 %copy-start.3 = (bf16[224,2048]{1,0:T(8,128)(2,1)S(1)}, bf16[224,2048]{1,0:T(8,128)(2,1)}, u32[]{:S(2)}) copy-start(bf16[224,2048]{1,0:T(8,128)(2,1)} %copy-done.2) | copy-start | bytes 2752516
  148.1 42.1 %collective-permute-start.6 = (bf16[56,2048]{1,0:T(8,128)(2,1)S(1)}, bf16[56,2048]{1,0:T(8,128)(2,1)S(1)}, u32[]{:S(2)}, u32[]{:S(2)}) collective-permute-start(bf16[56,2048]{1,0:T(8,128)(2,1)S(1)} %get-tuple-element.31), channel_id=1, source_target_pairs={{0,128},{128,256},{256,384},{384,0},{1,129},{129,257},{257,385},{3... | collective-permute-start | bytes 688136 | tf_op jit(solution)/shard_map/ppermute | solution.py:19
  152.8 32.8 %collective-permute-start.8 = (bf16[56,2048]{1,0:T(8,128)(2,1)S(1)}, bf16[56,2048]{1,0:T(8,128)(2,1)S(1)}, u32[]{:S(2)}, u32[]{:S(2)}) collective-permute-start(bf16[56,2048]{1,0:T(8,128)(2,1)S(1)} %get-tuple-element.31), channel_id=1, source_target_pairs={{0,384},{128,0},{256,128},{384,256},{1,385},{129,1},{257,129},{385... | collective-permute-start | bytes 688136 | tf_op jit(solution)/shard_map/ppermute | solution.py:19
  157.3 22.1 %collective-permute-start.5 = (bf16[56,2048]{1,0:T(8,128)(2,1)S(1)}, bf16[56,2048]{1,0:T(8,128)(2,1)S(1)}, u32[]{:S(2)}, u32[]{:S(2)}) collective-permute-start(bf16[56,2048]{1,0:T(8,128)(2,1)S(1)} %get-tuple-element.33), channel_id=1, source_target_pairs={{0,128},{128,256},{256,384},{384,0},{1,129},{129,257},{257,385},{3... | collective-permute-start | bytes 688136 | tf_op jit(solution)/shard_map/ppermute | solution.py:19
  162.0 41.0 %collective-permute-start.10 = (bf16[56,2048]{1,0:T(8,128)(2,1)S(1)}, bf16[56,2048]{1,0:T(8,128)(2,1)S(1)}, u32[]{:S(2)}, u32[]{:S(2)}) collective-permute-start(bf16[56,2048]{1,0:T(8,128)(2,1)S(1)} %get-tuple-element.33), channel_id=1, source_target_pairs={{0,384},{128,0},{256,128},{384,256},{1,385},{129,1},{257,129},{385... | collective-permute-start | bytes 688136 | tf_op jit(solution)/shard_map/ppermute | solution.py:19
  166.6 36.9 %copy-start.6 = (bf16[448,512]{1,0:T(8,128)(2,1)S(1)}, bf16[448,512]{1,0:T(8,128)(2,1)}, u32[]{:S(2)}) copy-start(bf16[448,512]{1,0:T(8,128)(2,1)} %param.16) | copy-start | bytes 1376260
  179.5 23.4 %collective-permute-start.7 = (bf16[56,2048]{1,0:T(8,128)(2,1)S(1)}, bf16[56,2048]{1,0:T(8,128)(2,1)S(1)}, u32[]{:S(2)}, u32[]{:S(2)}) collective-permute-start(bf16[56,2048]{1,0:T(8,128)(2,1)S(1)} %collective-permute-done.5), channel_id=1, source_target_pairs={{0,128},{128,256},{256,384},{384,0},{1,129},{129,257},{257,385},{3... | collective-permute-start | bytes 688136 | tf_op jit(solution)/shard_map/ppermute | solution.py:19
  185.6 17.3 %collective-permute-start.9 = (bf16[56,2048]{1,0:T(8,128)(2,1)S(1)}, bf16[56,2048]{1,0:T(8,128)(2,1)S(1)}, u32[]{:S(2)}, u32[]{:S(2)}) collective-permute-start(bf16[56,2048]{1,0:T(8,128)(2,1)S(1)} %collective-permute-done.8), channel_id=1, source_target_pairs={{0,384},{128,0},{256,128},{384,256},{1,385},{129,1},{257,129},{385... | collective-permute-start | bytes 688136 | tf_op jit(solution)/shard_map/ppermute | solution.py:19
  205.4 6.1 %collective-permute-start.11 = (bf16[1280,512]{1,0:T(8,128)(2,1)}, bf16[1280,512]{1,0:T(8,128)(2,1)}, u32[]{:S(2)}, u32[]{:S(2)}) collective-permute-start(bf16[1280,512]{1,0:T(8,128)(2,1)} %pad_maximum_fusion), channel_id=1, source_target_pairs={{0,1},{1,0},{2,3},{3,2},{4,5},{5,4},{6,7},{7,6},{8,9},{9,8},{10,11... | collective-permute-start | bytes 3932168 | tf_op jit(solution)/shard_map/ppermute | solution.py:19
  214.1 60.3 %all-to-all-start.1 = ((bf16[4,1280,128]{2,1,0:T(8,128)(2,1)}), bf16[4,1280,128]{2,1,0:T(8,128)(2,1)}, u32[]{:S(2)}, u32[]{:S(2)}) async-start(bf16[4,1280,128]{2,1,0:T(8,128)(2,1)} %bitcast_bitcast_fusion), calls=%async_computation.1 | async-start | bytes 2621440 | tf_op jit(solution)/shard_map/all_to_all | solution.py:168
  237.6 88.9 %reduce-scatter.3.cloned.1.call-start = ((), (), s32[]{:S(2)}) async-start(), calls=%async_computation.10 | async-start | bytes 2359296 | tf_op jit(solution)/shard_map/reduce_scatter | solution.py:185
  276.9 18.7 %all-to-all-start.2 = ((bf16[16,2,32,128]{3,2,1,0:T(8,128)(2,1)}), bf16[16,2,32,128]{3,2,1,0:T(8,128)(2,1)}, u32[]{:S(2)}, u32[]{:S(2)}) async-start(bf16[16,2,32,128]{3,2,1,0:T(8,128)(2,1)} %copy.31), calls=%async_computation.2 | async-start | bytes 524288 | tf_op jit(solution)/shard_map/all_to_all | solution.py:204
  282.4 11.9 %collective-permute-start.14 = (bf16[256,128]{1,0:T(8,128)(2,1)S(1)}, bf16[256,128]{1,0:T(8,128)(2,1)S(1)}, u32[]{:S(2)}, u32[]{:S(2)}) collective-permute-start(bf16[256,128]{1,0:T(8,128)(2,1)S(1)} %get-tuple-element.42), channel_id=1, source_target_pairs={{0,2},{2,4},{4,6},{6,0},{1,3},{3,5},{5,7},{7,1},{8,10},{10,12},{12... | collective-permute-start | bytes 196616 | tf_op jit(solution)/shard_map/ppermute | solution.py:19
  285.8 9.2 %collective-permute-start.15 = (bf16[256,128]{1,0:T(8,128)(2,1)S(1)}, bf16[256,128]{1,0:T(8,128)(2,1)S(1)}, u32[]{:S(2)}, u32[]{:S(2)}) collective-permute-start(bf16[256,128]{1,0:T(8,128)(2,1)S(1)} %get-tuple-element.42), channel_id=1, source_target_pairs={{0,4},{2,6},{4,0},{6,2},{1,5},{3,7},{5,1},{7,3},{8,12},{10,14},{12... | collective-permute-start | bytes 196616 | tf_op jit(solution)/shard_map/ppermute | solution.py:19
  292.4 16.7 %collective-permute-start.16 = (bf16[256,128]{1,0:T(8,128)(2,1)S(1)}, bf16[256,128]{1,0:T(8,128)(2,1)S(1)}, u32[]{:S(2)}, u32[]{:S(2)}) collective-permute-start(bf16[256,128]{1,0:T(8,128)(2,1)S(1)} %get-tuple-element.42), channel_id=1, source_target_pairs={{0,6},{2,0},{4,2},{6,4},{1,7},{3,1},{5,3},{7,5},{8,14},{10,8},{12,... | collective-permute-start | bytes 196616 | tf_op jit(solution)/shard_map/ppermute | solution.py:19
  297.2 14.4 %collective-permute-start.12 = (bf16[128,128]{1,0:T(8,128)(2,1)S(1)}, bf16[128,128]{1,0:T(8,128)(2,1)S(1)}, u32[]{:S(2)}, u32[]{:S(2)}) collective-permute-start(bf16[128,128]{1,0:T(8,128)(2,1)S(1)} %get-tuple-element.53), channel_id=1, source_target_pairs={{0,0},{1,256},{128,128},{129,384},{256,1},{257,257},{384,129},{385... | collective-permute-start | bytes 98312 | tf_op jit(solution)/shard_map/ppermute | solution.py:86
  307.1 9.2 %collective-permute-start.13 = (bf16[128,128]{1,0:T(8,128)(2,1)S(1)}, bf16[128,128]{1,0:T(8,128)(2,1)S(1)}, u32[]{:S(2)}, u32[]{:S(2)}) collective-permute-start(bf16[128,128]{1,0:T(8,128)(2,1)S(1)} %get-tuple-element.52), channel_id=1, source_target_pairs={{0,128},{1,384},{128,0},{129,256},{256,129},{257,385},{384,1},{385... | collective-permute-start | bytes 98312 | tf_op jit(solution)/shard_map/ppermute | solution.py:86
  309.7 15.7 %collective-permute-start.17 = (bf16[256,512]{1,0:T(8,128)(2,1)}, bf16[256,512]{1,0:T(8,128)(2,1)}, u32[]{:S(2)}, u32[]{:S(2)}) collective-permute-start(bf16[256,512]{1,0:T(8,128)(2,1)} %constant_dynamic-update-slice_fusion.4), channel_id=1, source_target_pairs={{0,1},{1,0},{2,3},{3,2},{4,5},{5,4},{6,7},{7,6},{8,9},{9,8},{10,11... | collective-permute-start | bytes 786440 | tf_op jit(solution)/shard_map/ppermute | solution.py:19
  317.5 14.5 %all-to-all-start.3 = ((bf16[16,32,256]{2,1,0:T(8,128)(2,1)}), bf16[16,32,256]{2,1,0:T(8,128)(2,1)}, u32[]{:S(2)}, u32[]{:S(2)}) async-start(bf16[16,32,256]{2,1,0:T(8,128)(2,1)} %bitcast.53), calls=%async_computation.3 | async-start | bytes 524288 | tf_op jit(solution)/shard_map/all_to_all | solution.py:204
  334.0 11.0 %all-to-all-start.4 = ((bf16[16,32,256]{2,1,0:T(8,128)(2,1)}), bf16[16,32,256]{2,1,0:T(8,128)(2,1)S(1)}, u32[]{:S(2)}, u32[]{:S(2)}) async-start(bf16[16,32,256]{2,1,0:T(8,128)(2,1)} %bitcast.178), calls=%async_computation.5 | async-start | bytes 524288 | tf_op jit(solution)/shard_map/all_to_all | solution.py:204
  346.0 14.0 %collective-permute-start.18 = (bf16[128,128]{1,0:T(8,128)(2,1)S(1)}, bf16[128,128]{1,0:T(8,128)(2,1)S(1)}, u32[]{:S(2)}, u32[]{:S(2)}) collective-permute-start(bf16[128,128]{1,0:T(8,128)(2,1)S(1)} %get-tuple-element.47), channel_id=1, source_target_pairs={{0,0},{1,256},{128,128},{129,384},{256,1},{257,257},{384,129},{385... | collective-permute-start | bytes 98312 | tf_op jit(solution)/shard_map/ppermute | solution.py:86
  355.0 9.2 %collective-permute-start.19 = (bf16[128,128]{1,0:T(8,128)(2,1)S(1)}, bf16[128,128]{1,0:T(8,128)(2,1)S(1)}, u32[]{:S(2)}, u32[]{:S(2)}) collective-permute-start(bf16[128,128]{1,0:T(8,128)(2,1)S(1)} %get-tuple-element.46), channel_id=1, source_target_pairs={{0,128},{1,384},{128,0},{129,256},{256,129},{257,385},{384,1},{385... | collective-permute-start | bytes 98312 | tf_op jit(solution)/shard_map/ppermute | solution.py:86
  376.2 66.3 %all-to-all-start.6 = ((bf16[4,1024,128]{2,1,0:T(8,128)(2,1)}), bf16[4,1024,128]{2,1,0:T(8,128)(2,1)}, u32[]{:S(2)}, u32[]{:S(2)}) async-start(bf16[4,1024,128]{2,1,0:T(8,128)(2,1)} %broadcast_in_dim.117), calls=%async_computation.7 | async-start | bytes 2097152 | tf_op jit(solution)/shard_map/all_to_all | solution.py:221
  381.8 83.0 %reduce-scatter.5.cloned.1.call-start = ((), (), s32[]{:S(2)}) async-start(), calls=%async_computation.11 | async-start | bytes 2293760 | tf_op jit(solution)/shard_map/reduce_scatter | solution.py:194
  444.1 4.7 collective-permute-start.20
Sparse Core Ops, SparseCore 0:
  23.8 116.5 all-gather.1
  242.0 51.4 reduce-scatter.2
  385.4 79.2 reduce-scatter.4

commit v3 on v2

--- a/solution.py
+++ b/solution.py
@@ -178,15 +178,17 @@
 
     give = products(1 - q).astype(BF16)
     got = shift(give, "core", 1)
-    both = over_zlo(products(q) + got.astype(F32)).astype(BF16)
+    both = (products(q) + got.astype(F32)).astype(BF16)
 
     control_move = dot(own, control, 0, 0).astype(BF16).reshape(rows, ns, pair * cols)
     control_move = control_move.transpose(1, 0, 2).reshape(ns * rows, pair * cols)
     control_move = lax.psum_scatter(control_move, ("zlo", "core"), scatter_dimension=0, tiled=True)
 
-    gram = both[pair * rows :]
-    gram = [gram] + [shift(gram, "zlo", k) for k in range(1, nz)]
-    gram = place(gram, lambda k: (zl - k) % nz, 1)
+    gram = both[pair * rows :].astype(F32)
+    for k in range(1, nz):
+        part = shift(both[pair * rows :], "zlo", k)
+        gram = gram + part.astype(F32)
+    gram = gram.astype(BF16)
     other = shift(gram, "core", 1)
     gram = place([gram, other], lambda k: (q + k) % CORES, 0)
 
@@ -203,9 +205,10 @@
     def exchange(x):
         return lax.all_to_all(x, "expert", 0, 0, tiled=True)
 
-    value = both[: pair * rows].reshape(pair, nm, cap, cols).transpose(1, 0, 2, 3)
+    value = both[: pair * rows].reshape(pair, nm, cap, wide).transpose(1, 0, 2, 3)
     value = exchange(value)
-    value = hop(jnp.stack([to_tokens(combines[a], value[:, a]) for a in range(pair)]).astype(BF16))
+    value = over_zlo(jnp.concatenate([to_tokens(combines[a], value[:, a]) for a in range(pair)], axis=0))
+    value = hop(value.astype(BF16).reshape(pair, tok, cols))
     residual = live * (jnp.concatenate([value[a] for a in range(pair)], axis=1).astype(F32) - goal)
     cotangent = exchange(jnp.repeat(to_rows(combine, residual), copies, axis=0))
     cotangent = cotangent.reshape(rows, pair * cols)
@@ -213,13 +216,13 @@
     change = exchange(change.astype(BF16).reshape(nm, cap, pair * cols))
     mean = share[c] * (residual - (step_size / LOCAL_STEPS) * live * to_tokens(combine, change))
     mean = hop(jnp.stack([mean[:, a * cols : (a + 1) * cols] for a in range(pair)]).astype(BF16))
-    cotangent = jnp.stack([to_rows(combines[a], mean[a].astype(F32)) for a in range(pair)], axis=1)
+
+    mean = jnp.broadcast_to(mean.reshape(1, pair * tok, cols), (nz, pair * tok, cols))
+    mean = lax.all_to_all(mean, "zlo", 0, 0, tiled=True)
+    mean = mean.transpose(1, 0, 2).reshape(pair, tok, wide).astype(F32)
+    cotangent = jnp.stack([to_rows(combines[a], mean[a]) for a in range(pair)], axis=1)
     cotangent = exchange(jnp.repeat(cotangent, copies, axis=0))
-    cotangent = cotangent.transpose(1, 0, 2, 3).reshape(pair * rows, cols)
-
-    cotangent = jnp.broadcast_to(cotangent[None], (nz, pair * rows, cols))
-    cotangent = lax.all_to_all(cotangent, "zlo", 0, 0, tiled=True)
-    cotangent = cotangent.transpose(1, 0, 2).reshape(pair * rows, wide)
+    cotangent = cotangent.transpose(1, 0, 2, 3).reshape(pair * rows, wide)
     other = shift(cotangent, "core", 1)
     cotangent = place([cotangent, other], lambda k: (q + k) % CORES, 0)
     return dot(full, cotangent, 1, 0) + control_sum.astype(F32)

time: 477 us -> 455 us (0.954)
  the two profiles are of different devices: /device:TPU:33 before, /device:TPU:1 now
where the time goes in v3:
time: 455 us; the launch traced here: 453 us
  waiting for transfers between devices  164 us (36%)
  starting transfers between devices  131 us (29%)
  blocking collectives  63.5 us (14%)
  local copies, waits for them, and re-layouts  34.2 us (8%)
  matrix products  23.6 us (5%)
  other arithmetic  21.4 us (5%)
  between operations  15 us (3%)
    ppermute x15, starting transfers between devices, shift(): return lax.ppermute(x, axis, [(i, (i + by) % n) for i in range(n)])  57.9 us
    reduce_scatter x1, waiting for transfers between devices, local(): lax.psum_scatter(control_sum, 'client', scatter_dimension=0, tiled=True)  50.5 us
    ppermute x15, waiting for transfers between devices, shift(): return lax.ppermute(x, axis, [(i, (i + by) % n) for i in range(n)])  50.2 us
    all_to_all x2, blocking collectives, exchange(): return lax.all_to_all(x, 'expert', 0, 0, tiled=True)  48.6 us
    ppermute x6, starting transfers between devices, hop(): arrived.append(lax.ppermute(item, ('client', 'core'), ends))  48 us
    all_gather x1, waiting for transfers between devices, local(): lax.all_gather(features, ('client', 'zlo', 'core'), axis=0, tiled=True)  33.9 us
    dot_general x20, matrix products, dot(): lax.dot_general(a, b, (((da,), (db,)), ((), ())), preferred_element_type=...  23.6 us
    all_to_all x1, blocking collectives, local(): lax.all_to_all(sent, 'expert', 0, 0, tiled=True).reshape(nm * few, -1)  14.9 us
  transfers between devices with their start and end apart: 28, of which 13 were waited for; matrix products, arithmetic and copies ran while one was open for 13% of the time, Pallas kernels for 0%

profile of v3, /device:TPU:1, one launch (start us, length us, event | category | flops | bytes accessed | tf_op | source)
XLA Modules:
  0.0 453.1 jit_solution(13543448743952293048)
XLA Ops:
  8.8 14.9 %all_to_all.35 = bf16[16,4,2048]{2,1,0:T(4,128)(2,1)S(1)} all-to-all(bf16[16,4,2048]{2,1,0:T(4,128)(2,1)S(1)} %bitcast.192), channel_id=1, replica_groups=mesh['client'=4,'expert'=16,'zlo'=4,'core'=2] {'expert'}, dimensions={0} | all-to-all | bytes 524288 | tf_op jit(solution)/shard_map/all_to_all | solution.py:108
  25.3 17.4 %collective-permute-start.3 = (f32[4,128]{1,0:T(4,128)}, f32[4,128]{1,0:T(4,128)}, u32[]{:S(2)}, u32[]{:S(2)}) collective-permute-start(f32[4,128]{1,0:T(4,128)} %get-tuple-element.64), channel_id=1, source_target_pairs={{0,0},{1,256},{128,128},{129,384},{256,1},{257,257},{384,129},{385... | collective-permute-start | bytes 6152 | tf_op jit(solution)/shard_map/ppermute | solution.py:86
  42.7 1.9 collective-permute-start.4
  46.2 2.0 collective-permute-start.1
  48.9 5.2 %collective-permute-start = (bf16[224,512]{1,0:T(8,128)(2,1)}, bf16[224,512]{1,0:T(8,128)(2,1)}, u32[]{:S(2)}, u32[]{:S(2)}) collective-permute-start(bf16[224,512]{1,0:T(8,128)(2,1)} %pad_maximum_fusion.3), channel_id=1, source_target_pairs={{0,128},{128,256},{256,384},{384,0},{1,129},{129,257},{257,385},{3... | collective-permute-start | bytes 688136 | tf_op jit(solution)/shard_map/ppermute | solution.py:19
  54.8 5.9 %collective-permute-start.2 = (bf16[224,512]{1,0:T(8,128)(2,1)}, bf16[224,512]{1,0:T(8,128)(2,1)}, u32[]{:S(2)}, u32[]{:S(2)}) collective-permute-start(bf16[224,512]{1,0:T(8,128)(2,1)} %pad_maximum_fusion.5), channel_id=1, source_target_pairs={{0,384},{128,0},{256,128},{384,256},{1,385},{129,1},{257,129},{385... | collective-permute-start | bytes 688136 | tf_op jit(solution)/shard_map/ppermute | solution.py:19
  64.7 0.9 maximum_dynamic-update-slice_fusion
  78.5 2.2 multiply_convert_fusion
  80.7 1.0 fusion.9
  84.1 20.8 %collective-permute-done = bf16[224,512]{1,0:T(8,128)(2,1)} collective-permute-done((bf16[224,512]{1,0:T(8,128)(2,1)}, bf16[224,512]{1,0:T(8,128)(2,1)}, u32[]{:S(2)}, u32[]{:S(2)}) %collective-permute-start) | collective-permute-done | bytes 229408 | tf_op jit(solution)/shard_map/ppermute | solution.py:19
  104.9 1.0 constant_dynamic-update-slice_fusion.14
  105.9 1.0 constant_dynamic-update-slice_fusion.13
  106.9 1.0 constant_dynamic-update-slice_fusion.12
  107.8 33.9 %all-gather.2.cloned.1.call-done = bf16[2048,2048]{1,0:T(8,128)(2,1)} async-done(((bf16[64,2048]{1,0:T(8,128)(2,1)}), bf16[2048,2048]{1,0:T(8,128)(2,1)}) %all-gather.2.cloned.1.call-update) | async-done | bytes 8388624 | tf_op jit(solution)/shard_map/all_gather | solution.py:109
  141.7 6.0 %fusion.71 = f32[224,2048]{1,0:T(8,128)S(1)} fusion(bf16[224,2048]{1,0:T(8,128)(2,1)S(1)} %constant_dynamic-update-slice_fusion.12, bf16[2048,2048]{1,0:T(8,128)(2,1)} %all-gather.2.cloned.1.call-done), kind=kOutput, calls=%fused_computation.222 | convolution fusion | flops 1879048192 | bytes 11141120 | tf_op jit(solution)/shard_map/dot_general | solution.py:27
  149.5 4.9 %collective-permute-start.6 = (bf16[56,2048]{1,0:T(8,128)(2,1)S(1)}, bf16[56,2048]{1,0:T(8,128)(2,1)S(1)}, u32[]{:S(2)}, u32[]{:S(2)}) collective-permute-start(bf16[56,2048]{1,0:T(8,128)(2,1)S(1)} %get-tuple-element.35), channel_id=1, source_target_pairs={{0,128},{128,256},{256,384},{384,0},{1,129},{129,257},{257,385},{3... | collective-permute-start | bytes 688136 | tf_op jit(solution)/shard_map/ppermute | solution.py:19
  154.4 4.3 collective-permute-start.8
  158.7 4.9 %collective-permute-start.5 = (bf16[56,2048]{1,0:T(8,128)(2,1)S(1)}, bf16[56,2048]{1,0:T(8,128)(2,1)S(1)}, u32[]{:S(2)}, u32[]{:S(2)}) collective-permute-start(bf16[56,2048]{1,0:T(8,128)(2,1)S(1)} %get-tuple-element.37), channel_id=1, source_target_pairs={{0,128},{128,256},{256,384},{384,0},{1,129},{129,257},{257,385},{3... | collective-permute-start | bytes 688136 | tf_op jit(solution)/shard_map/ppermute | solution.py:19
  163.6 4.3 collective-permute-start.10
  167.9 13.7 %collective-permute-done.5 = bf16[56,2048]{1,0:T(8,128)(2,1)S(1)} collective-permute-done((bf16[56,2048]{1,0:T(8,128)(2,1)S(1)}, bf16[56,2048]{1,0:T(8,128)(2,1)S(1)}, u32[]{:S(2)}, u32[]{:S(2)}) %collective-permute-start.5) | collective-permute-done | bytes 229408 | tf_op jit(solution)/shard_map/ppermute | solution.py:19
  181.7 6.5 %collective-permute-start.7 = (bf16[56,2048]{1,0:T(8,128)(2,1)S(1)}, bf16[56,2048]{1,0:T(8,128)(2,1)S(1)}, u32[]{:S(2)}, u32[]{:S(2)}) collective-permute-start(bf16[56,2048]{1,0:T(8,128)(2,1)S(1)} %collective-permute-done.5), channel_id=1, source_target_pairs={{0,128},{128,256},{256,384},{384,0},{1,129},{129,257},{257,385},{3... | collective-permute-start | bytes 688136 | tf_op jit(solution)/shard_map/ppermute | solution.py:19
  188.2 2.7 collective-permute-start.9
  190.9 13.2 %collective-permute-done.7 = bf16[56,2048]{1,0:T(8,128)(2,1)S(1)} collective-permute-done((bf16[56,2048]{1,0:T(8,128)(2,1)S(1)}, bf16[56,2048]{1,0:T(8,128)(2,1)S(1)}, u32[]{:S(2)}, u32[]{:S(2)}) %collective-permute-start.7) | collective-permute-done | bytes 229408 | tf_op jit(solution)/shard_map/ppermute | solution.py:19
  204.1 2.3 collective-permute-done.9
  207.8 1.1 pad_maximum_fusion
  208.9 3.0 collective-permute-start.11
  212.0 2.8 convolution_convert_fusion
  214.8 1.5 copy.50
  217.5 1.8 fusion
  220.3 33.8 %all_to_all.36 = bf16[16,2,32,512]{3,2,1,0:T(8,128)(2,1)S(1)} all-to-all(bf16[16,2,32,512]{3,2,1,0:T(8,128)(2,1)S(1)} %bitcast.177), channel_id=1, replica_groups=mesh['client'=4,'expert'=16,'zlo'=4,'core'=2] {'expert'}, dimensions={0} | all-to-all | bytes 2097152 | tf_op jit(solution)/shard_map/all_to_all | solution.py:206
  254.1 0.9 fusion.68
  255.3 2.0 convert_reduce_fusion
  257.2 1.2 copy.46
  258.5 1.5 convolution_convert_fusion.7
  260.1 1.5 convolution_convert_fusion.6
  262.3 10.4 %all-to-all-start.2 = ((bf16[4,256,128]{2,1,0:T(8,128)(2,1)}), bf16[4,256,128]{2,1,0:T(8,128)(2,1)S(1)}, u32[]{:S(2)}, u32[]{:S(2)}) async-start(bf16[4,256,128]{2,1,0:T(8,128)(2,1)} %maximum_bitcast_fusion), calls=%async_computation.2 | async-start | bytes 524288 | tf_op jit(solution)/shard_map/all_to_all | solution.py:168
  272.7 1.0 slice.250
  273.7 3.4 collective-permute-start.14
  277.1 4.0 collective-permute-start.15
  281.1 3.1 collective-permute-start.16
  285.6 16.5 %collective-permute-start.12 = (bf16[128,128]{1,0:T(8,128)(2,1)S(1)}, bf16[128,128]{1,0:T(8,128)(2,1)S(1)}, u32[]{:S(2)}, u32[]{:S(2)}) collective-permute-start(bf16[128,128]{1,0:T(8,128)(2,1)S(1)} %get-tuple-element.57), channel_id=1, source_target_pairs={{0,0},{1,256},{128,128},{129,384},{256,1},{257,257},{384,129},{385... | collective-permute-start | bytes 98312 | tf_op jit(solution)/shard_map/ppermute | solution.py:86
  302.1 1.9 collective-permute-start.13
  304.1 2.0 constant_dynamic-update-slice_fusion.3
  306.0 1.9 collective-permute-start.17
  308.0 3.3 collective-permute-done.13
  312.4 5.4 %all-to-all-start.3 = ((bf16[16,32,256]{2,1,0:T(8,128)(2,1)}), bf16[16,32,256]{2,1,0:T(8,128)(2,1)S(1)}, u32[]{:S(2)}, u32[]{:S(2)}) async-start(bf16[16,32,256]{2,1,0:T(8,128)(2,1)} %bitcast.189), calls=%async_computation.3 | async-start | bytes 524288 | tf_op jit(solution)/shard_map/all_to_all | solution.py:206
  317.9 1.0 constant_dynamic-update-slice_fusion.2
  318.8 6.5 %all-to-all-done.3 = bf16[16,32,256]{2,1,0:T(8,128)(2,1)S(1)} async-done(((bf16[16,32,256]{2,1,0:T(8,128)(2,1)}), bf16[16,32,256]{2,1,0:T(8,128)(2,1)S(1)}, u32[]{:S(2)}, u32[]{:S(2)}) %all-to-all-start.3) | async-done | bytes 262176 | tf_op jit(solution)/shard_map/all_to_all | solution.py:206
  325.4 2.0 fusion.1
  327.3 3.5 all-to-all-start.4
  331.5 7.4 %all-to-all-done.4 = bf16[16,32,256]{2,1,0:T(8,128)(2,1)S(1)} async-done(((bf16[16,32,256]{2,1,0:T(8,128)(2,1)}), bf16[16,32,256]{2,1,0:T(8,128)(2,1)S(1)}, u32[]{:S(2)}, u32[]{:S(2)}) %all-to-all-start.4) | async-done | bytes 262176 | tf_op jit(solution)/shard_map/all_to_all | solution.py:206
  339.9 7.7 %collective-permute-start.18 = (bf16[128,128]{1,0:T(8,128)(2,1)S(1)}, bf16[128,128]{1,0:T(8,128)(2,1)S(1)}, u32[]{:S(2)}, u32[]{:S(2)}) collective-permute-start(bf16[128,128]{1,0:T(8,128)(2,1)S(1)} %get-tuple-element.51), channel_id=1, source_target_pairs={{0,0},{1,256},{128,128},{129,384},{256,1},{257,257},{384,129},{385... | collective-permute-start | bytes 98312 | tf_op jit(solution)/shard_map/ppermute | solution.py:86
  347.6 2.5 collective-permute-start.19
  350.1 3.9 collective-permute-done.18
  354.0 2.9 collective-permute-done.19
  357.8 6.0 %all-to-all-start.5 = ((bf16[4,256,128]{1,2,0:T(8,128)(2,1)}), bf16[4,256,128]{1,2,0:T(8,128)(2,1)S(1)}, u32[]{:S(2)}, u32[]{:S(2)}) async-start(bf16[4,256,128]{1,2,0:T(8,128)(2,1)} %broadcast_in_dim.112), calls=%async_computation.6 | async-start | bytes 524288 | tf_op jit(solution)/shard_map/all_to_all | solution.py:221
  364.5 4.9 %all-to-all-done.5 = bf16[4,256,128]{1,2,0:T(8,128)(2,1)S(1)} async-done(((bf16[4,256,128]{1,2,0:T(8,128)(2,1)}), bf16[4,256,128]{1,2,0:T(8,128)(2,1)S(1)}, u32[]{:S(2)}, u32[]{:S(2)}) %all-to-all-start.5) | async-done | bytes 262176 | tf_op jit(solution)/shard_map/all_to_all | solution.py:221
  370.5 14.8 %all_to_all.37 = bf16[16,2,32,512]{3,2,1,0:T(8,128)(2,1)S(1)} all-to-all(bf16[16,2,32,512]{3,2,1,0:T(8,128)(2,1)S(1)} %bitcast.178), channel_id=1, replica_groups=mesh['client'=4,'expert'=16,'zlo'=4,'core'=2] {'expert'}, dimensions={0} | all-to-all | bytes 2097152 | tf_op jit(solution)/shard_map/all_to_all | solution.py:206
  385.4 1.9 collective-permute-start.20
  387.4 1.5 broadcast_in_dim.108
  388.9 1.1 constant_dynamic-update-slice_fusion.1
  390.1 2.3 constant_dynamic-update-slice_fusion
  392.4 50.5 %reduce-scatter.5.cloned.1.call-done = bf16[448,512]{1,0:T(8,128)(2,1)} async-done(((bf16[1792,512]{1,0:T(8,128)(2,1)}), bf16[448,512]{1,0:T(8,128)(2,1)}) %reduce-scatter.5.cloned.1.call-update) | async-done | bytes 458768 | tf_op jit(solution)/shard_map/reduce_scatter | solution.py:196
  442.9 3.7 convolution_add_fusion
  (159 shorter events, 38.6 us)
Async XLA Ops:
  6.5 1.8 copy-start
  6.5 18.1 %copy-start.9 = (f32[1,128,2]{1,2,0:T(2,128)S(1)}, f32[1,128,2]{1,2,0:T(2,128)}, u32[]{:S(2)}) copy-start(f32[1,128,2]{1,2,0:T(2,128)} %param.12) | copy-start | bytes 3076
  6.5 38.2 %copy-start.7 = (bf16[448,512]{1,0:T(8,128)(2,1)S(1)}, bf16[448,512]{1,0:T(8,128)(2,1)}, u32[]{:S(2)}) copy-start(bf16[448,512]{1,0:T(8,128)(2,1)} %param.14) | copy-start | bytes 1376260
  6.5 38.2 %copy-start.6 = (bf16[448,512]{1,0:T(8,128)(2,1)S(1)}, bf16[448,512]{1,0:T(8,128)(2,1)}, u32[]{:S(2)}) copy-start(bf16[448,512]{1,0:T(8,128)(2,1)} %param.15) | copy-start | bytes 1376260
  6.5 135.2 %all-gather.2.cloned.1.call-start = ((), (), s32[]{:S(2)}) async-start(), calls=%async_computation.9 | async-start | bytes 8650752 | tf_op jit(solution)/shard_map/all_gather | solution.py:109
  24.5 36.2 %copy-start.13 = (s32[4]{0:T(128)S(1)}, s32[4]{0:T(128)}, u32[]{:S(2)}) copy-start(s32[4]{0:T(128)} %param.13) | copy-start | bytes 52
  24.5 300.9 %reduce-scatter.3.cloned.1.call-start = ((), (), s32[]{:S(2)}) async-start(), calls=%async_computation.10 | async-start | bytes 2359296 | tf_op jit(solution)/shard_map/reduce_scatter | solution.py:185
  25.3 56.5 %collective-permute-start.3 = (f32[4,128]{1,0:T(4,128)}, f32[4,128]{1,0:T(4,128)}, u32[]{:S(2)}, u32[]{:S(2)}) collective-permute-start(f32[4,128]{1,0:T(4,128)} %get-tuple-element.64), channel_id=1, source_target_pairs={{0,0},{1,256},{128,128},{129,384},{256,1},{257,257},{384,129},{385... | collective-permute-start | bytes 6152 | tf_op jit(solution)/shard_map/ppermute | solution.py:86
  42.7 39.1 %collective-permute-start.4 = (f32[4,128]{1,0:T(4,128)}, f32[4,128]{1,0:T(4,128)}, u32[]{:S(2)}, u32[]{:S(2)}) collective-permute-start(f32[4,128]{1,0:T(4,128)} %get-tuple-element.65), channel_id=1, source_target_pairs={{0,128},{1,384},{128,0},{129,256},{256,129},{257,385},{384,1},{385... | collective-permute-start | bytes 6152 | tf_op jit(solution)/shard_map/ppermute | solution.py:86
  45.5 21.7 %copy-start.1 = (bf16[1,448,2048]{2,1,0:T(8,128)(2,1)S(1)}, bf16[1,448,2048]{2,1,0:T(8,128)(2,1)}, u32[]{:S(2)}) copy-start(bf16[1,448,2048]{2,1,0:T(8,128)(2,1)} %param.17) | copy-start | bytes 5505028
  46.2 59.7 %collective-permute-start.1 = (bf16[224,512]{1,0:T(8,128)(2,1)}, bf16[224,512]{1,0:T(8,128)(2,1)}, u32[]{:S(2)}, u32[]{:S(2)}) collective-permute-start(bf16[224,512]{1,0:T(8,128)(2,1)} %pad_maximum_fusion.4), channel_id=1, source_target_pairs={{0,256},{128,384},{256,0},{384,128},{1,257},{129,385},{257,1},{385... | collective-permute-start | bytes 688136 | tf_op jit(solution)/shard_map/ppermute | solution.py:19
  48.9 56.0 %collective-permute-start = (bf16[224,512]{1,0:T(8,128)(2,1)}, bf16[224,512]{1,0:T(8,128)(2,1)}, u32[]{:S(2)}, u32[]{:S(2)}) collective-permute-start(bf16[224,512]{1,0:T(8,128)(2,1)} %pad_maximum_fusion.3), channel_id=1, source_target_pairs={{0,128},{128,256},{256,384},{384,0},{1,129},{129,257},{257,385},{3... | collective-permute-start | bytes 688136 | tf_op jit(solution)/shard_map/ppermute | solution.py:19
  54.8 52.1 %collective-permute-start.2 = (bf16[224,512]{1,0:T(8,128)(2,1)}, bf16[224,512]{1,0:T(8,128)(2,1)}, u32[]{:S(2)}, u32[]{:S(2)}) collective-permute-start(bf16[224,512]{1,0:T(8,128)(2,1)} %pad_maximum_fusion.5), channel_id=1, source_target_pairs={{0,384},{128,0},{256,128},{384,256},{1,385},{129,1},{257,129},{385... | collective-permute-start | bytes 688136 | tf_op jit(solution)/shard_map/ppermute | solution.py:19
  78.5 2.2 copy-start.10
  78.5 2.2 copy-start.11
  78.5 2.2 copy-start.12
  149.5 41.4 %collective-permute-start.6 = (bf16[56,2048]{1,0:T(8,128)(2,1)S(1)}, bf16[56,2048]{1,0:T(8,128)(2,1)S(1)}, u32[]{:S(2)}, u32[]{:S(2)}) collective-permute-start(bf16[56,2048]{1,0:T(8,128)(2,1)S(1)} %get-tuple-element.35), channel_id=1, source_target_pairs={{0,128},{128,256},{256,384},{384,0},{1,129},{129,257},{257,385},{3... | collective-permute-start | bytes 688136 | tf_op jit(solution)/shard_map/ppermute | solution.py:19
  154.4 33.8 %collective-permute-start.8 = (bf16[56,2048]{1,0:T(8,128)(2,1)S(1)}, bf16[56,2048]{1,0:T(8,128)(2,1)S(1)}, u32[]{:S(2)}, u32[]{:S(2)}) collective-permute-start(bf16[56,2048]{1,0:T(8,128)(2,1)S(1)} %get-tuple-element.35), channel_id=1, source_target_pairs={{0,384},{128,0},{256,128},{384,256},{1,385},{129,1},{257,129},{385... | collective-permute-start | bytes 688136 | tf_op jit(solution)/shard_map/ppermute | solution.py:19
  158.7 23.0 %collective-permute-start.5 = (bf16[56,2048]{1,0:T(8,128)(2,1)S(1)}, bf16[56,2048]{1,0:T(8,128)(2,1)S(1)}, u32[]{:S(2)}, u32[]{:S(2)}) collective-permute-start(bf16[56,2048]{1,0:T(8,128)(2,1)S(1)} %get-tuple-element.37), channel_id=1, source_target_pairs={{0,128},{128,256},{256,384},{384,0},{1,129},{129,257},{257,385},{3... | collective-permute-start | bytes 688136 | tf_op jit(solution)/shard_map/ppermute | solution.py:19
  163.6 42.9 %collective-permute-start.10 = (bf16[56,2048]{1,0:T(8,128)(2,1)S(1)}, bf16[56,2048]{1,0:T(8,128)(2,1)S(1)}, u32[]{:S(2)}, u32[]{:S(2)}) collective-permute-start(bf16[56,2048]{1,0:T(8,128)(2,1)S(1)} %get-tuple-element.37), channel_id=1, source_target_pairs={{0,384},{128,0},{256,128},{384,256},{1,385},{129,1},{257,129},{385... | collective-permute-start | bytes 688136 | tf_op jit(solution)/shard_map/ppermute | solution.py:19
  167.9 39.1 %copy-start.8 = (bf16[448,512]{1,0:T(8,128)(2,1)S(1)}, bf16[448,512]{1,0:T(8,128)(2,1)}, u32[]{:S(2)}) copy-start(bf16[448,512]{1,0:T(8,128)(2,1)} %param.16) | copy-start | bytes 1376260
  181.7 22.4 %collective-permute-start.7 = (bf16[56,2048]{1,0:T(8,128)(2,1)S(1)}, bf16[56,2048]{1,0:T(8,128)(2,1)S(1)}, u32[]{:S(2)}, u32[]{:S(2)}) collective-permute-start(bf16[56,2048]{1,0:T(8,128)(2,1)S(1)} %collective-permute-done.5), channel_id=1, source_target_pairs={{0,128},{128,256},{256,384},{384,0},{1,129},{129,257},{257,385},{3... | collective-permute-start | bytes 688136 | tf_op jit(solution)/shard_map/ppermute | solution.py:19
  188.2 18.3 %collective-permute-start.9 = (bf16[56,2048]{1,0:T(8,128)(2,1)S(1)}, bf16[56,2048]{1,0:T(8,128)(2,1)S(1)}, u32[]{:S(2)}, u32[]{:S(2)}) collective-permute-start(bf16[56,2048]{1,0:T(8,128)(2,1)S(1)} %collective-permute-done.8), channel_id=1, source_target_pairs={{0,384},{128,0},{256,128},{384,256},{1,385},{129,1},{257,129},{385... | collective-permute-start | bytes 688136 | tf_op jit(solution)/shard_map/ppermute | solution.py:19
  208.9 8.5 %collective-permute-start.11 = (bf16[1280,512]{1,0:T(8,128)(2,1)}, bf16[1280,512]{1,0:T(8,128)(2,1)}, u32[]{:S(2)}, u32[]{:S(2)}) collective-permute-start(bf16[1280,512]{1,0:T(8,128)(2,1)} %pad_maximum_fusion), channel_id=1, source_target_pairs={{0,1},{1,0},{2,3},{3,2},{4,5},{5,4},{6,7},{7,6},{8,9},{9,8},{10,11... | collective-permute-start | bytes 3932168 | tf_op jit(solution)/shard_map/ppermute | solution.py:19
  219.2 1.1 copy-start.2
  258.5 25.7 %copy-start.14 = (s32[4]{0:T(128)S(1)}, s32[4]{0:T(128)}, u32[]{:S(2)}) copy-start(s32[4]{0:T(128)} %param.13) | copy-start | bytes 52
  262.3 48.9 %copy-start.3 = (f32[128,256]{1,0:T(8,128)S(1)}, f32[128,256]{1,0:T(8,128)}, u32[]{:S(2)}) copy-start(f32[128,256]{1,0:T(8,128)} %select_add_fusion.2) | copy-start | bytes 393220
  262.3 23.2 %all-to-all-start.2 = ((bf16[4,256,128]{2,1,0:T(8,128)(2,1)}), bf16[4,256,128]{2,1,0:T(8,128)(2,1)S(1)}, u32[]{:S(2)}, u32[]{:S(2)}) async-start(bf16[4,256,128]{2,1,0:T(8,128)(2,1)} %maximum_bitcast_fusion), calls=%async_computation.2 | async-start | bytes 524288 | tf_op jit(solution)/shard_map/all_to_all | solution.py:168
  273.7 30.3 %collective-permute-start.14 = (bf16[256,512]{1,0:T(8,128)(2,1)S(1)}, bf16[256,512]{1,0:T(8,128)(2,1)S(1)}, u32[]{:S(2)}, u32[]{:S(2)}) collective-permute-start(bf16[256,512]{1,0:T(8,128)(2,1)S(1)} %slice.250), channel_id=1, source_target_pairs={{0,2},{2,4},{4,6},{6,0},{1,3},{3,5},{5,7},{7,1},{8,10},{10,12},{12... | collective-permute-start | bytes 786440 | tf_op jit(solution)/shard_map/ppermute | solution.py:19
  277.1 27.0 %collective-permute-start.15 = (bf16[256,512]{1,0:T(8,128)(2,1)S(1)}, bf16[256,512]{1,0:T(8,128)(2,1)}, u32[]{:S(2)}, u32[]{:S(2)}) collective-permute-start(bf16[256,512]{1,0:T(8,128)(2,1)S(1)} %slice.250), channel_id=1, source_target_pairs={{0,4},{2,6},{4,0},{6,2},{1,5},{3,7},{5,1},{7,3},{8,12},{10,14},{12... | collective-permute-start | bytes 786440 | tf_op jit(solution)/shard_map/ppermute | solution.py:19
  281.1 23.0 %collective-permute-start.16 = (bf16[256,512]{1,0:T(8,128)(2,1)S(1)}, bf16[256,512]{1,0:T(8,128)(2,1)}, u32[]{:S(2)}, u32[]{:S(2)}) collective-permute-start(bf16[256,512]{1,0:T(8,128)(2,1)S(1)} %slice.250), channel_id=1, source_target_pairs={{0,6},{2,0},{4,2},{6,4},{1,7},{3,1},{5,3},{7,5},{8,14},{10,8},{12,... | collective-permute-start | bytes 786440 | tf_op jit(solution)/shard_map/ppermute | solution.py:19
  285.6 22.4 %collective-permute-start.12 = (bf16[128,128]{1,0:T(8,128)(2,1)S(1)}, bf16[128,128]{1,0:T(8,128)(2,1)S(1)}, u32[]{:S(2)}, u32[]{:S(2)}) collective-permute-start(bf16[128,128]{1,0:T(8,128)(2,1)S(1)} %get-tuple-element.57), channel_id=1, source_target_pairs={{0,0},{1,256},{128,128},{129,384},{256,1},{257,257},{384,129},{385... | collective-permute-start | bytes 98312 | tf_op jit(solution)/shard_map/ppermute | solution.py:86
  302.1 9.1 %collective-permute-start.13 = (bf16[128,128]{1,0:T(8,128)(2,1)S(1)}, bf16[128,128]{1,0:T(8,128)(2,1)S(1)}, u32[]{:S(2)}, u32[]{:S(2)}) collective-permute-start(bf16[128,128]{1,0:T(8,128)(2,1)S(1)} %get-tuple-element.56), channel_id=1, source_target_pairs={{0,128},{1,384},{128,0},{129,256},{256,129},{257,385},{384,1},{385... | collective-permute-start | bytes 98312 | tf_op jit(solution)/shard_map/ppermute | solution.py:86
  306.0 11.8 %collective-permute-start.17 = (bf16[256,512]{1,0:T(8,128)(2,1)}, bf16[256,512]{1,0:T(8,128)(2,1)}, u32[]{:S(2)}, u32[]{:S(2)}) collective-permute-start(bf16[256,512]{1,0:T(8,128)(2,1)} %get-tuple-element.24), channel_id=1, source_target_pairs={{0,1},{1,0},{2,3},{3,2},{4,5},{5,4},{6,7},{7,6},{8,9},{9,8},{10,11... | collective-permute-start | bytes 786440 | tf_op jit(solution)/shard_map/ppermute | solution.py:19
  312.4 12.9 %all-to-all-start.3 = ((bf16[16,32,256]{2,1,0:T(8,128)(2,1)}), bf16[16,32,256]{2,1,0:T(8,128)(2,1)S(1)}, u32[]{:S(2)}, u32[]{:S(2)}) async-start(bf16[16,32,256]{2,1,0:T(8,128)(2,1)} %bitcast.189), calls=%async_computation.3 | async-start | bytes 524288 | tf_op jit(solution)/shard_map/all_to_all | solution.py:206
  327.3 11.6 %all-to-all-start.4 = ((bf16[16,32,256]{2,1,0:T(8,128)(2,1)}), bf16[16,32,256]{2,1,0:T(8,128)(2,1)S(1)}, u32[]{:S(2)}, u32[]{:S(2)}) async-start(bf16[16,32,256]{2,1,0:T(8,128)(2,1)} %bitcast.188), calls=%async_computation.5 | async-start | bytes 524288 | tf_op jit(solution)/shard_map/all_to_all | solution.py:206
  339.9 29.5 %copy-start.5 = (f32[128,256]{1,0:T(8,128)S(1)}, f32[128,256]{1,0:T(8,128)}, u32[]{:S(2)}) copy-start(f32[128,256]{1,0:T(8,128)} %select_add_fusion.1) | copy-start | bytes 393220
  339.9 14.1 %collective-permute-start.18 = (bf16[128,128]{1,0:T(8,128)(2,1)S(1)}, bf16[128,128]{1,0:T(8,128)(2,1)S(1)}, u32[]{:S(2)}, u32[]{:S(2)}) collective-permute-start(bf16[128,128]{1,0:T(8,128)(2,1)S(1)} %get-tuple-element.51), channel_id=1, source_target_pairs={{0,0},{1,256},{128,128},{129,384},{256,1},{257,257},{384,129},{385... | collective-permute-start | bytes 98312 | tf_op jit(solution)/shard_map/ppermute | solution.py:86
  347.6 9.2 %collective-permute-start.19 = (bf16[128,128]{1,0:T(8,128)(2,1)S(1)}, bf16[128,128]{1,0:T(8,128)(2,1)S(1)}, u32[]{:S(2)}, u32[]{:S(2)}) collective-permute-start(bf16[128,128]{1,0:T(8,128)(2,1)S(1)} %get-tuple-element.50), channel_id=1, source_target_pairs={{0,128},{1,384},{128,0},{129,256},{256,129},{257,385},{384,1},{385... | collective-permute-start | bytes 98312 | tf_op jit(solution)/shard_map/ppermute | solution.py:86
  357.0 12.8 %copy-start.4 = (f32[128,256]{1,0:T(8,128)S(1)}, f32[128,256]{1,0:T(8,128)}, u32[]{:S(2)}) copy-start(f32[128,256]{1,0:T(8,128)} %select_add_fusion) | copy-start | bytes 393220
  357.8 11.6 %all-to-all-start.5 = ((bf16[4,256,128]{1,2,0:T(8,128)(2,1)}), bf16[4,256,128]{1,2,0:T(8,128)(2,1)S(1)}, u32[]{:S(2)}, u32[]{:S(2)}) async-start(bf16[4,256,128]{1,2,0:T(8,128)(2,1)} %broadcast_in_dim.112), calls=%async_computation.6 | async-start | bytes 524288 | tf_op jit(solution)/shard_map/all_to_all | solution.py:221
  363.7 79.2 %reduce-scatter.5.cloned.1.call-start = ((), (), s32[]{:S(2)}) async-start(), calls=%async_computation.11 | async-start | bytes 2293760 | tf_op jit(solution)/shard_map/reduce_scatter | solution.py:196
  385.4 4.7 %collective-permute-start.20 = (bf16[1024,512]{1,0:T(8,128)(2,1)S(1)}, bf16[1024,512]{1,0:T(8,128)(2,1)}, u32[]{:S(2)}, u32[]{:S(2)}) collective-permute-start(bf16[1024,512]{1,0:T(8,128)(2,1)S(1)} %bitcast.175), channel_id=1, source_target_pairs={{0,1},{1,0},{2,3},{3,2},{4,5},{5,4},{6,7},{7,6},{8,9},{9,8},{10,11... | collective-permute-start | bytes 3145736 | tf_op jit(solution)/shard_map/ppermute | solution.py:19
Sparse Core Ops, SparseCore 0:
  24.6 117.0 all-gather.1
  216.4 56.7 reduce-scatter.2
  367.4 75.4 reduce-scatter.4

commit v4 on v3

--- a/solution.py
+++ b/solution.py
@@ -192,8 +192,18 @@
     other = shift(gram, "core", 1)
     gram = place([gram, other], lambda k: (q + k) % CORES, 0)
 
-    control_sum, _ = lax.optimization_barrier((control_sum, both))
-    control_sum = lax.psum_scatter(control_sum, "client", scatter_dimension=0, tiled=True)
+    def control_to(k):
+        return at(control_sum, (c + k) % nc * units, units, 0)
+
+    mid = units // 2
+    far = control_to(2)
+    from_left = shift(far[:mid], "client", 1).astype(F32)
+    from_right = shift(far[mid:], "client", -1).astype(F32)
+    to_right, to_left = control_to(1), control_to(3)
+    to_right = jnp.concatenate([(to_right[:mid].astype(F32) + from_left).astype(BF16), to_right[mid:]], axis=0)
+    to_left = jnp.concatenate([to_left[:mid], (to_left[mid:].astype(F32) + from_right).astype(BF16)], axis=0)
+    from_left, from_right = shift(to_right, "client", 1), shift(to_left, "client", -1)
+    control_sum = control_to(0).astype(F32) + from_left.astype(F32) + from_right.astype(F32)
 
     def to_tokens(weight, x):
         x = jnp.sum(x.astype(F32).reshape(EXPERTS, copies, cap, x.shape[-1]), axis=1)
@@ -225,7 +235,7 @@
     cotangent = cotangent.transpose(1, 0, 2, 3).reshape(pair * rows, wide)
     other = shift(cotangent, "core", 1)
     cotangent = place([cotangent, other], lambda k: (q + k) % CORES, 0)
-    return dot(full, cotangent, 1, 0) + control_sum.astype(F32)
+    return dot(full, cotangent, 1, 0) + control_sum
 
 
 def solution(mesh):

time: 455 us -> 479 us (1.053)
  the two profiles are of different devices: /device:TPU:1 before, /device:TPU:33 now
where the time goes in v4:
time: 479 us; the launch traced here: 478 us
  waiting for transfers between devices  194 us (41%)
  starting transfers between devices  149 us (31%)
  blocking collectives  42.7 us (9%)
  local copies, waits for them, and re-layouts  32 us (7%)
  matrix products  23.4 us (5%)
  other arithmetic  21.2 us (4%)
  between operations  15.5 us (3%)
    ppermute x19, waiting for transfers between devices, shift(): return lax.ppermute(x, axis, [(i, (i + by) % n) for i in range(n)])  102 us
    ppermute x19, starting transfers between devices, shift(): return lax.ppermute(x, axis, [(i, (i + by) % n) for i in range(n)])  87.1 us
    ppermute x6, starting transfers between devices, hop(): arrived.append(lax.ppermute(item, ('client', 'core'), ends))  38.4 us
    all_gather x1, waiting for transfers between devices, local(): lax.all_gather(features, ('client', 'zlo', 'core'), axis=0, tiled=True)  36.1 us
    all_to_all x3, waiting for transfers between devices, exchange(): return lax.all_to_all(x, 'expert', 0, 0, tiled=True)  29.1 us
    ppermute x6, waiting for transfers between devices, hop(): arrived.append(lax.ppermute(item, ('client', 'core'), ends))  26.6 us
    dot_general x20, matrix products, dot(): lax.dot_general(a, b, (((da,), (db,)), ((), ())), preferred_element_type=...  23.4 us
    all_to_all x1, blocking collectives, exchange(): return lax.all_to_all(x, 'expert', 0, 0, tiled=True)  19.6 us
  transfers between devices with their start and end apart: 31, of which 16 were waited for; matrix products, arithmetic and copies ran while one was open for 11% of the time, Pallas kernels for 0%

profile of v4, /device:TPU:33, one launch (start us, length us, event | category | flops | bytes accessed | tf_op | source)
XLA Modules:
  0.0 477.6 jit_solution(11642187572784515951)
XLA Ops:
  8.8 14.1 %all_to_all.35 = bf16[16,4,2048]{2,1,0:T(4,128)(2,1)S(1)} all-to-all(bf16[16,4,2048]{2,1,0:T(4,128)(2,1)S(1)} %bitcast.189), channel_id=1, replica_groups=mesh['client'=4,'expert'=16,'zlo'=4,'core'=2] {'expert'}, dimensions={0} | all-to-all | bytes 524288 | tf_op jit(solution)/shard_map/all_to_all | solution.py:108
  25.3 8.8 %collective-permute-start = (bf16[224,512]{1,0:T(8,128)(2,1)}, bf16[224,512]{1,0:T(8,128)(2,1)}, u32[]{:S(2)}, u32[]{:S(2)}) collective-permute-start(bf16[224,512]{1,0:T(8,128)(2,1)} %pad_maximum_fusion.5), channel_id=1, source_target_pairs={{0,128},{128,256},{256,384},{384,0},{1,129},{129,257},{257,385},{3... | collective-permute-start | bytes 688136 | tf_op jit(solution)/shard_map/ppermute | solution.py:19
  34.8 9.9 %collective-permute-start.1 = (bf16[224,512]{1,0:T(8,128)(2,1)}, bf16[224,512]{1,0:T(8,128)(2,1)}, u32[]{:S(2)}, u32[]{:S(2)}) collective-permute-start(bf16[224,512]{1,0:T(8,128)(2,1)} %pad_maximum_fusion.6), channel_id=1, source_target_pairs={{0,256},{128,384},{256,0},{384,128},{1,257},{129,385},{257,1},{385... | collective-permute-start | bytes 688136 | tf_op jit(solution)/shard_map/ppermute | solution.py:19
  45.3 5.2 %collective-permute-start.2 = (bf16[224,512]{1,0:T(8,128)(2,1)}, bf16[224,512]{1,0:T(8,128)(2,1)}, u32[]{:S(2)}, u32[]{:S(2)}) collective-permute-start(bf16[224,512]{1,0:T(8,128)(2,1)} %pad_maximum_fusion.7), channel_id=1, source_target_pairs={{0,384},{128,0},{256,128},{384,256},{1,385},{129,1},{257,129},{385... | collective-permute-start | bytes 688136 | tf_op jit(solution)/shard_map/ppermute | solution.py:19
  50.7 4.5 collective-permute-start.4
  55.1 6.8 %collective-permute-start.3 = (f32[4,128]{1,0:T(4,128)S(1)}, f32[4,128]{1,0:T(4,128)S(1)}, u32[]{:S(2)}, u32[]{:S(2)}) collective-permute-start(f32[4,128]{1,0:T(4,128)S(1)} %get-tuple-element.68), channel_id=1, source_target_pairs={{0,0},{1,256},{128,128},{129,384},{256,1},{257,257},{384,129},{385... | collective-permute-start | bytes 6152 | tf_op jit(solution)/shard_map/ppermute | solution.py:86
  77.2 2.3 multiply_convert_fusion
  80.6 12.2 %collective-permute-done.4 = f32[4,128]{1,0:T(4,128)S(1)} collective-permute-done((f32[4,128]{1,0:T(4,128)S(1)}, f32[4,128]{1,0:T(4,128)S(1)}, u32[]{:S(2)}, u32[]{:S(2)}) %collective-permute-start.4) | collective-permute-done | bytes 2080 | tf_op jit(solution)/shard_map/ppermute | solution.py:86
  92.8 4.3 collective-permute-done.3
  101.7 36.1 %all-gather.2.cloned.1.call-done = bf16[2048,2048]{1,0:T(8,128)(2,1)} async-done(((bf16[64,2048]{1,0:T(8,128)(2,1)}), bf16[2048,2048]{1,0:T(8,128)(2,1)}) %all-gather.2.cloned.1.call-update) | async-done | bytes 8388624 | tf_op jit(solution)/shard_map/all_gather | solution.py:109
  137.8 6.0 %fusion.71 = f32[224,2048]{1,0:T(8,128)S(1)} fusion(bf16[224,2048]{1,0:T(8,128)(2,1)S(1)} %constant_dynamic-update-slice_fusion.12, bf16[2048,2048]{1,0:T(8,128)(2,1)} %all-gather.2.cloned.1.call-done), kind=kOutput, calls=%fused_computation.230 | convolution fusion | flops 1879048192 | bytes 11141120 | tf_op jit(solution)/shard_map/dot_general | solution.py:27
  145.5 4.8 %collective-permute-start.6 = (bf16[56,2048]{1,0:T(8,128)(2,1)S(1)}, bf16[56,2048]{1,0:T(8,128)(2,1)S(1)}, u32[]{:S(2)}, u32[]{:S(2)}) collective-permute-start(bf16[56,2048]{1,0:T(8,128)(2,1)S(1)} %get-tuple-element.39), channel_id=1, source_target_pairs={{0,128},{128,256},{256,384},{384,0},{1,129},{129,257},{257,385},{3... | collective-permute-start | bytes 688136 | tf_op jit(solution)/shard_map/ppermute | solution.py:19
  150.3 4.4 collective-permute-start.8
  154.7 4.8 %collective-permute-start.5 = (bf16[56,2048]{1,0:T(8,128)(2,1)S(1)}, bf16[56,2048]{1,0:T(8,128)(2,1)S(1)}, u32[]{:S(2)}, u32[]{:S(2)}) collective-permute-start(bf16[56,2048]{1,0:T(8,128)(2,1)S(1)} %get-tuple-element.41), channel_id=1, source_target_pairs={{0,128},{128,256},{256,384},{384,0},{1,129},{129,257},{257,385},{3... | collective-permute-start | bytes 688136 | tf_op jit(solution)/shard_map/ppermute | solution.py:19
  159.5 4.4 collective-permute-start.10
  164.0 13.4 %collective-permute-done.5 = bf16[56,2048]{1,0:T(8,128)(2,1)S(1)} collective-permute-done((bf16[56,2048]{1,0:T(8,128)(2,1)S(1)}, bf16[56,2048]{1,0:T(8,128)(2,1)S(1)}, u32[]{:S(2)}, u32[]{:S(2)}) %collective-permute-start.5) | collective-permute-done | bytes 229408 | tf_op jit(solution)/shard_map/ppermute | solution.py:19
  177.3 6.4 %collective-permute-start.7 = (bf16[56,2048]{1,0:T(8,128)(2,1)S(1)}, bf16[56,2048]{1,0:T(8,128)(2,1)S(1)}, u32[]{:S(2)}, u32[]{:S(2)}) collective-permute-start(bf16[56,2048]{1,0:T(8,128)(2,1)S(1)} %collective-permute-done.5), channel_id=1, source_target_pairs={{0,128},{128,256},{256,384},{384,0},{1,129},{129,257},{257,385},{3... | collective-permute-start | bytes 688136 | tf_op jit(solution)/shard_map/ppermute | solution.py:19
  183.8 2.8 collective-permute-start.9
  186.6 18.8 %collective-permute-done.7 = bf16[56,2048]{1,0:T(8,128)(2,1)S(1)} collective-permute-done((bf16[56,2048]{1,0:T(8,128)(2,1)S(1)}, bf16[56,2048]{1,0:T(8,128)(2,1)S(1)}, u32[]{:S(2)}, u32[]{:S(2)}) %collective-permute-start.7) | collective-permute-done | bytes 229408 | tf_op jit(solution)/shard_map/ppermute | solution.py:19
  205.5 11.8 %collective-permute-done.9 = bf16[56,2048]{1,0:T(8,128)(2,1)S(1)} collective-permute-done((bf16[56,2048]{1,0:T(8,128)(2,1)S(1)}, bf16[56,2048]{1,0:T(8,128)(2,1)S(1)}, u32[]{:S(2)}, u32[]{:S(2)}) %collective-permute-start.9) | collective-permute-done | bytes 229408 | tf_op jit(solution)/shard_map/ppermute | solution.py:19
  218.6 1.2 pad_maximum_fusion
  219.7 2.6 collective-permute-start.11
  222.3 2.8 convolution_convert_fusion
  225.1 1.5 copy.50
  228.4 1.8 fusion
  231.2 19.6 %all_to_all.36 = bf16[16,2,32,512]{3,2,1,0:T(8,128)(2,1)S(1)} all-to-all(bf16[16,2,32,512]{3,2,1,0:T(8,128)(2,1)S(1)} %bitcast.177), channel_id=1, replica_groups=mesh['client'=4,'expert'=16,'zlo'=4,'core'=2] {'expert'}, dimensions={0} | all-to-all | bytes 2097152 | tf_op jit(solution)/shard_map/all_to_all | solution.py:216
  252.0 1.2 convert_reduce_fusion.1
  253.4 1.5 convolution_convert_fusion.6
  254.9 1.5 convolution_convert_fusion.7
  257.2 9.0 %all-to-all-start.2 = ((bf16[4,256,128]{2,1,0:T(8,128)(2,1)}), bf16[4,256,128]{2,1,0:T(8,128)(2,1)S(1)}, u32[]{:S(2)}, u32[]{:S(2)}) async-start(bf16[4,256,128]{2,1,0:T(8,128)(2,1)} %maximum_bitcast_fusion), calls=%async_computation.2 | async-start | bytes 524288 | tf_op jit(solution)/shard_map/all_to_all | solution.py:168
  267.2 1.9 collective-permute-start.16
  269.1 4.3 collective-permute-start.15
  273.4 4.0 collective-permute-start.14
  278.7 14.6 %collective-permute-start.12 = (bf16[128,128]{1,0:T(8,128)(2,1)S(1)}, bf16[128,128]{1,0:T(8,128)(2,1)S(1)}, u32[]{:S(2)}, u32[]{:S(2)}) collective-permute-start(bf16[128,128]{1,0:T(8,128)(2,1)S(1)} %get-tuple-element.61), channel_id=1, source_target_pairs={{0,0},{1,256},{128,128},{129,384},{256,1},{257,257},{384,129},{385... | collective-permute-start | bytes 98312 | tf_op jit(solution)/shard_map/ppermute | solution.py:86
  293.4 1.9 collective-permute-start.13
  295.3 1.5 collective-permute-done.14
  296.8 1.9 constant_dynamic-update-slice_fusion.3
  298.7 2.7 collective-permute-start.17
  303.8 6.3 %all-to-all-start.3 = ((bf16[16,32,256]{2,1,0:T(8,128)(2,1)}), bf16[16,32,256]{2,1,0:T(8,128)(2,1)S(1)}, u32[]{:S(2)}, u32[]{:S(2)}) async-start(bf16[16,32,256]{2,1,0:T(8,128)(2,1)} %bitcast.58), calls=%async_computation.3 | async-start | bytes 524288 | tf_op jit(solution)/shard_map/all_to_all | solution.py:216
  310.1 9.2 %all-to-all-done.3 = bf16[16,32,256]{2,1,0:T(8,128)(2,1)S(1)} async-done(((bf16[16,32,256]{2,1,0:T(8,128)(2,1)}), bf16[16,32,256]{2,1,0:T(8,128)(2,1)S(1)}, u32[]{:S(2)}, u32[]{:S(2)}) %all-to-all-start.3) | async-done | bytes 262176 | tf_op jit(solution)/shard_map/all_to_all | solution.py:216
  319.3 1.9 fusion.1
  321.2 3.7 all-to-all-start.4
  325.5 7.7 %all-to-all-done.4 = bf16[16,32,256]{2,1,0:T(8,128)(2,1)S(1)} async-done(((bf16[16,32,256]{2,1,0:T(8,128)(2,1)}), bf16[16,32,256]{2,1,0:T(8,128)(2,1)S(1)}, u32[]{:S(2)}, u32[]{:S(2)}) %all-to-all-start.4) | async-done | bytes 262176 | tf_op jit(solution)/shard_map/all_to_all | solution.py:216
  334.3 8.7 %collective-permute-start.18 = (bf16[128,128]{1,0:T(8,128)(2,1)S(1)}, bf16[128,128]{1,0:T(8,128)(2,1)S(1)}, u32[]{:S(2)}, u32[]{:S(2)}) collective-permute-start(bf16[128,128]{1,0:T(8,128)(2,1)S(1)} %get-tuple-element.55), channel_id=1, source_target_pairs={{0,0},{1,256},{128,128},{129,384},{256,1},{257,257},{384,129},{385... | collective-permute-start | bytes 98312 | tf_op jit(solution)/shard_map/ppermute | solution.py:86
  343.0 1.9 collective-permute-start.19
  344.9 3.8 collective-permute-done.18
  348.7 5.2 %collective-permute-done.19 = bf16[128,128]{1,0:T(8,128)(2,1)S(1)} collective-permute-done((bf16[128,128]{1,0:T(8,128)(2,1)S(1)}, bf16[128,128]{1,0:T(8,128)(2,1)S(1)}, u32[]{:S(2)}, u32[]{:S(2)}) %collective-permute-start.19) | collective-permute-done | bytes 32800 | tf_op jit(solution)/shard_map/ppermute | solution.py:86
  354.2 9.0 %all_to_all.37 = bf16[4,256,128]{1,2,0:T(8,128)(2,1)S(1)} all-to-all(bf16[4,256,128]{1,2,0:T(8,128)(2,1)S(1)} %broadcast_in_dim.112), channel_id=1, replica_groups=mesh['client'=4,'expert'=16,'zlo'=4,'core'=2] {'zlo'}, dimensions={0} | all-to-all | bytes 524288 | tf_op jit(solution)/shard_map/all_to_all | solution.py:231
  364.2 1.1 broadcast_in_dim.113
  365.3 4.4 all-to-all-start.6
  369.7 12.2 %all-to-all-done.6 = bf16[16,2,32,512]{3,2,1,0:T(8,128)(2,1)} async-done(((bf16[16,2,32,512]{3,2,1,0:T(8,128)(2,1)}), bf16[16,2,32,512]{3,2,1,0:T(8,128)(2,1)}, u32[]{:S(2)}, u32[]{:S(2)}) %all-to-all-start.6) | async-done | bytes 1048608 | tf_op jit(solution)/shard_map/all_to_all | solution.py:216
  381.9 1.4 copy.44
  383.3 1.9 collective-permute-start.20
  386.1 4.4 collective-permute-start.21
  390.5 4.8 %collective-permute-start.23 = (bf16[224,512]{1,0:T(8,128)(2,1)S(1)}, bf16[224,512]{1,0:T(8,128)(2,1)}, u32[]{:S(2)}, u32[]{:S(2)}) collective-permute-start(bf16[224,512]{1,0:T(8,128)(2,1)S(1)} %get-tuple-element.29), channel_id=1, source_target_pairs={{0,384},{128,0},{256,128},{384,256},{1,385},{129,1},{257,129},{385... | collective-permute-start | bytes 688136 | tf_op jit(solution)/shard_map/ppermute | solution.py:19
  395.3 18.9 %collective-permute-done.21 = bf16[224,512]{1,0:T(8,128)(2,1)S(1)} collective-permute-done((bf16[224,512]{1,0:T(8,128)(2,1)}, bf16[224,512]{1,0:T(8,128)(2,1)S(1)}, u32[]{:S(2)}, u32[]{:S(2)}) %collective-permute-start.21) | collective-permute-done | bytes 229408 | tf_op jit(solution)/shard_map/ppermute | solution.py:19
  414.9 1.4 add_convert_fusion.2
  416.3 1.7 pad_maximum_fusion.4
  418.0 4.8 %collective-permute-start.24 = (bf16[448,512]{1,0:T(8,128)(2,1)}, bf16[448,512]{1,0:T(8,128)(2,1)}, u32[]{:S(2)}, u32[]{:S(2)}) collective-permute-start(bf16[448,512]{1,0:T(8,128)(2,1)} %pad_maximum_fusion.4), channel_id=1, source_target_pairs={{0,384},{128,0},{256,128},{384,256},{1,385},{129,1},{257,129},{385... | collective-permute-start | bytes 1376264 | tf_op jit(solution)/shard_map/ppermute | solution.py:19
  423.7 4.4 collective-permute-start.22
  428.3 1.3 constant_dynamic-update-slice_fusion
  429.7 11.8 %collective-permute-done.24 = bf16[448,512]{1,0:T(8,128)(2,1)} collective-permute-done((bf16[448,512]{1,0:T(8,128)(2,1)}, bf16[448,512]{1,0:T(8,128)(2,1)}, u32[]{:S(2)}, u32[]{:S(2)}) %collective-permute-start.24) | collective-permute-done | bytes 458784 | tf_op jit(solution)/shard_map/ppermute | solution.py:19
  441.4 25.9 %collective-permute-done.22 = bf16[448,512]{1,0:T(8,128)(2,1)} collective-permute-done((bf16[448,512]{1,0:T(8,128)(2,1)}, bf16[448,512]{1,0:T(8,128)(2,1)}, u32[]{:S(2)}, u32[]{:S(2)}) %collective-permute-start.22) | collective-permute-done | bytes 458784 | tf_op jit(solution)/shard_map/ppermute | solution.py:19
  467.3 3.4 convolution_add_fusion
  (172 shorter events, 43.8 us)
Async XLA Ops:
  6.5 1.8 copy-start
  6.5 17.2 %copy-start.9 = (bf16[448,512]{1,0:T(8,128)(2,1)S(1)}, bf16[448,512]{1,0:T(8,128)(2,1)}, u32[]{:S(2)}) copy-start(bf16[448,512]{1,0:T(8,128)(2,1)} %param.15) | copy-start | bytes 1376260
  6.5 17.2 %copy-start.10 = (bf16[448,512]{1,0:T(8,128)(2,1)S(1)}, bf16[448,512]{1,0:T(8,128)(2,1)}, u32[]{:S(2)}) copy-start(bf16[448,512]{1,0:T(8,128)(2,1)} %param.14) | copy-start | bytes 1376260
  6.5 131.3 %all-gather.2.cloned.1.call-start = ((), (), s32[]{:S(2)}) async-start(), calls=%async_computation.8 | async-start | bytes 8650752 | tf_op jit(solution)/shard_map/all_gather | solution.py:109
  23.6 27.0 %copy-start.15 = (f32[1,128,2]{1,2,0:T(2,128)S(1)}, f32[1,128,2]{1,2,0:T(2,128)}, u32[]{:S(2)}) copy-start(f32[1,128,2]{1,2,0:T(2,128)} %param.12) | copy-start | bytes 3076
  23.6 38.4 %copy-start.16 = (s32[4]{0:T(128)S(1)}, s32[4]{0:T(128)}, u32[]{:S(2)}) copy-start(s32[4]{0:T(128)} %param.13) | copy-start | bytes 52
  23.7 295.6 %reduce-scatter.2.cloned.1.call-start = ((), (), s32[]{:S(2)}) async-start(), calls=%async_computation.9 | async-start | bytes 2359296 | tf_op jit(solution)/shard_map/reduce_scatter | solution.py:185
  24.5 41.4 %copy-start.2 = (bf16[1,448,2048]{2,1,0:T(8,128)(2,1)S(1)}, bf16[1,448,2048]{2,1,0:T(8,128)(2,1)}, u32[]{:S(2)}) copy-start(bf16[1,448,2048]{2,1,0:T(8,128)(2,1)} %param.17) | copy-start | bytes 5505028
  25.3 73.5 %collective-permute-start = (bf16[224,512]{1,0:T(8,128)(2,1)}, bf16[224,512]{1,0:T(8,128)(2,1)}, u32[]{:S(2)}, u32[]{:S(2)}) collective-permute-start(bf16[224,512]{1,0:T(8,128)(2,1)} %pad_maximum_fusion.5), channel_id=1, source_target_pairs={{0,128},{128,256},{256,384},{384,0},{1,129},{129,257},{257,385},{3... | collective-permute-start | bytes 688136 | tf_op jit(solution)/shard_map/ppermute | solution.py:19
  34.8 30.3 %copy-start.11 = (bf16[112,512]{1,0:T(8,128)(2,1)S(1)}, bf16[112,512]{1,0:T(8,128)(2,1)}, u32[]{:S(2)}) copy-start(bf16[112,512]{1,0:T(8,128)(2,1)} %get-tuple-element.89) | copy-start | bytes 344068
  34.8 64.9 %collective-permute-start.1 = (bf16[224,512]{1,0:T(8,128)(2,1)}, bf16[224,512]{1,0:T(8,128)(2,1)}, u32[]{:S(2)}, u32[]{:S(2)}) collective-permute-start(bf16[224,512]{1,0:T(8,128)(2,1)} %pad_maximum_fusion.6), channel_id=1, source_target_pairs={{0,256},{128,384},{256,0},{384,128},{1,257},{129,385},{257,1},{385... | collective-permute-start | bytes 688136 | tf_op jit(solution)/shard_map/ppermute | solution.py:19
  45.3 55.3 %collective-permute-start.2 = (bf16[224,512]{1,0:T(8,128)(2,1)}, bf16[224,512]{1,0:T(8,128)(2,1)}, u32[]{:S(2)}, u32[]{:S(2)}) collective-permute-start(bf16[224,512]{1,0:T(8,128)(2,1)} %pad_maximum_fusion.7), channel_id=1, source_target_pairs={{0,384},{128,0},{256,128},{384,256},{1,385},{129,1},{257,129},{385... | collective-permute-start | bytes 688136 | tf_op jit(solution)/shard_map/ppermute | solution.py:19
  50.7 42.1 %collective-permute-start.4 = (f32[4,128]{1,0:T(4,128)S(1)}, f32[4,128]{1,0:T(4,128)S(1)}, u32[]{:S(2)}, u32[]{:S(2)}) collective-permute-start(f32[4,128]{1,0:T(4,128)S(1)} %get-tuple-element.69), channel_id=1, source_target_pairs={{0,128},{1,384},{128,0},{129,256},{256,129},{257,385},{384,1},{385... | collective-permute-start | bytes 6152 | tf_op jit(solution)/shard_map/ppermute | solution.py:86
  55.1 41.9 %collective-permute-start.3 = (f32[4,128]{1,0:T(4,128)S(1)}, f32[4,128]{1,0:T(4,128)S(1)}, u32[]{:S(2)}, u32[]{:S(2)}) collective-permute-start(f32[4,128]{1,0:T(4,128)S(1)} %get-tuple-element.68), channel_id=1, source_target_pairs={{0,0},{1,256},{128,128},{129,384},{256,1},{257,257},{384,129},{385... | collective-permute-start | bytes 6152 | tf_op jit(solution)/shard_map/ppermute | solution.py:86
  145.5 41.1 %collective-permute-start.6 = (bf16[56,2048]{1,0:T(8,128)(2,1)S(1)}, bf16[56,2048]{1,0:T(8,128)(2,1)S(1)}, u32[]{:S(2)}, u32[]{:S(2)}) collective-permute-start(bf16[56,2048]{1,0:T(8,128)(2,1)S(1)} %get-tuple-element.39), channel_id=1, source_target_pairs={{0,128},{128,256},{256,384},{384,0},{1,129},{129,257},{257,385},{3... | collective-permute-start | bytes 688136 | tf_op jit(solution)/shard_map/ppermute | solution.py:19
  150.3 33.4 %collective-permute-start.8 = (bf16[56,2048]{1,0:T(8,128)(2,1)S(1)}, bf16[56,2048]{1,0:T(8,128)(2,1)S(1)}, u32[]{:S(2)}, u32[]{:S(2)}) collective-permute-start(bf16[56,2048]{1,0:T(8,128)(2,1)S(1)} %get-tuple-element.39), channel_id=1, source_target_pairs={{0,384},{128,0},{256,128},{384,256},{1,385},{129,1},{257,129},{385... | collective-permute-start | bytes 688136 | tf_op jit(solution)/shard_map/ppermute | solution.py:19
  154.7 22.6 %collective-permute-start.5 = (bf16[56,2048]{1,0:T(8,128)(2,1)S(1)}, bf16[56,2048]{1,0:T(8,128)(2,1)S(1)}, u32[]{:S(2)}, u32[]{:S(2)}) collective-permute-start(bf16[56,2048]{1,0:T(8,128)(2,1)S(1)} %get-tuple-element.41), channel_id=1, source_target_pairs={{0,128},{128,256},{256,384},{384,0},{1,129},{129,257},{257,385},{3... | collective-permute-start | bytes 688136 | tf_op jit(solution)/shard_map/ppermute | solution.py:19
  159.5 57.7 %collective-permute-start.10 = (bf16[56,2048]{1,0:T(8,128)(2,1)S(1)}, bf16[56,2048]{1,0:T(8,128)(2,1)S(1)}, u32[]{:S(2)}, u32[]{:S(2)}) collective-permute-start(bf16[56,2048]{1,0:T(8,128)(2,1)S(1)} %get-tuple-element.41), channel_id=1, source_target_pairs={{0,384},{128,0},{256,128},{384,256},{1,385},{129,1},{257,129},{385... | collective-permute-start | bytes 688136 | tf_op jit(solution)/shard_map/ppermute | solution.py:19
  164.0 53.8 %copy-start.12 = (bf16[448,512]{1,0:T(8,128)(2,1)S(1)}, bf16[448,512]{1,0:T(8,128)(2,1)}, u32[]{:S(2)}) copy-start(bf16[448,512]{1,0:T(8,128)(2,1)} %param.16) | copy-start | bytes 1376260
  177.3 28.1 %collective-permute-start.7 = (bf16[56,2048]{1,0:T(8,128)(2,1)S(1)}, bf16[56,2048]{1,0:T(8,128)(2,1)S(1)}, u32[]{:S(2)}, u32[]{:S(2)}) collective-permute-start(bf16[56,2048]{1,0:T(8,128)(2,1)S(1)} %collective-permute-done.5), channel_id=1, source_target_pairs={{0,128},{128,256},{256,384},{384,0},{1,129},{129,257},{257,385},{3... | collective-permute-start | bytes 688136 | tf_op jit(solution)/shard_map/ppermute | solution.py:19
  183.8 33.5 %collective-permute-start.9 = (bf16[56,2048]{1,0:T(8,128)(2,1)S(1)}, bf16[56,2048]{1,0:T(8,128)(2,1)S(1)}, u32[]{:S(2)}, u32[]{:S(2)}) collective-permute-start(bf16[56,2048]{1,0:T(8,128)(2,1)S(1)} %collective-permute-done.8), channel_id=1, source_target_pairs={{0,384},{128,0},{256,128},{384,256},{1,385},{129,1},{257,129},{385... | collective-permute-start | bytes 688136 | tf_op jit(solution)/shard_map/ppermute | solution.py:19
  219.7 8.7 %collective-permute-start.11 = (bf16[1280,512]{1,0:T(8,128)(2,1)}, bf16[1280,512]{1,0:T(8,128)(2,1)}, u32[]{:S(2)}, u32[]{:S(2)}) collective-permute-start(bf16[1280,512]{1,0:T(8,128)(2,1)} %pad_maximum_fusion), channel_id=1, source_target_pairs={{0,1},{1,0},{2,3},{3,2},{4,5},{5,4},{6,7},{7,6},{8,9},{9,8},{10,11... | collective-permute-start | bytes 3932168 | tf_op jit(solution)/shard_map/ppermute | solution.py:19
  226.6 1.0 copy-start.13
  230.1 1.1 copy-start.3
  257.2 45.3 %copy-start.5 = (f32[128,256]{1,0:T(8,128)S(1)}, f32[128,256]{1,0:T(8,128)}, u32[]{:S(2)}) copy-start(f32[128,256]{1,0:T(8,128)} %select_add_fusion.2) | copy-start | bytes 393220
  257.2 21.5 %all-to-all-start.2 = ((bf16[4,256,128]{2,1,0:T(8,128)(2,1)}), bf16[4,256,128]{2,1,0:T(8,128)(2,1)S(1)}, u32[]{:S(2)}, u32[]{:S(2)}) async-start(bf16[4,256,128]{2,1,0:T(8,128)(2,1)} %maximum_bitcast_fusion), calls=%async_computation.2 | async-start | bytes 524288 | tf_op jit(solution)/shard_map/all_to_all | solution.py:168
  267.2 28.1 %collective-permute-start.16 = (bf16[256,512]{1,0:T(8,128)(2,1)S(1)}, bf16[256,512]{1,0:T(8,128)(2,1)S(1)}, u32[]{:S(2)}, u32[]{:S(2)}) collective-permute-start(bf16[256,512]{1,0:T(8,128)(2,1)S(1)} %slice.274), channel_id=1, source_target_pairs={{0,6},{2,0},{4,2},{6,4},{1,7},{3,1},{5,3},{7,5},{8,14},{10,8},{12,... | collective-permute-start | bytes 786440 | tf_op jit(solution)/shard_map/ppermute | solution.py:19
  269.1 26.2 %collective-permute-start.15 = (bf16[256,512]{1,0:T(8,128)(2,1)S(1)}, bf16[256,512]{1,0:T(8,128)(2,1)S(1)}, u32[]{:S(2)}, u32[]{:S(2)}) collective-permute-start(bf16[256,512]{1,0:T(8,128)(2,1)S(1)} %slice.274), channel_id=1, source_target_pairs={{0,4},{2,6},{4,0},{6,2},{1,5},{3,7},{5,1},{7,3},{8,12},{10,14},{12... | collective-permute-start | bytes 786440 | tf_op jit(solution)/shard_map/ppermute | solution.py:19
  273.4 23.4 %collective-permute-start.14 = (bf16[256,512]{1,0:T(8,128)(2,1)S(1)}, bf16[256,512]{1,0:T(8,128)(2,1)}, u32[]{:S(2)}, u32[]{:S(2)}) collective-permute-start(bf16[256,512]{1,0:T(8,128)(2,1)S(1)} %slice.274), channel_id=1, source_target_pairs={{0,2},{2,4},{4,6},{6,0},{1,3},{3,5},{5,7},{7,1},{8,10},{10,12},{12... | collective-permute-start | bytes 786440 | tf_op jit(solution)/shard_map/ppermute | solution.py:19
  278.7 22.7 %collective-permute-start.12 = (bf16[128,128]{1,0:T(8,128)(2,1)S(1)}, bf16[128,128]{1,0:T(8,128)(2,1)S(1)}, u32[]{:S(2)}, u32[]{:S(2)}) collective-permute-start(bf16[128,128]{1,0:T(8,128)(2,1)S(1)} %get-tuple-element.61), channel_id=1, source_target_pairs={{0,0},{1,256},{128,128},{129,384},{256,1},{257,257},{384,129},{385... | collective-permute-start | bytes 98312 | tf_op jit(solution)/shard_map/ppermute | solution.py:86
  293.4 9.1 %collective-permute-start.13 = (bf16[128,128]{1,0:T(8,128)(2,1)S(1)}, bf16[128,128]{1,0:T(8,128)(2,1)S(1)}, u32[]{:S(2)}, u32[]{:S(2)}) collective-permute-start(bf16[128,128]{1,0:T(8,128)(2,1)S(1)} %get-tuple-element.60), channel_id=1, source_target_pairs={{0,128},{1,384},{128,0},{129,256},{256,129},{257,385},{384,1},{385... | collective-permute-start | bytes 98312 | tf_op jit(solution)/shard_map/ppermute | solution.py:86
  298.7 11.3 %collective-permute-start.17 = (bf16[256,512]{1,0:T(8,128)(2,1)}, bf16[256,512]{1,0:T(8,128)(2,1)S(1)}, u32[]{:S(2)}, u32[]{:S(2)}) collective-permute-start(bf16[256,512]{1,0:T(8,128)(2,1)} %get-tuple-element.22), channel_id=1, source_target_pairs={{0,1},{1,0},{2,3},{3,2},{4,5},{5,4},{6,7},{7,6},{8,9},{9,8},{10,11... | collective-permute-start | bytes 786440 | tf_op jit(solution)/shard_map/ppermute | solution.py:19
  303.8 15.5 %all-to-all-start.3 = ((bf16[16,32,256]{2,1,0:T(8,128)(2,1)}), bf16[16,32,256]{2,1,0:T(8,128)(2,1)S(1)}, u32[]{:S(2)}, u32[]{:S(2)}) async-start(bf16[16,32,256]{2,1,0:T(8,128)(2,1)} %bitcast.58), calls=%async_computation.3 | async-start | bytes 524288 | tf_op jit(solution)/shard_map/all_to_all | solution.py:216
  321.2 42.0 %copy-start.7 = (f32[128,256]{1,0:T(8,128)S(1)}, f32[128,256]{1,0:T(8,128)}, u32[]{:S(2)}) copy-start(f32[128,256]{1,0:T(8,128)} %select_add_fusion) | copy-start | bytes 393220
  321.2 12.0 %all-to-all-start.4 = ((bf16[16,32,256]{2,1,0:T(8,128)(2,1)}), bf16[16,32,256]{2,1,0:T(8,128)(2,1)S(1)}, u32[]{:S(2)}, u32[]{:S(2)}) async-start(bf16[16,32,256]{2,1,0:T(8,128)(2,1)} %bitcast.62), calls=%async_computation.5 | async-start | bytes 524288 | tf_op jit(solution)/shard_map/all_to_all | solution.py:216
  325.5 38.1 %copy-start.6 = (f32[128,256]{1,0:T(8,128)S(1)}, f32[128,256]{1,0:T(8,128)}, u32[]{:S(2)}) copy-start(f32[128,256]{1,0:T(8,128)} %select_add_fusion.1) | copy-start | bytes 393220
  334.3 14.4 %collective-permute-start.18 = (bf16[128,128]{1,0:T(8,128)(2,1)S(1)}, bf16[128,128]{1,0:T(8,128)(2,1)S(1)}, u32[]{:S(2)}, u32[]{:S(2)}) collective-permute-start(bf16[128,128]{1,0:T(8,128)(2,1)S(1)} %get-tuple-element.55), channel_id=1, source_target_pairs={{0,0},{1,256},{128,128},{129,384},{256,1},{257,257},{384,129},{385... | collective-permute-start | bytes 98312 | tf_op jit(solution)/shard_map/ppermute | solution.py:86
  343.0 11.0 %collective-permute-start.19 = (bf16[128,128]{1,0:T(8,128)(2,1)S(1)}, bf16[128,128]{1,0:T(8,128)(2,1)S(1)}, u32[]{:S(2)}, u32[]{:S(2)}) collective-permute-start(bf16[128,128]{1,0:T(8,128)(2,1)S(1)} %get-tuple-element.54), channel_id=1, source_target_pairs={{0,128},{1,384},{128,0},{129,256},{256,129},{257,385},{384,1},{385... | collective-permute-start | bytes 98312 | tf_op jit(solution)/shard_map/ppermute | solution.py:86
  365.3 16.6 %all-to-all-start.6 = ((bf16[16,2,32,512]{3,2,1,0:T(8,128)(2,1)}), bf16[16,2,32,512]{3,2,1,0:T(8,128)(2,1)}, u32[]{:S(2)}, u32[]{:S(2)}) async-start(bf16[16,2,32,512]{3,2,1,0:T(8,128)(2,1)} %bitcast.77), calls=%async_computation.7 | async-start | bytes 2097152 | tf_op jit(solution)/shard_map/all_to_all | solution.py:216
  381.9 3.4 copy-start.4
  383.3 45.0 %collective-permute-start.20 = (bf16[1024,512]{1,0:T(8,128)(2,1)S(1)}, bf16[1024,512]{1,0:T(8,128)(2,1)}, u32[]{:S(2)}, u32[]{:S(2)}) collective-permute-start(bf16[1024,512]{1,0:T(8,128)(2,1)S(1)} %bitcast.175), channel_id=1, source_target_pairs={{0,1},{1,0},{2,3},{3,2},{4,5},{5,4},{6,7},{7,6},{8,9},{9,8},{10,11... | collective-permute-start | bytes 3145736 | tf_op jit(solution)/shard_map/ppermute | solution.py:19
  386.1 28.1 %collective-permute-start.21 = (bf16[224,512]{1,0:T(8,128)(2,1)}, bf16[224,512]{1,0:T(8,128)(2,1)S(1)}, u32[]{:S(2)}, u32[]{:S(2)}) collective-permute-start(bf16[224,512]{1,0:T(8,128)(2,1)} %get-tuple-element.27), channel_id=1, source_target_pairs={{0,128},{128,256},{256,384},{384,0},{1,129},{129,257},{257,385},{3... | collective-permute-start | bytes 688136 | tf_op jit(solution)/shard_map/ppermute | solution.py:19
  390.5 24.4 %collective-permute-start.23 = (bf16[224,512]{1,0:T(8,128)(2,1)S(1)}, bf16[224,512]{1,0:T(8,128)(2,1)}, u32[]{:S(2)}, u32[]{:S(2)}) collective-permute-start(bf16[224,512]{1,0:T(8,128)(2,1)S(1)} %get-tuple-element.29), channel_id=1, source_target_pairs={{0,384},{128,0},{256,128},{384,256},{1,385},{129,1},{257,129},{385... | collective-permute-start | bytes 688136 | tf_op jit(solution)/shard_map/ppermute | solution.py:19
  395.3 27.5 %copy-start.8 = (bf16[224,512]{1,0:T(8,128)(2,1)S(1)}, bf16[224,512]{1,0:T(8,128)(2,1)}, u32[]{:S(2)}) copy-start(bf16[224,512]{1,0:T(8,128)(2,1)} %get-tuple-element.30) | copy-start | bytes 688132
  414.2 0.7 copy-start.14
  418.0 23.4 %collective-permute-start.24 = (bf16[448,512]{1,0:T(8,128)(2,1)}, bf16[448,512]{1,0:T(8,128)(2,1)}, u32[]{:S(2)}, u32[]{:S(2)}) collective-permute-start(bf16[448,512]{1,0:T(8,128)(2,1)} %pad_maximum_fusion.4), channel_id=1, source_target_pairs={{0,384},{128,0},{256,128},{384,256},{1,385},{129,1},{257,129},{385... | collective-permute-start | bytes 1376264 | tf_op jit(solution)/shard_map/ppermute | solution.py:19
  423.7 43.7 %collective-permute-start.22 = (bf16[448,512]{1,0:T(8,128)(2,1)}, bf16[448,512]{1,0:T(8,128)(2,1)}, u32[]{:S(2)}, u32[]{:S(2)}) collective-permute-start(bf16[448,512]{1,0:T(8,128)(2,1)} %pad_maximum_fusion.3), channel_id=1, source_target_pairs={{0,128},{128,256},{256,384},{384,0},{1,129},{129,257},{257,385},{3... | collective-permute-start | bytes 1376264 | tf_op jit(solution)/shard_map/ppermute | solution.py:19
  467.3 3.4 copy-start.1
Sparse Core Ops, SparseCore 0:
  23.8 113.9 all-gather.1
  226.7 37.2 reduce-scatter.1
